TPU v7x, 32 devices: a whole 2x2x4 slice. The times are simulated.
32 devices in a mesh: grp: 8 (over y, x, core), seq: 4 (over z).
Axes of the slice: x: 2, y: 2, z: 4, core: 2. Of those that a mesh axis runs over, the one named last changes fastest.
Arguments:
- tokens: bfloat16 [16, 16, 256, 384], P(None, 'grp', 'seq'), may hold values from -6 to 6
- cotangent: bfloat16 [16, 16, 256, 384], P(None, 'grp', 'seq'), may hold values from -6 to 6
- condition: float32 [16, 16, 384], P(None, 'grp'), may hold values from -6 to 6
- mask_flags: int32 [16, 16], P(None, 'grp'), may hold values 0 or 1
- noise_levels: int32 [16, 16], P(None, 'grp'), may hold values from 0 to 63
- level_table: float32 [64, 384], replicated, may hold values from -6 to 6
- ada_weight: bfloat16 [384, 2304], replicated, may hold values from -0.3125 to 0.3125
- ada_bias: float32 [2304], replicated, may hold values from -3 to 3
- qkv_weight: bfloat16 [384, 1152], replicated, may hold values from -0.3125 to 0.3125
- query_value_bias: float32 [768], replicated, may hold values from -1.75 to 1.75
- output_weight: bfloat16 [384, 384], replicated, may hold values from -1.25 to 1.25
- output_bias: float32 [384], replicated, may hold values from -1.75 to 1.75
- up_weight: bfloat16 [384, 1536], replicated, may hold values from -0.3125 to 0.3125
- up_bias: float32 [1536], replicated, may hold values from -1.75 to 1.75
- down_weight: bfloat16 [1536, 384], replicated, may hold values from -0.15625 to 0.15625
- down_bias: float32 [384], replicated, may hold values from -1.75 to 1.75
Outputs:
- layer_out: bfloat16 [16, 16, 256, 384], P(None, 'grp', 'seq')
- grad_tokens: bfloat16 [16, 16, 256, 384], P(None, 'grp', 'seq')
- grad_condition: float32 [16, 16, 384], P(None, 'grp')
- grad_level_table: float32 [64, 384], replicated
- grad_ada_weight: float32 [384, 2304], replicated
- grad_ada_bias: float32 [2304], replicated
- grad_qkv_weight: float32 [384, 1152], replicated
- grad_query_value_bias: float32 [768], replicated
- grad_output_weight: float32 [384, 384], replicated
- grad_output_bias: float32 [384], replicated
- grad_up_weight: float32 [384, 1536], replicated
- grad_up_bias: float32 [1536], replicated
- grad_down_weight: float32 [1536, 384], replicated
- grad_down_bias: float32 [384], replicated
Inputs may be any that keep to these rules, and one draw needn't show every extreme that they name: `mask_flags`: 1 marks an image of which only the first 128 rows are kept patches; its other rows are padding.
All inputs are finite; a program needn't handle non-finite values. No bound on the sum of `mask_flags` on one device may be relied on, other than what follows from the above.
Results may differ from a plain program's by a relative error of at most 0.015.
The roundings to bfloat16 on the way count: a program that leaves them out, or rounds other values in their place, can miss the bound.
Values may be sent and summed in bfloat16 or wider, within the bound.
No kernel may reach another device: no remote copies, remote signals or barrier semaphores. Data moves between devices by JAX's collectives and lax.ppermute only.
A program may use at most 128 MiB of HBM per device.

v0:
```python
import math

import jax
import jax.numpy as jnp
from jax import lax
from jax.sharding import PartitionSpec as P

D = 384
HEADS = 6
HEAD_DIM = 64
SEQ_LEN = 256
KEEP = 128
LEVELS = 64


highest = lax.Precision.HIGHEST
EPSILON = 1e-06


def layer_norm(values):
    average = jnp.mean(values, -1, keepdims=True)
    centered = values - average
    rstd_vals = lax.rsqrt(jnp.mean(centered * centered, -1, keepdims=True) + EPSILON)
    return (centered * rstd_vals, rstd_vals)


def norm_back(grad_norm, normed, rstd_vals):
    return rstd_vals * (
        grad_norm
        - jnp.mean(grad_norm, -1, keepdims=True)
        - normed * jnp.mean(grad_norm * normed, -1, keepdims=True)
    )


def matmul(operand, factor):
    return jnp.dot(operand, factor, preferred_element_type=jnp.float32)


def matmul_trans(operand, factor):
    return lax.dot_general(
        operand, factor, (((1,), (1,)), ((), ())), preferred_element_type=jnp.float32
    )


def outer_sum(operand, factor):
    return lax.dot_general(
        operand, factor, (((0,), (0,)), ((), ())), preferred_element_type=jnp.float32
    )


def gelu_tanh(values):
    return jax.nn.gelu(values, approximate=True)


def pick(array, index):
    return lax.dynamic_index_in_dim(array, index, 0, keepdims=False)


def shards(
    tokens,
    cotangent,
    condition,
    mask_flags,
    noise_levels,
    level_table,
    ada_weight,
    ada_bias,
    qkv_weight,
    query_value_bias,
    output_weight,
    output_bias,
    up_weight,
    up_bias,
    down_weight,
    down_bias,
):
    batches = tokens.shape[0]
    images = tokens.shape[1]
    rows = tokens.shape[2]
    flat_rows = images * rows
    inv_root = 1.0 / math.sqrt(HEAD_DIM)
    row_index = lax.axis_index("seq") * rows + jnp.arange(rows, dtype=jnp.int32)
    key_index = jnp.arange(SEQ_LEN, dtype=jnp.int32)
    level_ids = jnp.arange(LEVELS, dtype=jnp.int32)
    ada_wide = ada_weight.astype(jnp.float32)
    bias_full = jnp.concatenate(
        [query_value_bias[:D], jnp.zeros((D,), jnp.float32), query_value_bias[D:]]
    )
    accums = (
        jnp.zeros(level_table.shape, jnp.float32),
        jnp.zeros(ada_weight.shape, jnp.float32),
        jnp.zeros(ada_bias.shape, jnp.float32),
        jnp.zeros(qkv_weight.shape, jnp.float32),
        jnp.zeros(query_value_bias.shape, jnp.float32),
        jnp.zeros(output_weight.shape, jnp.float32),
        jnp.zeros(output_bias.shape, jnp.float32),
        jnp.zeros(up_weight.shape, jnp.float32),
        jnp.zeros(up_bias.shape, jnp.float32),
        jnp.zeros(down_weight.shape, jnp.float32),
        jnp.zeros(down_bias.shape, jnp.float32),
    )
    buffers = (
        jnp.zeros(tokens.shape, jnp.bfloat16),
        jnp.zeros(tokens.shape, jnp.bfloat16),
        jnp.zeros(condition.shape, jnp.float32),
    )

    def one_batch(batch_index, state):
        (
            acc_level,
            acc_ada_weight,
            acc_ada_bias,
            acc_qkv_weight,
            acc_qv_bias,
            acc_out_weight,
            acc_out_bias,
            acc_up_weight,
            acc_up_bias,
            acc_down_weight,
            acc_down_bias,
        ), (out_buf, gtok_buf, cond_buf) = state
        token_rows = pick(tokens, batch_index).astype(jnp.float32)
        whole_image = (pick(mask_flags, batch_index) == 0)[:, None]
        live_rows = jnp.logical_or(whole_image, row_index[None, :] < KEEP).astype(jnp.float32)
        live_keys = jnp.logical_or(whole_image, key_index[None, :] < KEEP)
        live_col = live_rows[..., None]
        onehot = (pick(noise_levels, batch_index)[:, None] == level_ids[None, :]).astype(
            jnp.float32
        )
        cond_full = pick(condition, batch_index) + jnp.dot(onehot, level_table, precision=highest)
        activated = jax.nn.silu(cond_full).astype(jnp.bfloat16)
        modulation = matmul(activated, ada_weight) + ada_bias
        shift_one, scale_one, gate_one, shift_two, scale_two, gate_two = jnp.split(
            modulation[:, None, :], 6, axis=-1
        )
        norm_one, rstd_one = layer_norm(token_rows)
        in_one = (norm_one * (1.0 + scale_one) + shift_one).astype(jnp.bfloat16)
        in_one_flat = in_one.reshape(flat_rows, D)
        projected = (
            (matmul(in_one_flat, qkv_weight) + bias_full)
            .astype(jnp.bfloat16)
            .reshape(images, rows, 3 * D)
        )
        queries = projected[..., :D]
        keys_local = projected[..., D : 2 * D]
        values_local = projected[..., 2 * D :]
        keys_all, values_all = (
            lax.all_gather(keys_local, "seq", axis=1, tiled=True),
            lax.all_gather(values_local, "seq", axis=1, tiled=True),
        )
        query_heads = queries.reshape(images, rows, HEADS, HEAD_DIM)
        key_heads = keys_all.reshape(images, SEQ_LEN, HEADS, HEAD_DIM)
        value_heads = values_all.reshape(images, SEQ_LEN, HEADS, HEAD_DIM)
        scores = (
            jnp.einsum(
                "irhd,ishd->ihrs", query_heads, key_heads, preferred_element_type=jnp.float32
            )
            * inv_root
        )
        scores = jnp.where(live_keys[:, None, None, :], scores, -1e30)
        row_max = jnp.max(scores, -1, keepdims=True)
        exp_scores = jnp.exp(scores - row_max)
        row_total = jnp.sum(exp_scores, -1, keepdims=True)
        attn_probs = exp_scores / row_total
        probs_low = attn_probs.astype(jnp.bfloat16)
        attended = jnp.einsum(
            "ihrs,ishd->irhd", probs_low, value_heads, preferred_element_type=jnp.float32
        )
        attended_flat = attended.reshape(flat_rows, D).astype(jnp.bfloat16)
        attn_branch = (matmul(attended_flat, output_weight) + output_bias).reshape(images, rows, D)
        residual = token_rows + live_col * gate_one * attn_branch
        norm_two, rstd_two = layer_norm(residual)
        in_two_flat = (
            (norm_two * (1.0 + scale_two) + shift_two).astype(jnp.bfloat16).reshape(flat_rows, D)
        )
        pre_act = matmul(in_two_flat, up_weight) + up_bias
        hidden = gelu_tanh(pre_act).astype(jnp.bfloat16)
        ffn_branch = (matmul(hidden, down_weight) + down_bias).reshape(images, rows, D)
        layer_rows = (residual + live_col * gate_two * ffn_branch).astype(jnp.bfloat16)
        g_output = pick(cotangent, batch_index).astype(jnp.float32)
        g_ffn = (live_col * gate_two * g_output).astype(jnp.bfloat16).reshape(flat_rows, D)
        g_gate_two = jnp.sum(live_col * g_output * ffn_branch, axis=1)
        acc_down_weight = acc_down_weight + outer_sum(hidden, g_ffn)
        acc_down_bias = acc_down_bias + jnp.sum(g_ffn.astype(jnp.float32), 0)
        gelu_back = jax.vjp(gelu_tanh, pre_act)[1]
        g_pre = gelu_back(matmul_trans(g_ffn, down_weight))[0].astype(jnp.bfloat16)
        acc_up_weight = acc_up_weight + outer_sum(in_two_flat, g_pre)
        acc_up_bias = acc_up_bias + jnp.sum(g_pre.astype(jnp.float32), 0)
        g_in_two = matmul_trans(g_pre, up_weight).reshape(images, rows, D)
        g_scale_two = jnp.sum(g_in_two * norm_two, axis=1)
        g_shift_two = jnp.sum(g_in_two, axis=1)
        g_residual = g_output + norm_back(g_in_two * (1.0 + scale_two), norm_two, rstd_two)
        g_attn = (live_col * gate_one * g_residual).astype(jnp.bfloat16).reshape(flat_rows, D)
        g_gate_one = jnp.sum(live_col * g_residual * attn_branch, axis=1)
        acc_out_weight = acc_out_weight + outer_sum(attended_flat, g_attn)
        acc_out_bias = acc_out_bias + jnp.sum(g_attn.astype(jnp.float32), 0)
        g_attended = (
            matmul_trans(g_attn, output_weight)
            .astype(jnp.bfloat16)
            .reshape(images, rows, HEADS, HEAD_DIM)
        )
        g_probs = jnp.einsum(
            "irhd,ishd->ihrs", g_attended, value_heads, preferred_element_type=jnp.float32
        )
        prob_dot = jnp.sum(attn_probs * g_probs, -1)
        g_scores = (attn_probs * (g_probs - prob_dot[..., None])).astype(jnp.bfloat16)
        g_queries = (
            jnp.einsum("ihrs,ishd->irhd", g_scores, key_heads, preferred_element_type=jnp.float32)
            * inv_root
        )
        g_key_terms = (
            jnp.einsum("ihrs,irhd->ishd", g_scores, query_heads, preferred_element_type=jnp.float32)
            * inv_root
        )
        g_value_terms = jnp.einsum(
            "ihrs,irhd->ishd", probs_low, g_attended, preferred_element_type=jnp.float32
        )
        g_keys, g_values = (
            lax.psum_scatter(
                g_key_terms.reshape(images, SEQ_LEN, D).astype(jnp.bfloat16),
                "seq",
                scatter_dimension=1,
                tiled=True,
            ).astype(jnp.float32),
            lax.psum_scatter(
                g_value_terms.reshape(images, SEQ_LEN, D).astype(jnp.bfloat16),
                "seq",
                scatter_dimension=1,
                tiled=True,
            ).astype(jnp.float32),
        )
        g_projected = jnp.concatenate(
            [g_queries.reshape(images, rows, D), g_keys, g_values], axis=-1
        )
        g_projected = g_projected.astype(jnp.bfloat16).reshape(flat_rows, 3 * D)
        acc_qkv_weight = acc_qkv_weight + outer_sum(in_one_flat, g_projected)
        column_sums = jnp.sum(g_projected.astype(jnp.float32), 0)
        acc_qv_bias = acc_qv_bias + jnp.concatenate([column_sums[:D], column_sums[2 * D :]])
        g_in_one = matmul_trans(g_projected, qkv_weight).reshape(images, rows, D)
        g_scale_one = jnp.sum(g_in_one * norm_one, axis=1)
        g_shift_one = jnp.sum(g_in_one, axis=1)
        g_tokens = g_residual + norm_back(g_in_one * (1.0 + scale_one), norm_one, rstd_one)
        g_modulation = jnp.concatenate(
            [g_shift_one, g_scale_one, g_gate_one, g_shift_two, g_scale_two, g_gate_two], axis=1
        )
        acc_ada_weight = acc_ada_weight + lax.dot_general(
            activated.astype(jnp.float32),
            g_modulation,
            (((0,), (0,)), ((), ())),
            precision=highest,
            preferred_element_type=jnp.float32,
        )
        acc_ada_bias = acc_ada_bias + jnp.sum(g_modulation, 0)
        silu_back = jax.vjp(jax.nn.silu, cond_full)[1]
        g_activated = lax.dot_general(
            g_modulation,
            ada_wide,
            (((1,), (1,)), ((), ())),
            precision=highest,
            preferred_element_type=jnp.float32,
        )
        g_cond_part = silu_back(g_activated)[0]
        acc_level = acc_level + lax.dot_general(
            onehot,
            g_cond_part,
            (((0,), (0,)), ((), ())),
            precision=highest,
            preferred_element_type=jnp.float32,
        )
        out_buf = lax.dynamic_update_index_in_dim(out_buf, layer_rows, batch_index, 0)
        gtok_buf = lax.dynamic_update_index_in_dim(
            gtok_buf, g_tokens.astype(jnp.bfloat16), batch_index, 0
        )
        cond_buf = lax.dynamic_update_index_in_dim(cond_buf, g_cond_part, batch_index, 0)
        return (
            (
                acc_level,
                acc_ada_weight,
                acc_ada_bias,
                acc_qkv_weight,
                acc_qv_bias,
                acc_out_weight,
                acc_out_bias,
                acc_up_weight,
                acc_up_bias,
                acc_down_weight,
                acc_down_bias,
            ),
            (out_buf, gtok_buf, cond_buf),
        )

    final_acc, (out_buf, gtok_buf, cond_buf) = lax.fori_loop(
        0, batches, one_batch, (accums, buffers)
    )
    grad_condition = lax.psum(cond_buf.astype(jnp.bfloat16), "seq").astype(jnp.float32)
    summed = lax.psum(
        (
            final_acc[0],
            final_acc[1],
            final_acc[2],
            final_acc[3],
            final_acc[4],
            final_acc[5],
            final_acc[6],
            final_acc[7],
            final_acc[8],
            final_acc[9],
            final_acc[10],
        ),
        ("grp", "seq"),
    )
    return (
        out_buf,
        gtok_buf,
        grad_condition,
        summed[0],
        summed[1],
        summed[2],
        summed[3],
        summed[4],
        summed[5],
        summed[6],
        summed[7],
        summed[8],
        summed[9],
        summed[10],
    )


def solution(mesh):
    in_specs = (
        P(None, "grp", "seq", None),
        P(None, "grp", "seq", None),
        P(None, "grp", None),
        P(None, "grp"),
        P(None, "grp"),
        P(),
        P(),
        P(),
        P(),
        P(),
        P(),
        P(),
        P(),
        P(),
        P(),
        P(),
    )
    out_specs = (
        P(None, "grp", "seq", None),
        P(None, "grp", "seq", None),
        P(None, "grp", None),
        P(),
        P(),
        P(),
        P(),
        P(),
        P(),
        P(),
        P(),
        P(),
        P(),
        P(),
    )
    return jax.shard_map(shards, mesh=mesh, in_specs=in_specs, out_specs=out_specs, check_vma=False)
```

profile of v0, /device:TPU:0, one launch (start us, length us, event | category | flops | bytes accessed | tf_op | source)
XLA Modules:
  0.0 2264.6 jit_solution(10842693612826892349)
XLA Ops:
  15.7 2004.1 %while.42 = (s32[]{:T(128)}, f32[64,384]{1,0:T(8,128)}, f32[384,2304]{1,0:T(8,128)}, f32[2304]{0:T(1024)}, f32[384,1152]{1,0:T(8,128)}, /*index=5*/f32[768]{0:T(...) while((s32[]{:T(128)}, f32[64,384]{1,0:T(8,128)}, ...), condition=%wide.region_25.26_spmd.clone, body=%wide.region_0.25_spmd.clone.sunk | while | flops 1635717888 | bytes 119820984 | solution.py:292
  26.6 16.3 all_gather.24
  43.8 15.6 all_gather.25
  106.3 20.9 reduce-scatter.5.cloned.1.call-done
  154.0 14.3 all_gather.24
  169.2 15.0 all_gather.25
  231.6 18.5 reduce-scatter.5.cloned.1.call-done
  279.0 14.3 all_gather.24
  294.3 15.1 all_gather.25
  356.9 18.3 reduce-scatter.5.cloned.1.call-done
  404.1 14.4 all_gather.24
  419.4 15.2 all_gather.25
  482.0 18.4 reduce-scatter.5.cloned.1.call-done
  529.3 14.4 all_gather.24
  544.7 15.1 all_gather.25
  607.2 18.2 reduce-scatter.5.cloned.1.call-done
  654.3 14.4 all_gather.24
  669.7 15.1 all_gather.25
  732.2 18.2 reduce-scatter.5.cloned.1.call-done
  779.4 14.3 all_gather.24
  794.6 15.0 all_gather.25
  857.0 18.5 reduce-scatter.5.cloned.1.call-done
  904.5 14.3 all_gather.24
  919.8 15.1 all_gather.25
  982.3 18.3 reduce-scatter.5.cloned.1.call-done
  1029.5 14.4 all_gather.24
  1044.9 15.1 all_gather.25
  1107.4 18.3 reduce-scatter.5.cloned.1.call-done
  1169.8 15.0 all_gather.25
  1232.2 18.6 reduce-scatter.5.cloned.1.call-done
  1295.0 15.0 all_gather.25
  1357.4 18.6 reduce-scatter.5.cloned.1.call-done
  1404.9 14.3 all_gather.24
  1420.2 15.0 all_gather.25
  1482.6 18.6 reduce-scatter.5.cloned.1.call-done
  1530.1 14.4 all_gather.24
  1545.4 15.1 all_gather.25
  1608.0 18.2 reduce-scatter.5.cloned.1.call-done
  1655.1 14.3 all_gather.24
  1670.3 15.0 all_gather.25
  1732.8 18.6 reduce-scatter.5.cloned.1.call-done
  1795.5 15.0 all_gather.25
  1857.9 18.5 reduce-scatter.5.cloned.1.call-done
  1920.5 14.9 all_gather.25
  1982.9 18.8 reduce-scatter.5.cloned.1.call-done
  2021.3 15.9 psum.84
  2037.9 40.0 %all-reduce = (f32[2304]{0:T(1024)}, f32[768]{0:T(1024)}, f32[384]{0:T(512)}, f32[1536]{0:T(1024)}, f32[384]{0:T(512)}) all-reduce(f32[2304]{0:T(1024)S(1)} %copy-done.40, f32[768]{0:T(1024)S(1)} %copy-done.56, f32[384]{0:T(512)} %get-tuple-element.1592, f32[1536]{0:T(1024)S(1)} %copy-done.46, ...), channel_id=1, replica_groups=mesh['grp'=8,'seq'=4] {'grp','seq'}, use_global_device_ids=true, to_apply=%region_29.30 | all-reduce | flops 5376 | bytes 43008 | tf_op jit(solution)/shard_map/psum | solution.py:296
  2077.9 167.3 %all-reduce.4.cloned.1.call-done = (f32[64,384]{1,0:T(8,128)}, f32[384,2304]{1,0:T(8,128)}, f32[384,1152]{1,0:T(8,128)}, f32[384,384]{1,0:T(8,128)}, f32[384,1536]{1,0:T(8,128)}, /*index=5*/f32[1536,384]{1,0:T(8,128)}) async-done(((f32[64,384]{1,0:T(8,128)}, f32[384,2304]{1,0:T(8,128)}, f32[384,1152]{1,0:T(8,128)}, f32[384,384]{1,0:T(8,128)}, f32[384,1536]{1,0:T(8,128)}, /*index=5*/f32[1536,384]{1,0:T(8,128)}), ...) | async-done | bytes 10715152 | tf_op jit(solution)/shard_map/psum | solution.py:296
  (3607 shorter events, 1297.5 us)
Async XLA Ops:
  15.7 89.5 %reduce-scatter.3.cloned.1.call-start = ((), (), s32[]{:S(2)}) async-start(), calls=%async_computation.3 | async-start | bytes 491520 | tf_op jit(solution)/shard_map/while/body/eval_jaxpr/reduce_scatter | solution.py:225
  26.6 35.0 %copy-start.15 = (bf16[2,64,384]{1,2,0:T(8,128)(2,1)}, bf16[2,64,384]{1,2,0:T(8,128)(2,1)S(1)}, u32[]{:S(2)}) copy-start(bf16[2,64,384]{1,2,0:T(8,128)(2,1)S(1)} %copy.87) | copy-start | bytes 294916 | tf_op jit(solution)/shard_map/while
  83.7 43.5 %reduce-scatter.5.cloned.1.call-start = ((), (), s32[]{:S(2)}) async-start(), calls=%async_computation.4 | async-start | bytes 491520 | tf_op jit(solution)/shard_map/while/body/eval_jaxpr/reduce_scatter | solution.py:219
  143.2 87.4 %reduce-scatter.3.cloned.1.call-start = ((), (), s32[]{:S(2)}) async-start(), calls=%async_computation.3 | async-start | bytes 491520 | tf_op jit(solution)/shard_map/while/body/eval_jaxpr/reduce_scatter | solution.py:225
  154.0 32.4 %copy-start.15 = (bf16[2,64,384]{1,2,0:T(8,128)(2,1)}, bf16[2,64,384]{1,2,0:T(8,128)(2,1)S(1)}, u32[]{:S(2)}) copy-start(bf16[2,64,384]{1,2,0:T(8,128)(2,1)S(1)} %copy.87) | copy-start | bytes 294916 | tf_op jit(solution)/shard_map/while
  208.5 41.6 %reduce-scatter.5.cloned.1.call-start = ((), (), s32[]{:S(2)}) async-start(), calls=%async_computation.4 | async-start | bytes 491520 | tf_op jit(solution)/shard_map/while/body/eval_jaxpr/reduce_scatter | solution.py:219
  268.2 87.6 %reduce-scatter.3.cloned.1.call-start = ((), (), s32[]{:S(2)}) async-start(), calls=%async_computation.3 | async-start | bytes 491520 | tf_op jit(solution)/shard_map/while/body/eval_jaxpr/reduce_scatter | solution.py:225
  279.0 32.6 %copy-start.15 = (bf16[2,64,384]{1,2,0:T(8,128)(2,1)}, bf16[2,64,384]{1,2,0:T(8,128)(2,1)S(1)}, u32[]{:S(2)}) copy-start(bf16[2,64,384]{1,2,0:T(8,128)(2,1)S(1)} %copy.87) | copy-start | bytes 294916 | tf_op jit(solution)/shard_map/while
  333.8 41.3 %reduce-scatter.5.cloned.1.call-start = ((), (), s32[]{:S(2)}) async-start(), calls=%async_computation.4 | async-start | bytes 491520 | tf_op jit(solution)/shard_map/while/body/eval_jaxpr/reduce_scatter | solution.py:219
  393.2 87.8 %reduce-scatter.3.cloned.1.call-start = ((), (), s32[]{:S(2)}) async-start(), calls=%async_computation.3 | async-start | bytes 491520 | tf_op jit(solution)/shard_map/while/body/eval_jaxpr/reduce_scatter | solution.py:225
  404.1 32.7 %copy-start.15 = (bf16[2,64,384]{1,2,0:T(8,128)(2,1)}, bf16[2,64,384]{1,2,0:T(8,128)(2,1)S(1)}, u32[]{:S(2)}) copy-start(bf16[2,64,384]{1,2,0:T(8,128)(2,1)S(1)} %copy.87) | copy-start | bytes 294916 | tf_op jit(solution)/shard_map/while
  458.9 41.4 %reduce-scatter.5.cloned.1.call-start = ((), (), s32[]{:S(2)}) async-start(), calls=%async_computation.4 | async-start | bytes 491520 | tf_op jit(solution)/shard_map/while/body/eval_jaxpr/reduce_scatter | solution.py:219
  518.5 87.7 %reduce-scatter.3.cloned.1.call-start = ((), (), s32[]{:S(2)}) async-start(), calls=%async_computation.3 | async-start | bytes 491520 | tf_op jit(solution)/shard_map/while/body/eval_jaxpr/reduce_scatter | solution.py:225
  529.3 32.7 %copy-start.15 = (bf16[2,64,384]{1,2,0:T(8,128)(2,1)}, bf16[2,64,384]{1,2,0:T(8,128)(2,1)S(1)}, u32[]{:S(2)}) copy-start(bf16[2,64,384]{1,2,0:T(8,128)(2,1)S(1)} %copy.87) | copy-start | bytes 294916 | tf_op jit(solution)/shard_map/while
  584.1 41.3 %reduce-scatter.5.cloned.1.call-start = ((), (), s32[]{:S(2)}) async-start(), calls=%async_computation.4 | async-start | bytes 491520 | tf_op jit(solution)/shard_map/while/body/eval_jaxpr/reduce_scatter | solution.py:219
  643.5 87.6 %reduce-scatter.3.cloned.1.call-start = ((), (), s32[]{:S(2)}) async-start(), calls=%async_computation.3 | async-start | bytes 491520 | tf_op jit(solution)/shard_map/while/body/eval_jaxpr/reduce_scatter | solution.py:225
  654.3 32.6 %copy-start.15 = (bf16[2,64,384]{1,2,0:T(8,128)(2,1)}, bf16[2,64,384]{1,2,0:T(8,128)(2,1)S(1)}, u32[]{:S(2)}) copy-start(bf16[2,64,384]{1,2,0:T(8,128)(2,1)S(1)} %copy.87) | copy-start | bytes 294916 | tf_op jit(solution)/shard_map/while
  709.1 41.3 %reduce-scatter.5.cloned.1.call-start = ((), (), s32[]{:S(2)}) async-start(), calls=%async_computation.4 | async-start | bytes 491520 | tf_op jit(solution)/shard_map/while/body/eval_jaxpr/reduce_scatter | solution.py:219
  768.5 87.4 %reduce-scatter.3.cloned.1.call-start = ((), (), s32[]{:S(2)}) async-start(), calls=%async_computation.3 | async-start | bytes 491520 | tf_op jit(solution)/shard_map/while/body/eval_jaxpr/reduce_scatter | solution.py:225
  779.3 32.4 %copy-start.15 = (bf16[2,64,384]{1,2,0:T(8,128)(2,1)}, bf16[2,64,384]{1,2,0:T(8,128)(2,1)S(1)}, u32[]{:S(2)}) copy-start(bf16[2,64,384]{1,2,0:T(8,128)(2,1)S(1)} %copy.87) | copy-start | bytes 294916 | tf_op jit(solution)/shard_map/while
  833.9 41.6 %reduce-scatter.5.cloned.1.call-start = ((), (), s32[]{:S(2)}) async-start(), calls=%async_computation.4 | async-start | bytes 491520 | tf_op jit(solution)/shard_map/while/body/eval_jaxpr/reduce_scatter | solution.py:219
  893.6 87.6 %reduce-scatter.3.cloned.1.call-start = ((), (), s32[]{:S(2)}) async-start(), calls=%async_computation.3 | async-start | bytes 491520 | tf_op jit(solution)/shard_map/while/body/eval_jaxpr/reduce_scatter | solution.py:225
  904.5 32.6 %copy-start.15 = (bf16[2,64,384]{1,2,0:T(8,128)(2,1)}, bf16[2,64,384]{1,2,0:T(8,128)(2,1)S(1)}, u32[]{:S(2)}) copy-start(bf16[2,64,384]{1,2,0:T(8,128)(2,1)S(1)} %copy.87) | copy-start | bytes 294916 | tf_op jit(solution)/shard_map/while
  959.2 41.4 %reduce-scatter.5.cloned.1.call-start = ((), (), s32[]{:S(2)}) async-start(), calls=%async_computation.4 | async-start | bytes 491520 | tf_op jit(solution)/shard_map/while/body/eval_jaxpr/reduce_scatter | solution.py:219
  1018.7 87.7 %reduce-scatter.3.cloned.1.call-start = ((), (), s32[]{:S(2)}) async-start(), calls=%async_computation.3 | async-start | bytes 491520 | tf_op jit(solution)/shard_map/while/body/eval_jaxpr/reduce_scatter | solution.py:225
  1029.5 32.7 %copy-start.15 = (bf16[2,64,384]{1,2,0:T(8,128)(2,1)}, bf16[2,64,384]{1,2,0:T(8,128)(2,1)S(1)}, u32[]{:S(2)}) copy-start(bf16[2,64,384]{1,2,0:T(8,128)(2,1)S(1)} %copy.87) | copy-start | bytes 294916 | tf_op jit(solution)/shard_map/while
  1084.3 41.3 %reduce-scatter.5.cloned.1.call-start = ((), (), s32[]{:S(2)}) async-start(), calls=%async_computation.4 | async-start | bytes 491520 | tf_op jit(solution)/shard_map/while/body/eval_jaxpr/reduce_scatter | solution.py:219
  1143.8 87.4 %reduce-scatter.3.cloned.1.call-start = ((), (), s32[]{:S(2)}) async-start(), calls=%async_computation.3 | async-start | bytes 491520 | tf_op jit(solution)/shard_map/while/body/eval_jaxpr/reduce_scatter | solution.py:225
  1154.6 32.4 %copy-start.15 = (bf16[2,64,384]{1,2,0:T(8,128)(2,1)}, bf16[2,64,384]{1,2,0:T(8,128)(2,1)S(1)}, u32[]{:S(2)}) copy-start(bf16[2,64,384]{1,2,0:T(8,128)(2,1)S(1)} %copy.87) | copy-start | bytes 294916 | tf_op jit(solution)/shard_map/while
  1209.2 41.6 %reduce-scatter.5.cloned.1.call-start = ((), (), s32[]{:S(2)}) async-start(), calls=%async_computation.4 | async-start | bytes 491520 | tf_op jit(solution)/shard_map/while/body/eval_jaxpr/reduce_scatter | solution.py:219
  1268.9 87.4 %reduce-scatter.3.cloned.1.call-start = ((), (), s32[]{:S(2)}) async-start(), calls=%async_computation.3 | async-start | bytes 491520 | tf_op jit(solution)/shard_map/while/body/eval_jaxpr/reduce_scatter | solution.py:225
  1279.7 32.4 %copy-start.15 = (bf16[2,64,384]{1,2,0:T(8,128)(2,1)}, bf16[2,64,384]{1,2,0:T(8,128)(2,1)S(1)}, u32[]{:S(2)}) copy-start(bf16[2,64,384]{1,2,0:T(8,128)(2,1)S(1)} %copy.87) | copy-start | bytes 294916 | tf_op jit(solution)/shard_map/while
  1334.3 41.7 %reduce-scatter.5.cloned.1.call-start = ((), (), s32[]{:S(2)}) async-start(), calls=%async_computation.4 | async-start | bytes 491520 | tf_op jit(solution)/shard_map/while/body/eval_jaxpr/reduce_scatter | solution.py:219
  1394.1 87.4 %reduce-scatter.3.cloned.1.call-start = ((), (), s32[]{:S(2)}) async-start(), calls=%async_computation.3 | async-start | bytes 491520 | tf_op jit(solution)/shard_map/while/body/eval_jaxpr/reduce_scatter | solution.py:225
  1404.9 32.4 %copy-start.15 = (bf16[2,64,384]{1,2,0:T(8,128)(2,1)}, bf16[2,64,384]{1,2,0:T(8,128)(2,1)S(1)}, u32[]{:S(2)}) copy-start(bf16[2,64,384]{1,2,0:T(8,128)(2,1)S(1)} %copy.87) | copy-start | bytes 294916 | tf_op jit(solution)/shard_map/while
  1459.5 41.7 %reduce-scatter.5.cloned.1.call-start = ((), (), s32[]{:S(2)}) async-start(), calls=%async_computation.4 | async-start | bytes 491520 | tf_op jit(solution)/shard_map/while/body/eval_jaxpr/reduce_scatter | solution.py:219
  1519.3 87.7 %reduce-scatter.3.cloned.1.call-start = ((), (), s32[]{:S(2)}) async-start(), calls=%async_computation.3 | async-start | bytes 491520 | tf_op jit(solution)/shard_map/while/body/eval_jaxpr/reduce_scatter | solution.py:225
  1530.1 32.7 %copy-start.15 = (bf16[2,64,384]{1,2,0:T(8,128)(2,1)}, bf16[2,64,384]{1,2,0:T(8,128)(2,1)S(1)}, u32[]{:S(2)}) copy-start(bf16[2,64,384]{1,2,0:T(8,128)(2,1)S(1)} %copy.87) | copy-start | bytes 294916 | tf_op jit(solution)/shard_map/while
  1584.9 41.3 %reduce-scatter.5.cloned.1.call-start = ((), (), s32[]{:S(2)}) async-start(), calls=%async_computation.4 | async-start | bytes 491520 | tf_op jit(solution)/shard_map/while/body/eval_jaxpr/reduce_scatter | solution.py:219
  1644.3 87.4 %reduce-scatter.3.cloned.1.call-start = ((), (), s32[]{:S(2)}) async-start(), calls=%async_computation.3 | async-start | bytes 491520 | tf_op jit(solution)/shard_map/while/body/eval_jaxpr/reduce_scatter | solution.py:225
  1655.1 32.5 %copy-start.15 = (bf16[2,64,384]{1,2,0:T(8,128)(2,1)}, bf16[2,64,384]{1,2,0:T(8,128)(2,1)S(1)}, u32[]{:S(2)}) copy-start(bf16[2,64,384]{1,2,0:T(8,128)(2,1)S(1)} %copy.87) | copy-start | bytes 294916 | tf_op jit(solution)/shard_map/while
  1709.7 41.7 %reduce-scatter.5.cloned.1.call-start = ((), (), s32[]{:S(2)}) async-start(), calls=%async_computation.4 | async-start | bytes 491520 | tf_op jit(solution)/shard_map/while/body/eval_jaxpr/reduce_scatter | solution.py:219
  1769.5 87.4 %reduce-scatter.3.cloned.1.call-start = ((), (), s32[]{:S(2)}) async-start(), calls=%async_computation.3 | async-start | bytes 491520 | tf_op jit(solution)/shard_map/while/body/eval_jaxpr/reduce_scatter | solution.py:225
  1780.3 32.4 %copy-start.15 = (bf16[2,64,384]{1,2,0:T(8,128)(2,1)}, bf16[2,64,384]{1,2,0:T(8,128)(2,1)S(1)}, u32[]{:S(2)}) copy-start(bf16[2,64,384]{1,2,0:T(8,128)(2,1)S(1)} %copy.87) | copy-start | bytes 294916 | tf_op jit(solution)/shard_map/while
  1834.9 41.5 %reduce-scatter.5.cloned.1.call-start = ((), (), s32[]{:S(2)}) async-start(), calls=%async_computation.4 | async-start | bytes 491520 | tf_op jit(solution)/shard_map/while/body/eval_jaxpr/reduce_scatter | solution.py:219
  1894.5 87.3 %reduce-scatter.3.cloned.1.call-start = ((), (), s32[]{:S(2)}) async-start(), calls=%async_computation.3 | async-start | bytes 491520 | tf_op jit(solution)/shard_map/while/body/eval_jaxpr/reduce_scatter | solution.py:225
  1959.8 41.9 %reduce-scatter.5.cloned.1.call-start = ((), (), s32[]{:S(2)}) async-start(), calls=%async_computation.4 | async-start | bytes 491520 | tf_op jit(solution)/shard_map/while/body/eval_jaxpr/reduce_scatter | solution.py:219
  2019.8 225.4 %all-reduce.4.cloned.1.call-start = ((), (), s32[]{:S(2)}) async-start(), calls=%async_computation.2 | async-start | bytes 21430272 | tf_op jit(solution)/shard_map/psum | solution.py:296
  (1036 other events, 5138.9 us)
Sparse Core Ops, SparseCore 0:
  83.8 21.4 reduce-scatter.2
  108.1 18.9 reduce-scatter.4
  208.7 19.6 reduce-scatter.2
  231.0 19.0 reduce-scatter.4
  333.9 19.4 reduce-scatter.2
  356.1 19.0 reduce-scatter.4
  459.1 19.2 reduce-scatter.2
  481.3 19.0 reduce-scatter.4
  584.2 19.3 reduce-scatter.2
  606.3 19.0 reduce-scatter.4
  709.2 19.4 reduce-scatter.2
  731.4 18.9 reduce-scatter.4
  834.0 19.8 reduce-scatter.2
  856.6 18.8 reduce-scatter.4
  959.3 19.5 reduce-scatter.2
  981.6 18.8 reduce-scatter.4
  1084.4 19.4 reduce-scatter.2
  1106.7 18.9 reduce-scatter.4
  1209.3 19.6 reduce-scatter.2
  1231.7 19.0 reduce-scatter.4
  1334.4 19.6 reduce-scatter.2
  1356.9 19.0 reduce-scatter.4
  1459.6 19.6 reduce-scatter.2
  1482.0 19.0 reduce-scatter.4
  1585.0 19.2 reduce-scatter.2
  1607.0 19.0 reduce-scatter.4
  1709.8 19.5 reduce-scatter.2
  1732.2 19.0 reduce-scatter.4
  1835.0 19.7 reduce-scatter.2
  1857.5 18.9 reduce-scatter.4
  1959.9 19.7 reduce-scatter.2
  1982.6 19.0 reduce-scatter.4
Sparse Core Ops, SparseCore 1:
  2027.9 217.3 all-reduce.3
where the time goes:
time: 2280 us; the launch traced here: 2260 us
  matrix products  667 us (29%)
  blocking collectives  529 us (23%)
  waiting for transfers between devices  467 us (20%)
  local copies, waits for them, and re-layouts  291 us (13%)
  other arithmetic  280 us (12%)
    reduce_scatter x16, waiting for transfers between devices, one_batch(): lax.psum_scatter(g_key_terms.reshape(images, SEQ_LEN, D).astype(jnp.bfloa...  297 us
    all_gather x16, blocking collectives, one_batch(): lax.all_gather(keys_local, 'seq', axis=1, tiled=True)  241 us
    all_gather x16, blocking collectives, one_batch(): lax.all_gather(values_local, 'seq', axis=1, tiled=True)  231 us
    psum x1, waiting for transfers between devices, shards(): lax.psum((final_acc[0], final_acc[1], final_acc[2], final_acc[3], final_a...  167 us
    dot_general x64, matrix products, outer_sum(): lax.dot_general(operand, factor, (((0,), (0,)), ((), ())), preferred_elem...  142 us
    dot_general x80, matrix products, matmul(): return jnp.dot(operand, factor, preferred_element_type=jnp.float32)  118 us
    dot_general x64, matrix products, matmul_trans(): lax.dot_general(operand, factor, (((1,), (1,)), ((), ())), preferred_elem...  88.1 us
    dot_general x16, matrix products, one_batch(): lax.dot_general(activated.astype(jnp.float32), g_modulation, (((0,), (0,)...  87.2 us
  transfers between devices with their start and end apart: 33, of which 18 were waited for; matrix products, arithmetic and copies ran while one was open for 16% of the time, Pallas kernels for 0%

commit v1 on v0

v1 whole, which is shorter than its diff:
```python
import functools
import math

import jax
import jax.numpy as jnp
from jax import lax
from jax.experimental import pallas as pl
from jax.experimental.pallas import tpu as pltpu
from jax.sharding import PartitionSpec as P

D = 384
HEADS = 6
HEAD_DIM = 64
FF = 1536
SEQ_LEN = 256
KEEP = 128
LEVELS = 64
EPSILON = 1e-06
highest = lax.Precision.HIGHEST

UP, DOWN, QKV, OUT, WIDE = 0, FF, 2 * FF, 2 * FF + 3 * D, 2 * FF + 4 * D
FF_TILE = 512
CHUNKS = 4


def dot_nn(a, b):
    return lax.dot_general(a, b, (((1,), (0,)), ((), ())), preferred_element_type=jnp.float32)


def dot_nt(a, b):
    return lax.dot_general(a, b, (((1,), (1,)), ((), ())), preferred_element_type=jnp.float32)


def dot_tn(a, b):
    return lax.dot_general(a, b, (((0,), (0,)), ((), ())), preferred_element_type=jnp.float32)


def row_mean(values):
    return jnp.mean(values, -1, keepdims=True)


def layer_norm(values):
    centered = values - row_mean(values)
    rstd = lax.rsqrt(row_mean(centered * centered) + EPSILON)
    return centered * rstd, rstd


def norm_back(grad, normed, rstd):
    return rstd * (grad - row_mean(grad) - normed * row_mean(grad * normed))


def col_sum(values):
    return jnp.sum(values, 0, keepdims=True)


def layer_kernel(parts, first, last, *refs):
    live_ref = refs[0]
    ins = refs[1 : 1 + parts]
    (mod_ref, wqkv, wqkv_t, wout, wout_t, wup, wup_t, wdown, wdown_t, bqkv, bout, bup, bdown) = refs[
        1 + parts : 14 + parts
    ]
    rest = refs[14 + parts :]
    if not first:
        acc_in, bias_in = rest[:2]
        rest = rest[2:]
    outs = rest[:parts]
    gmod_ref, acc_out, bias_acc, acc, probs_ref, sem = rest[parts : parts + 6]
    if last:
        acc_low = rest[parts + 6]
    step = pl.program_id(0)
    steps = pl.num_programs(0)

    @pl.when(step == 0)
    def _():
        if first:
            acc[...] = jnp.zeros_like(acc)
            bias_acc[...] = jnp.zeros_like(bias_acc)
        else:
            copy = pltpu.make_async_copy(acc_in, acc, sem)
            copy.start()
            bias_acc[...] = bias_in[...]
            copy.wait()

    rows = ins[0].shape[2]
    full = parts * rows
    tokens = jnp.concatenate([ref[0, 0] for ref in ins], 0).astype(jnp.float32)
    live_parts = [live_ref[step, p] for p in range(parts)]
    live = jnp.concatenate([jnp.full((rows, 1), flag, jnp.float32) for flag in live_parts], 0)
    key_part = lax.broadcasted_iota(jnp.int32, (1, full), 1) // rows
    live_keys = jnp.zeros((1, full), jnp.float32)
    for p in range(parts):
        live_keys = jnp.where(key_part == p, live_parts[p], live_keys)
    live_keys = live_keys > 0.5
    mod = mod_ref[0]
    shift_one, scale_one, gate_one = mod[0:1], 1.0 + mod[1:2], mod[2:3]
    shift_two, scale_two, gate_two = mod[3:4], 1.0 + mod[4:5], mod[5:6]

    norm_one, rstd_one = layer_norm(tokens)
    in_one = (norm_one * scale_one + shift_one).astype(jnp.bfloat16)
    projected = dot_nn(in_one, wqkv[...]) + bqkv[...]
    inv_root = 1.0 / math.sqrt(HEAD_DIM)
    queries = (projected[:, :D].astype(jnp.bfloat16) * jnp.bfloat16(inv_root)).astype(jnp.bfloat16)
    keys = projected[:, D : 2 * D].astype(jnp.bfloat16)
    values = projected[:, 2 * D :].astype(jnp.bfloat16)
    lanes = lax.broadcasted_iota(jnp.int32, (1, 2 * HEAD_DIM), 1)
    halves = (lanes < HEAD_DIM, lanes >= HEAD_DIM)

    def pair(array, j):
        return array[:, j * 2 * HEAD_DIM : (j + 1) * 2 * HEAD_DIM]

    def half(array, h):
        return jnp.where(halves[h], array, jnp.zeros_like(array))

    attended = []
    for j in range(HEADS // 2):
        total = None
        for h in range(2):
            scores = dot_nt(pair(queries, j), half(pair(keys, j), h))
            scores = jnp.where(live_keys, scores, -1e30)
            exps = jnp.exp(scores - jnp.max(scores, -1, keepdims=True))
            probs = exps * (1.0 / jnp.sum(exps, -1, keepdims=True))
            probs_ref[2 * j + h] = probs
            term = dot_nn(probs.astype(jnp.bfloat16), half(pair(values, j), h))
            total = term if total is None else total + term
        attended.append(total.astype(jnp.bfloat16))
    attended = jnp.concatenate(attended, 1)
    attn_branch = dot_nn(attended, wout[...]) + bout[...]
    live_gate_one = live * gate_one
    residual = tokens + live_gate_one * attn_branch
    norm_two, rstd_two = layer_norm(residual)
    in_two = (norm_two * scale_two + shift_two).astype(jnp.bfloat16)

    g_output = jnp.concatenate([ref[1, 0] for ref in ins], 0).astype(jnp.float32)
    live_out = live * g_output
    g_ffn = (live_out * gate_two).astype(jnp.bfloat16)
    in_two_t = in_two.T
    g_ffn_t = g_ffn.T
    ffn = None
    g_in_two = None
    root = math.sqrt(2.0 / math.pi)
    for tile in range(FF // FF_TILE):
        cols = slice(tile * FF_TILE, (tile + 1) * FF_TILE)
        pre = dot_nn(in_two, wup[:, cols]) + bup[:, cols]
        square = pre * pre
        gate = 0.5 + 0.5 * jnp.tanh(pre * (root + (root * 0.044715) * square))
        hidden_wide = pre * gate
        slope = gate + hidden_wide * (1.0 - gate) * (2.0 * root + (6.0 * root * 0.044715) * square)
        hidden = hidden_wide.astype(jnp.bfloat16)
        term = dot_nn(hidden, wdown[cols, :])
        ffn = term if ffn is None else ffn + term
        g_pre_wide = dot_nn(g_ffn, wdown_t[:, cols]) * slope
        g_pre = g_pre_wide.astype(jnp.bfloat16)
        acc[:, DOWN + tile * FF_TILE : DOWN + (tile + 1) * FF_TILE] += dot_nn(g_ffn_t, hidden)
        acc[:, UP + tile * FF_TILE : UP + (tile + 1) * FF_TILE] += dot_nn(in_two_t, g_pre)
        bias_acc[:, UP + tile * FF_TILE : UP + (tile + 1) * FF_TILE] += col_sum(g_pre.astype(jnp.float32))
        term = dot_nn(g_pre, wup_t[cols, :])
        g_in_two = term if g_in_two is None else g_in_two + term
    bias_acc[:, DOWN : DOWN + D] += col_sum(g_ffn.astype(jnp.float32))
    ffn = ffn + bdown[...]
    layer_out = (residual + live * gate_two * ffn).astype(jnp.bfloat16)
    for p in range(parts):
        outs[p][0, 0] = layer_out[p * rows : (p + 1) * rows]
    gmod_ref[0, 5:6] = col_sum(live_out * ffn)
    gmod_ref[0, 4:5] = col_sum(g_in_two * norm_two)
    gmod_ref[0, 3:4] = col_sum(g_in_two)
    g_residual = g_output + norm_back(g_in_two * scale_two, norm_two, rstd_two)
    g_attn = (live_gate_one * g_residual).astype(jnp.bfloat16)
    gmod_ref[0, 2:3] = col_sum(live * g_residual * attn_branch)
    acc[:, OUT : OUT + D] += dot_tn(attended, g_attn)
    bias_acc[:, OUT : OUT + D] += col_sum(g_attn.astype(jnp.float32))
    g_attended = dot_nn(g_attn, wout_t[...]).astype(jnp.bfloat16)

    g_queries, g_keys, g_values = [], [], []
    for j in range(HEADS // 2):
        gq = gk = gv = None
        for h in range(2):
            probs = probs_ref[2 * j + h]
            g_probs = dot_nt(pair(g_attended, j), half(pair(values, j), h))
            weighted = probs * g_probs
            g_scores = (weighted - probs * jnp.sum(weighted, -1, keepdims=True)).astype(jnp.bfloat16)
            tq = dot_nn(g_scores, half(pair(keys, j), h))
            tk = dot_tn(g_scores, half(pair(queries, j), h))
            tv = dot_tn(probs.astype(jnp.bfloat16), half(pair(g_attended, j), h))
            gq, gk, gv = (tq, tk, tv) if gq is None else (gq + tq, gk + tk, gv + tv)
        g_queries.append((gq * inv_root).astype(jnp.bfloat16))
        g_keys.append(gk.astype(jnp.bfloat16))
        g_values.append(gv.astype(jnp.bfloat16))
    g_projected = jnp.concatenate(g_queries + g_keys + g_values, 1)
    acc[:, QKV : QKV + 3 * D] += dot_tn(in_one, g_projected)
    bias_acc[:, QKV : QKV + 3 * D] += col_sum(g_projected.astype(jnp.float32))
    g_in_one = dot_nn(g_projected, wqkv_t[...])
    gmod_ref[0, 1:2] = col_sum(g_in_one * norm_one)
    gmod_ref[0, 0:1] = col_sum(g_in_one)
    g_tokens = (g_residual + norm_back(g_in_one * scale_one, norm_one, rstd_one)).astype(jnp.bfloat16)
    for p in range(parts):
        outs[p][1, 0] = g_tokens[p * rows : (p + 1) * rows]

    @pl.when(step == steps - 1)
    def _():
        if last:
            acc_low[...] = acc[...].astype(jnp.bfloat16)
            copy = pltpu.make_async_copy(acc_low, acc_out, sem)
        else:
            copy = pltpu.make_async_copy(acc, acc_out, sem)
        copy.start()
        copy.wait()


def layer_call(live, blocks, mod, weights, carried, last):
    parts = len(blocks)
    images, rows = blocks[0].shape[1:3]
    first = carried is None
    resident = [pl.BlockSpec(w.shape, lambda i: (0, 0), pipeline_mode=pl.Buffered(1)) for w in weights]
    block_spec = pl.BlockSpec((2, 1, rows, D), lambda i: (0, i, 0, 0))
    mod_spec = pl.BlockSpec((1, 6, D), lambda i: (i, 0, 0))
    any_spec = pl.BlockSpec(memory_space=pl.ANY)
    bias_spec = pl.BlockSpec((1, WIDE), lambda i: (0, 0))
    in_specs = (
        [pl.BlockSpec(memory_space=pltpu.SMEM)] + [block_spec] * parts + [mod_spec] + resident
    )
    args = [live, *blocks, mod, *weights]
    aliases = {}
    if not first:
        in_specs += [any_spec, bias_spec]
        if not last:
            aliases = {len(args): parts + 1}
        args += list(carried)
    acc_type = jnp.bfloat16 if last else jnp.float32
    scratch = [
        pltpu.VMEM((D, WIDE), jnp.float32),
        pltpu.VMEM((HEADS, parts * rows, parts * rows), jnp.float32),
        pltpu.SemaphoreType.DMA,
    ]
    if last:
        scratch.append(pltpu.VMEM((D, WIDE), jnp.bfloat16))
    result = pl.pallas_call(
        functools.partial(layer_kernel, parts, first, last),
        grid=(images,),
        in_specs=in_specs,
        out_specs=[block_spec] * parts + [mod_spec, any_spec, bias_spec],
        out_shape=[jax.ShapeDtypeStruct(b.shape, jnp.bfloat16) for b in blocks]
        + [
            jax.ShapeDtypeStruct((images, 6, D), jnp.float32),
            jax.ShapeDtypeStruct((D, WIDE), acc_type),
            jax.ShapeDtypeStruct((1, WIDE), jnp.float32),
        ],
        scratch_shapes=scratch,
        input_output_aliases=aliases,
        compiler_params=pltpu.CompilerParams(vmem_limit_bytes=52 * 1024 * 1024),
    )(*args)
    return result[:parts], result[parts], (result[parts + 1], result[parts + 2])


def cut(array, start, size, axis=0):
    return lax.dynamic_slice_in_dim(array, start, size, axis)


def group_stages(size):
    bits = [1 << k for k in range(size.bit_length() - 1)]
    if size == 8:
        table = [[1] * 8, [2 if i % 2 == 0 else 4 for i in range(8)], [4 if i % 2 == 0 else 2 for i in range(8)]]
    else:
        table = [[bit] * size for bit in bits]
    return table


def stage_bit(stage, index):
    masks = jnp.asarray(stage, jnp.int32)[index] if len(set(stage)) > 1 else stage[0]
    return jnp.where((index & masks) != 0, 1, 0)


def swap(array, stage):
    return lax.ppermute(array, "grp", [(i, i ^ bit) for i, bit in enumerate(stage)])


def seq_shift(array, shift, size):
    return lax.ppermute(array, "seq", [(i, (i + shift) % size) for i in range(size)])


def reduce_all(array, group, seq):
    index = lax.axis_index("grp")
    place = lax.axis_index("seq")
    stages = group_stages(group)
    for stage in stages:
        size = array.shape[0] // 2
        bit = stage_bit(stage, index)
        got = swap(cut(array, (1 - bit) * size, size), stage)
        array = (cut(array, bit * size, size).astype(jnp.float32) + got.astype(jnp.float32)).astype(jnp.bfloat16)
    size = array.shape[1] // seq
    total = cut(array, place * size, size, 1).astype(jnp.float32)
    for shift in (2, 1, 3) if seq == 4 else range(1, seq):
        total = total + seq_shift(cut(array, ((place + shift) % seq) * size, size, 1), shift, seq).astype(jnp.float32)
    array = gather_seq(total.astype(jnp.bfloat16), place, seq, 1)
    return gather_group(array, index, stages)


def gather_seq(array, place, seq, axis):
    size = array.shape[axis]
    shape = list(array.shape)
    shape[axis] = size * seq
    whole = lax.dynamic_update_slice_in_dim(jnp.zeros(shape, array.dtype), array, place * size, axis)
    for shift in (2, 1, 3) if seq == 4 else range(1, seq):
        got = seq_shift(array, shift, seq)
        whole = lax.dynamic_update_slice_in_dim(whole, got, ((place - shift) % seq) * size, axis)
    return whole


def gather_group(array, index, stages):
    for stage in reversed(stages):
        bit = stage_bit(stage, index)
        got = swap(array, stage)
        array = jnp.where(bit == 0, jnp.concatenate([array, got], 0), jnp.concatenate([got, array], 0))
    return array


def shards(
    group,
    seq,
    tokens,
    cotangent,
    condition,
    mask_flags,
    noise_levels,
    level_table,
    ada_weight,
    ada_bias,
    qkv_weight,
    query_value_bias,
    output_weight,
    output_bias,
    up_weight,
    up_bias,
    down_weight,
    down_bias,
):
    batches, images, rows = tokens.shape[:3]
    count = batches * images
    own = count // seq
    step = own // CHUNKS
    place = lax.axis_index("seq")
    index = lax.axis_index("grp")
    stages = group_stages(group)
    tokens = tokens.reshape(count, rows, D)
    cotangent = cotangent.reshape(count, rows, D)
    shifts = (0, 2, 1, 3) if seq == 4 else tuple(range(seq))

    def fetch(chunk):
        blocks = []
        for shift in shifts:
            start = ((place + shift) % seq) * own + chunk * step
            block = jnp.stack([cut(tokens, start, step), cut(cotangent, start, step)])
            blocks.append(block if shift == 0 else seq_shift(block, shift, seq))
        return blocks

    flags = cut(mask_flags.reshape(count), place * own, own)
    sources = jnp.stack([(place - shift) % seq for shift in shifts])
    kept = sources * rows < KEEP
    live = jnp.logical_or(flags[:, None] == 0, kept[None, :]).astype(jnp.float32)

    table = jnp.concatenate(
        [condition.reshape(count, D), jnp.broadcast_to(noise_levels.reshape(count, 1).astype(jnp.float32), (count, 128))],
        1,
    )
    gathered = gather_group_plain(table, index, group)
    onehot = (gathered[:, D : D + 1].astype(jnp.int32) == jnp.arange(LEVELS, dtype=jnp.int32)[None, :]).astype(
        jnp.float32
    )
    cond_full = gathered[:, :D] + jnp.dot(onehot, level_table, precision=highest)
    activated = jax.nn.silu(cond_full).astype(jnp.bfloat16)
    mine = (noise_levels.reshape(count)[:, None] == jnp.arange(LEVELS, dtype=jnp.int32)[None, :]).astype(jnp.float32)
    mine = cut(condition.reshape(count, D), place * own, own) + jnp.dot(
        cut(mine, place * own, own), level_table, precision=highest
    )
    modulation = (
        jnp.dot(jax.nn.silu(mine).astype(jnp.bfloat16), ada_weight, preferred_element_type=jnp.float32) + ada_bias
    ).reshape(own, 6, D)

    bias_full = jnp.concatenate([query_value_bias[:D], jnp.zeros((D,), jnp.float32), query_value_bias[D:]])
    weights = (
        qkv_weight,
        qkv_weight.T,
        output_weight,
        output_weight.T,
        up_weight,
        up_weight.T,
        down_weight,
        down_weight.T,
        bias_full[None],
        output_bias[None],
        up_bias[None],
        down_bias[None],
    )
    out_rows = jnp.zeros((count, rows, D), jnp.bfloat16)
    grad_rows = jnp.zeros((count, rows, D), jnp.bfloat16)
    carried = None
    g_mods = []
    blocks = fetch(0)
    for chunk in range(CHUNKS):
        following = fetch(chunk + 1) if chunk + 1 < CHUNKS else None
        span = slice(chunk * step, (chunk + 1) * step)
        results, g_mod, carried = layer_call(
            live[span], blocks, modulation[span], weights, carried, chunk + 1 == CHUNKS
        )
        g_mods.append(g_mod)
        for shift, result in zip(shifts, results):
            back = result if shift == 0 else seq_shift(result, -shift, seq)
            start = ((place + shift) % seq) * own + chunk * step
            out_rows = lax.dynamic_update_slice_in_dim(out_rows, back[0], start, 0)
            grad_rows = lax.dynamic_update_slice_in_dim(grad_rows, back[1], start, 0)
        blocks = following

    summed, bias_sums = carried
    flat = jnp.concatenate([jnp.concatenate(g_mods).reshape(-1), bias_sums.reshape(-1)])
    lines = -(-flat.shape[0] // 2048) * 16
    flat = jnp.pad(flat, (0, lines * 128 - flat.shape[0])).reshape(lines, 128).astype(jnp.bfloat16)
    small = gather_seq(flat, place, seq, 0)
    small = gather_group_plain(small, index, group).reshape(group * seq, lines * 128)
    g_all = small[:, : own * 6 * D].reshape(group * count, 6 * D)
    bias_all = jnp.sum(small[:, own * 6 * D : own * 6 * D + WIDE].astype(jnp.float32), 0)

    grad_ada = lax.dot_general(activated, g_all, (((0,), (0,)), ((), ())), preferred_element_type=jnp.float32)
    grad_ada_bias = jnp.sum(g_all.astype(jnp.float32), 0)
    g_activated = lax.dot_general(g_all, ada_weight, (((1,), (1,)), ((), ())), preferred_element_type=jnp.float32)
    g_cond = jax.vjp(jax.nn.silu, cond_full)[1](g_activated)[0]
    grad_level = lax.dot_general(
        onehot, g_cond, (((0,), (0,)), ((), ())), precision=highest, preferred_element_type=jnp.float32
    )
    grad_condition = cut(g_cond, index * count, count).reshape(batches, images, D)

    summed = reduce_all(summed, group, seq)
    grad_down = summed[:, DOWN : DOWN + FF].T.astype(jnp.float32)
    return (
        out_rows.reshape(batches, images, rows, D),
        grad_rows.reshape(batches, images, rows, D),
        grad_condition,
        grad_level,
        grad_ada,
        grad_ada_bias,
        summed[:, QKV : QKV + 3 * D].astype(jnp.float32),
        jnp.concatenate([bias_all[QKV : QKV + D], bias_all[QKV + 2 * D : QKV + 3 * D]]),
        summed[:, OUT : OUT + D].astype(jnp.float32),
        bias_all[OUT : OUT + D],
        summed[:, UP : UP + FF].astype(jnp.float32),
        bias_all[UP : UP + FF],
        grad_down,
        bias_all[DOWN : DOWN + D],
    )


def gather_group_plain(array, index, group):
    size = array.shape[0]
    bit = 1
    while bit < group:
        got = swap(array, [bit] * group)
        high = (index & bit) != 0
        array = jnp.where(high, jnp.concatenate([got, array], 0), jnp.concatenate([array, got], 0))
        bit *= 2
    return array.reshape((group * size,) + array.shape[1:])


def solution(mesh):
    rows = P(None, "grp", "seq", None)
    in_specs = (rows, rows, P(None, "grp", None), P(None, "grp"), P(None, "grp")) + (P(),) * 11
    out_specs = (rows, rows, P(None, "grp", None)) + (P(),) * 11
    body = functools.partial(shards, mesh.shape["grp"], mesh.shape["seq"])
    return jax.shard_map(body, mesh=mesh, in_specs=in_specs, out_specs=out_specs, check_vma=False)
```

time: 2280 us -> 364 us (0.16)
  matrix products: 667 us -> 7.67 us
  blocking collectives: 529 us -> 0 us
  waiting for transfers between devices: 467 us -> 88.9 us
  local copies, waits for them, and re-layouts: 291 us -> 41.5 us
  other arithmetic: 280 us -> 37.9 us
  Pallas kernels: 0 us -> 101 us
  starting transfers between devices: 0.73 us -> 78.5 us
    dot_general x352 -> x6, matrix products: 635 us -> 7.67 us  [the longest x1 2.51 us: shards(): lax.dot_general(activated, g_all, (((0,), (0,)), ((), ())), preferred_ele...]
    all_gather x32 -> x0, blocking collectives: 473 us -> none  [the longest x16 241 us: one_batch(): lax.all_gather(keys_local, 'seq', axis=1, tiled=True)]
    reduce_scatter x32 -> x0, waiting for transfers between devices: 299 us -> none  [the longest x16 297 us: one_batch(): lax.psum_scatter(g_key_terms.reshape(images, SEQ_LEN, D).astype(jnp.bfloa...]
    psum x1 -> x0, waiting for transfers between devices: 167 us -> none  [shards(): lax.psum((final_acc[0], final_acc[1], final_acc[2], final_acc[3], final_a...]
    pallas_call x0 -> x4, Pallas kernels: none -> 101 us  [layer_call(): pl.pallas_call(functools.partial(layer_kernel, parts, first, last), grid=...]
    reduce_sum x112 -> x2, other arithmetic: 97.8 us -> 1.9 us  [the longest x1 1.11 us: shards(): jnp.sum(small[:, own * 6 * D:own * 6 * D + WIDE].astype(jnp.float32), 0)]
    ppermute x0 -> x45, waiting for transfers between devices: none -> 88.9 us  [the longest x33 55 us: seq_shift(): lax.ppermute(array, 'seq', [(i, (i + shift) % size) for i in range(size)])]
    ppermute x0 -> x45, starting transfers between devices: none -> 78.5 us  [the longest x33 71.9 us: seq_shift(): lax.ppermute(array, 'seq', [(i, (i + shift) % size) for i in range(size)])]
  transfers between devices with their start and end apart: 33 -> 45, of which waited for: 18 -> 17; matrix products, arithmetic and copies ran while one was open for 16% -> 18% of each run, Pallas kernels for 0% -> 28%
where the time goes in v1:
time: 364 us; the launch traced here: 359 us
  Pallas kernels  101 us (28%)
  waiting for transfers between devices  88.9 us (24%)
  starting transfers between devices  78.5 us (22%)
  local copies, waits for them, and re-layouts  41.5 us (11%)
  other arithmetic  37.9 us (10%)
  matrix products  7.67 us (2%)
    pallas_call x4, Pallas kernels, layer_call(): pl.pallas_call(functools.partial(layer_kernel, parts, first, last), grid=...  101 us
    ppermute x33, starting transfers between devices, seq_shift(): lax.ppermute(array, 'seq', [(i, (i + shift) % size) for i in range(size)])  71.9 us
    ppermute x33, waiting for transfers between devices, seq_shift(): lax.ppermute(array, 'seq', [(i, (i + shift) % size) for i in range(size)])  55 us
    ppermute x12, waiting for transfers between devices, swap(): lax.ppermute(array, 'grp', [(i, i ^ bit) for i, bit in enumerate(stage)])  33.9 us
    unnamed x103, local copies, waits for them, and re-layouts  19.1 us
    another operation x16, other arithmetic, fetch(): block = jnp.stack([cut(tokens, start, step), cut(cotangent, start, step)])  16.3 us
  transfers between devices with their start and end apart: 45, of which 17 were waited for; matrix products, arithmetic and copies ran while one was open for 18% of the time, Pallas kernels for 28%

profile of v1, /device:TPU:0, one launch (start us, length us, event | category | flops | bytes accessed | tf_op | source)
XLA Modules:
  0.0 358.8 jit_solution(13952648055903023632)
XLA Ops:
  0.8 3.6 dynamic-slice_bitcast_fusion
  5.1 5.1 %collective-permute-start.2 = (bf16[2,2,64,384]{3,2,1,0:T(8,128)(2,1)}, bf16[2,2,64,384]{3,2,1,0:T(8,128)(2,1)S(1)}, u32[]{:S(2)}, u32[]{:S(2)}) collective-permute-start(bf16[2,2,64,384]{3,2,1,0:T(8,128)(2,1)} %pad_maximum_fusion.3), channel_id=1, source_target_pairs={{0,3},{1,0},{2,1},{3,2},{4,7},{5,4},{6,5},{7,6},{8,11},{9,8},{10,9... | collective-permute-start | bytes 589832 | tf_op jit(solution)/shard_map/ppermute | solution.py:277
  13.3 1.9 collective-permute-start.6
  27.2 1.6 pad_maximum_fusion.10
  40.6 2.4 copy.73
  43.0 2.4 copy.74
  45.4 2.3 copy.71
  53.1 2.4 collective-permute-start.8
  56.9 2.0 collective-permute-start.13
  58.9 1.9 collective-permute-start.14
  61.4 5.5 %collective-permute-start.18 = (bf16[2,2,64,384]{3,2,1,0:T(8,128)(2,1)}, bf16[2,2,64,384]{3,2,1,0:T(8,128)(2,1)S(1)}, u32[]{:S(2)}, u32[]{:S(2)}) collective-permute-start(bf16[2,2,64,384]{3,2,1,0:T(8,128)(2,1)} %pad_maximum_fusion.13), channel_id=1, source_target_pairs={{0,2},{1,3},{2,0},{3,1},{4,6},{5,7},{6,4},{7,5},{8,10},{9,11},{10,... | collective-permute-start | bytes 589832 | tf_op jit(solution)/shard_map/ppermute | solution.py:277
  66.9 2.4 collective-permute-start.19
  69.3 9.0 %collective-permute-done.12.refs_2_ = bf16[2,2,64,384]{3,2,1,0:T(8,128)(2,1)S(1)} collective-permute-done((bf16[2,2,64,384]{3,2,1,0:T(8,128)(2,1)}, bf16[2,2,64,384]{3,2,1,0:T(8,128)(2,1)S(1)}, u32[]{:S(2)}, u32[]{:S(2)}) %collective-permute-start.12) | collective-permute-done | bytes 196640 | tf_op jit(solution)/shard_map/ppermute | solution.py:277
  79.5 1.8 maximum_select_fusion.7
  83.6 23.3 %shard_map.299 = (bf16[2,2,64,384]{3,2,1,0:T(8,128)(2,1)S(1)}, bf16[2,2,64,384]{3,2,1,0:T(8,128)(2,1)S(1)}, bf16[2,2,64,384]{3,2,1,0:T(8,128)(2,1)S(1)}, bf16[2,...) custom-call(f32[2,4]{1,0:T(2,128)S(1)} %get-tuple-element.206.refs_0_, ...), custom_call_target="tpu_custom_call" | custom-call | tf_op jit(solution)/shard_map/pallas_call | solution.py:236
  108.2 26.1 %shard_map.300 = (bf16[2,2,64,384]{3,2,1,0:T(8,128)(2,1)S(1)}, bf16[2,2,64,384]{3,2,1,0:T(8,128)(2,1)S(1)}, bf16[2,2,64,384]{3,2,1,0:T(8,128)(2,1)S(1)}, bf16[2,...) custom-call(f32[2,4]{1,0:T(2,128)S(1)} %get-tuple-element.205.refs_0, ...), custom_call_target="tpu_custom_call", output_to_operand_aliasing={{5}: (18, {})} | custom-call | tf_op jit(solution)/shard_map/pallas_call | solution.py:236
  137.2 26.3 %shard_map.301 = (bf16[2,2,64,384]{3,2,1,0:T(8,128)(2,1)S(1)}, bf16[2,2,64,384]{3,2,1,0:T(8,128)(2,1)S(1)}, bf16[2,2,64,384]{3,2,1,0:T(8,128)(2,1)S(1)}, bf16[2,...) custom-call(f32[2,4]{1,0:T(2,128)S(1)} %get-tuple-element.204.refs_0, ...), custom_call_target="tpu_custom_call", output_to_operand_aliasing={{5}: (18, {})} | custom-call | tf_op jit(solution)/shard_map/pallas_call | solution.py:236
  163.6 25.4 %shard_map.302 = (bf16[2,2,64,384]{3,2,1,0:T(8,128)(2,1)S(1)}, bf16[2,2,64,384]{3,2,1,0:T(8,128)(2,1)S(1)}, bf16[2,2,64,384]{3,2,1,0:T(8,128)(2,1)S(1)}, bf16[2,...) custom-call(f32[2,4]{1,0:T(2,128)S(1)} %get-tuple-element.203.refs_0, ...), custom_call_target="tpu_custom_call" | custom-call | tf_op jit(solution)/shard_map/pallas_call | solution.py:236
  189.9 2.1 collective-permute-start.25
  192.0 2.3 collective-permute-start.26
  194.3 1.7 constant_dynamic-slice_fusion.5
  197.6 2.1 collective-permute-start.4
  199.9 9.9 %collective-permute-done.3 = bf16[2,2,64,384]{3,2,1,0:T(8,128)(2,1)S(1)} collective-permute-done((bf16[2,2,64,384]{3,2,1,0:T(8,128)(2,1)S(1)}, bf16[2,2,64,384]{3,2,1,0:T(8,128)(2,1)S(1)}, u32[]{:S(2)}, u32[]{:S(2)}) %collective-permute-start.3) | collective-permute-done | bytes 196640 | tf_op jit(solution)/shard_map/ppermute | solution.py:277
  209.8 3.6 %collective-permute-done.4 = bf16[2,2,64,384]{3,2,1,0:T(8,128)(2,1)S(1)} collective-permute-done((bf16[2,2,64,384]{3,2,1,0:T(8,128)(2,1)S(1)}, bf16[2,2,64,384]{3,2,1,0:T(8,128)(2,1)S(1)}, u32[]{:S(2)}, u32[]{:S(2)}) %collective-permute-start.4) | collective-permute-done | bytes 196640 | tf_op jit(solution)/shard_map/ppermute | solution.py:277
  213.4 2.4 collective-permute-start.10
  215.9 9.2 %collective-permute-start.11 = (bf16[2,2,64,384]{3,2,1,0:T(8,128)(2,1)S(1)}, bf16[2,2,64,384]{3,2,1,0:T(8,128)(2,1)S(1)}, u32[]{:S(2)}, u32[]{:S(2)}) collective-permute-start(bf16[2,2,64,384]{3,2,1,0:T(8,128)(2,1)S(1)} %copy-done.15), channel_id=1, source_target_pairs={{0,1},{1,2},{2,3},{3,0},{4,5},{5,6},{6,7},{7,4},{8,9},{9,10},{10,1... | collective-permute-start | bytes 589832 | tf_op jit(solution)/shard_map/ppermute | solution.py:277
  227.2 5.1 %collective-permute-start.16 = (bf16[2,2,64,384]{3,2,1,0:T(8,128)(2,1)S(1)}, bf16[2,2,64,384]{3,2,1,0:T(8,128)(2,1)S(1)}, u32[]{:S(2)}, u32[]{:S(2)}) collective-permute-start(bf16[2,2,64,384]{3,2,1,0:T(8,128)(2,1)S(1)} %copy-done.13), channel_id=1, source_target_pairs={{0,3},{1,0},{2,1},{3,2},{4,7},{5,4},{6,5},{7,6},{8,11},{9,8},{10,9... | collective-permute-start | bytes 589832 | tf_op jit(solution)/shard_map/ppermute | solution.py:277
  234.8 7.1 %collective-permute-start.17 = (bf16[2,2,64,384]{3,2,1,0:T(8,128)(2,1)S(1)}, bf16[2,2,64,384]{3,2,1,0:T(8,128)(2,1)S(1)}, u32[]{:S(2)}, u32[]{:S(2)}) collective-permute-start(bf16[2,2,64,384]{3,2,1,0:T(8,128)(2,1)S(1)} %copy-done.11), channel_id=1, source_target_pairs={{0,1},{1,2},{2,3},{3,0},{4,5},{5,6},{6,7},{7,4},{8,9},{9,10},{10,1... | collective-permute-start | bytes 589832 | tf_op jit(solution)/shard_map/ppermute | solution.py:277
  242.0 4.9 %collective-permute-done.15 = bf16[2,2,64,384]{3,2,1,0:T(8,128)(2,1)S(1)} collective-permute-done((bf16[2,2,64,384]{3,2,1,0:T(8,128)(2,1)S(1)}, bf16[2,2,64,384]{3,2,1,0:T(8,128)(2,1)S(1)}, u32[]{:S(2)}, u32[]{:S(2)}) %collective-permute-start.15) | collective-permute-done | bytes 196640 | tf_op jit(solution)/shard_map/ppermute | solution.py:277
  248.2 7.7 %collective-permute-done.35 = bf16[48,4608]{1,0:T(8,128)(2,1)S(1)} collective-permute-done((bf16[48,4608]{1,0:T(8,128)(2,1)S(1)}, bf16[48,4608]{1,0:T(8,128)(2,1)S(1)}, u32[]{:S(2)}, u32[]{:S(2)}) %collective-permute-start.35) | collective-permute-done | bytes 442400 | tf_op jit(solution)/shard_map/ppermute | solution.py:273
  256.0 3.8 %collective-permute-start.36 = (bf16[48,1152]{1,0:T(8,128)(2,1)S(1)}, bf16[48,1152]{1,0:T(8,128)(2,1)S(1)}, u32[]{:S(2)}, u32[]{:S(2)}) collective-permute-start(bf16[48,1152]{1,0:T(8,128)(2,1)S(1)} %get-tuple-element.162), channel_id=1, source_target_pairs={{0,2},{1,3},{2,0},{3,1},{4,6},{5,7},{6,4},{7,5},{8,10},{9,11},{10,... | collective-permute-start | bytes 331784 | tf_op jit(solution)/shard_map/ppermute | solution.py:277
  261.0 2.7 collective-permute-start.38
  263.7 2.1 collective-permute-done.36
  265.9 7.1 %collective-permute-start.22 = (bf16[2,2,64,384]{3,2,1,0:T(8,128)(2,1)S(1)}, bf16[2,2,64,384]{3,2,1,0:T(8,128)(2,1)S(1)}, u32[]{:S(2)}, u32[]{:S(2)}) collective-permute-start(bf16[2,2,64,384]{3,2,1,0:T(8,128)(2,1)S(1)} %get-tuple-element.62), channel_id=1, source_target_pairs={{0,3},{1,0},{2,1},{3,2},{4,7},{5,4},{6,5},{7,6},{8,11},{9,8},{10,9... | collective-permute-start | bytes 589832 | tf_op jit(solution)/shard_map/ppermute | solution.py:277
  273.9 10.2 %collective-permute-done.39 = bf16[48,1152]{1,0:T(8,128)(2,1)S(1)} collective-permute-done((bf16[48,1152]{1,0:T(8,128)(2,1)S(1)}, bf16[48,1152]{1,0:T(8,128)(2,1)S(1)}, u32[]{:S(2)}, u32[]{:S(2)}) %collective-permute-start.39) | collective-permute-done | bytes 110624 | tf_op jit(solution)/shard_map/ppermute | solution.py:277
  284.1 7.3 %collective-permute-done.40 = bf16[48,1152]{1,0:T(8,128)(2,1)S(1)} collective-permute-done((bf16[48,1152]{1,0:T(8,128)(2,1)S(1)}, bf16[48,1152]{1,0:T(8,128)(2,1)S(1)}, u32[]{:S(2)}, u32[]{:S(2)}) %collective-permute-start.40) | collective-permute-done | bytes 110624 | tf_op jit(solution)/shard_map/ppermute | solution.py:277
  291.4 4.7 %collective-permute-done.41 = bf16[48,1152]{1,0:T(8,128)(2,1)S(1)} collective-permute-done((bf16[48,1152]{1,0:T(8,128)(2,1)S(1)}, bf16[48,1152]{1,0:T(8,128)(2,1)S(1)}, u32[]{:S(2)}, u32[]{:S(2)}) %collective-permute-start.41) | collective-permute-done | bytes 110624 | tf_op jit(solution)/shard_map/ppermute | solution.py:277
  297.5 8.5 %collective-permute-done.42 = bf16[48,4608]{1,0:T(8,128)(2,1)S(1)} collective-permute-done((bf16[48,4608]{1,0:T(8,128)(2,1)S(1)}, bf16[48,4608]{1,0:T(8,128)(2,1)S(1)}, u32[]{:S(2)}, u32[]{:S(2)}) %collective-permute-start.42) | collective-permute-done | bytes 442400 | tf_op jit(solution)/shard_map/ppermute | solution.py:273
  306.9 2.1 maximum_select_fusion.5
  311.6 7.7 %collective-permute-done.43 = bf16[96,4608]{1,0:T(8,128)(2,1)S(1)} collective-permute-done((bf16[96,4608]{1,0:T(8,128)(2,1)S(1)}, bf16[96,4608]{1,0:T(8,128)(2,1)S(1)}, u32[]{:S(2)}, u32[]{:S(2)}) %collective-permute-start.43) | collective-permute-done | bytes 884768 | tf_op jit(solution)/shard_map/ppermute | solution.py:273
  320.8 9.6 %collective-permute-done.29 = bf16[3072,128]{1,0:T(8,128)(2,1)S(1)} collective-permute-done((bf16[3072,128]{1,0:T(8,128)(2,1)S(1)}, bf16[3072,128]{1,0:T(8,128)(2,1)S(1)}, u32[]{:S(2)}, u32[]{:S(2)}) %collective-permute-start.29) | collective-permute-done | bytes 786464 | tf_op jit(solution)/shard_map/ppermute | solution.py:273
  332.4 2.4 slice.264
  334.8 1.7 reshape.127
  336.5 1.8 fusion.1
  344.4 2.5 fusion.2
  346.9 3.7 %maximum_select_fusion = bf16[384,4608]{1,0:T(8,128)(2,1)S(1)} fusion(bf16[192,4608]{1,0:T(8,128)(2,1)} %collective-permute-done.44, bf16[192,4608]{1,0:T(8,128)(2,1)} %maximum_select_fusion.1, pred[]{:T(512)S(6)} %eq.98), kind=kLoop, calls=%fused_computation | loop fusion | flops 15925248 | bytes 7077889 | tf_op jit(solution)/shard_map/jit(_where)/select_n | solution.py:312
  350.6 2.8 convert_bitcast_fusion
  355.6 3.0 copy.75
  (264 shorter events, 68.3 us)
Async XLA Ops:
  5.1 48.0 %collective-permute-start.2 = (bf16[2,2,64,384]{3,2,1,0:T(8,128)(2,1)}, bf16[2,2,64,384]{3,2,1,0:T(8,128)(2,1)S(1)}, u32[]{:S(2)}, u32[]{:S(2)}) collective-permute-start(bf16[2,2,64,384]{3,2,1,0:T(8,128)(2,1)} %pad_maximum_fusion.3), channel_id=1, source_target_pairs={{0,3},{1,0},{2,1},{3,2},{4,7},{5,4},{6,5},{7,6},{8,11},{9,8},{10,9... | collective-permute-start | bytes 589832 | tf_op jit(solution)/shard_map/ppermute | solution.py:277
  10.9 44.6 %collective-permute-start.1 = (bf16[2,2,64,384]{3,2,1,0:T(8,128)(2,1)}, bf16[2,2,64,384]{3,2,1,0:T(8,128)(2,1)S(1)}, u32[]{:S(2)}, u32[]{:S(2)}) collective-permute-start(bf16[2,2,64,384]{3,2,1,0:T(8,128)(2,1)} %pad_maximum_fusion.2), channel_id=1, source_target_pairs={{0,1},{1,2},{2,3},{3,0},{4,5},{5,6},{6,7},{7,4},{8,9},{9,10},{10,1... | collective-permute-start | bytes 589832 | tf_op jit(solution)/shard_map/ppermute | solution.py:277
  11.6 45.3 %collective-permute-start = (bf16[2,2,64,384]{3,2,1,0:T(8,128)(2,1)}, bf16[2,2,64,384]{3,2,1,0:T(8,128)(2,1)S(1)}, u32[]{:S(2)}, u32[]{:S(2)}) collective-permute-start(bf16[2,2,64,384]{3,2,1,0:T(8,128)(2,1)} %pad_maximum_fusion.1), channel_id=1, source_target_pairs={{0,2},{1,3},{2,0},{3,1},{4,6},{5,7},{6,4},{7,5},{8,10},{9,11},{10,... | collective-permute-start | bytes 589832 | tf_op jit(solution)/shard_map/ppermute | solution.py:277
  13.3 45.7 %collective-permute-start.6 = (bf16[2,2,64,384]{3,2,1,0:T(8,128)(2,1)}, bf16[2,2,64,384]{3,2,1,0:T(8,128)(2,1)S(1)}, u32[]{:S(2)}, u32[]{:S(2)}) collective-permute-start(bf16[2,2,64,384]{3,2,1,0:T(8,128)(2,1)} %pad_maximum_fusion.5), channel_id=1, source_target_pairs={{0,2},{1,3},{2,0},{3,1},{4,6},{5,7},{6,4},{7,5},{8,10},{9,11},{10,... | collective-permute-start | bytes 589832 | tf_op jit(solution)/shard_map/ppermute | solution.py:277
  16.9 15.9 %collective-permute-start.30 = (f32[32,512]{1,0:T(8,128)}, f32[32,512]{1,0:T(8,128)}, u32[]{:S(2)}, u32[]{:S(2)}) collective-permute-start(f32[32,512]{1,0:T(8,128)} %pad_maximum_fusion.16), channel_id=1, source_target_pairs={{0,4},{4,0},{8,12},{12,8},{16,20},{20,16},{24,28},{28,24},{1,5},{5... | collective-permute-start | bytes 196616 | tf_op jit(solution)/shard_map/ppermute | solution.py:273
  34.4 17.1 %collective-permute-start.31 = (f32[64,512]{1,0:T(8,128)}, f32[64,512]{1,0:T(8,128)}, u32[]{:S(2)}, u32[]{:S(2)}) collective-permute-start(f32[64,512]{1,0:T(8,128)} %maximum_select_fusion.8), channel_id=1, source_target_pairs={{0,8},{4,12},{8,0},{12,4},{16,24},{20,28},{24,16},{28,20},{1,9},{5... | collective-permute-start | bytes 393224 | tf_op jit(solution)/shard_map/ppermute | solution.py:273
  51.6 9.9 %collective-permute-start.7 = (bf16[2,2,64,384]{3,2,1,0:T(8,128)(2,1)}, bf16[2,2,64,384]{3,2,1,0:T(8,128)(2,1)S(1)}, u32[]{:S(2)}, u32[]{:S(2)}) collective-permute-start(bf16[2,2,64,384]{3,2,1,0:T(8,128)(2,1)} %pad_maximum_fusion.6), channel_id=1, source_target_pairs={{0,1},{1,2},{2,3},{3,0},{4,5},{5,6},{6,7},{7,4},{8,9},{9,10},{10,1... | collective-permute-start | bytes 589832 | tf_op jit(solution)/shard_map/ppermute | solution.py:277
  53.1 13.9 %collective-permute-start.8 = (bf16[2,2,64,384]{3,2,1,0:T(8,128)(2,1)}, bf16[2,2,64,384]{3,2,1,0:T(8,128)(2,1)S(1)}, u32[]{:S(2)}, u32[]{:S(2)}) collective-permute-start(bf16[2,2,64,384]{3,2,1,0:T(8,128)(2,1)} %pad_maximum_fusion.7), channel_id=1, source_target_pairs={{0,3},{1,0},{2,1},{3,2},{4,7},{5,4},{6,5},{7,6},{8,11},{9,8},{10,9... | collective-permute-start | bytes 589832 | tf_op jit(solution)/shard_map/ppermute | solution.py:277
  55.5 22.8 %collective-permute-start.12 = (bf16[2,2,64,384]{3,2,1,0:T(8,128)(2,1)}, bf16[2,2,64,384]{3,2,1,0:T(8,128)(2,1)S(1)}, u32[]{:S(2)}, u32[]{:S(2)}) collective-permute-start(bf16[2,2,64,384]{3,2,1,0:T(8,128)(2,1)} %pad_maximum_fusion.9), channel_id=1, source_target_pairs={{0,2},{1,3},{2,0},{3,1},{4,6},{5,7},{6,4},{7,5},{8,10},{9,11},{10,... | collective-permute-start | bytes 589832 | tf_op jit(solution)/shard_map/ppermute | solution.py:277
  56.9 78.8 %collective-permute-start.13 = (bf16[2,2,64,384]{3,2,1,0:T(8,128)(2,1)}, bf16[2,2,64,384]{3,2,1,0:T(8,128)(2,1)S(1)}, u32[]{:S(2)}, u32[]{:S(2)}) collective-permute-start(bf16[2,2,64,384]{3,2,1,0:T(8,128)(2,1)} %pad_maximum_fusion.10), channel_id=1, source_target_pairs={{0,1},{1,2},{2,3},{3,0},{4,5},{5,6},{6,7},{7,4},{8,9},{9,10},{10,1... | collective-permute-start | bytes 589832 | tf_op jit(solution)/shard_map/ppermute | solution.py:277
  58.9 78.3 %collective-permute-start.14 = (bf16[2,2,64,384]{3,2,1,0:T(8,128)(2,1)}, bf16[2,2,64,384]{3,2,1,0:T(8,128)(2,1)S(1)}, u32[]{:S(2)}, u32[]{:S(2)}) collective-permute-start(bf16[2,2,64,384]{3,2,1,0:T(8,128)(2,1)} %pad_maximum_fusion.11), channel_id=1, source_target_pairs={{0,3},{1,0},{2,1},{3,2},{4,7},{5,4},{6,5},{7,6},{8,11},{9,8},{10,9... | collective-permute-start | bytes 589832 | tf_op jit(solution)/shard_map/ppermute | solution.py:277
  61.4 102.1 %collective-permute-start.18 = (bf16[2,2,64,384]{3,2,1,0:T(8,128)(2,1)}, bf16[2,2,64,384]{3,2,1,0:T(8,128)(2,1)S(1)}, u32[]{:S(2)}, u32[]{:S(2)}) collective-permute-start(bf16[2,2,64,384]{3,2,1,0:T(8,128)(2,1)} %pad_maximum_fusion.13), channel_id=1, source_target_pairs={{0,2},{1,3},{2,0},{3,1},{4,6},{5,7},{6,4},{7,5},{8,10},{9,11},{10,... | collective-permute-start | bytes 589832 | tf_op jit(solution)/shard_map/ppermute | solution.py:277
  66.9 96.6 %collective-permute-start.19 = (bf16[2,2,64,384]{3,2,1,0:T(8,128)(2,1)}, bf16[2,2,64,384]{3,2,1,0:T(8,128)(2,1)S(1)}, u32[]{:S(2)}, u32[]{:S(2)}) collective-permute-start(bf16[2,2,64,384]{3,2,1,0:T(8,128)(2,1)} %pad_maximum_fusion.14), channel_id=1, source_target_pairs={{0,1},{1,2},{2,3},{3,0},{4,5},{5,6},{6,7},{7,4},{8,9},{9,10},{10,1... | collective-permute-start | bytes 589832 | tf_op jit(solution)/shard_map/ppermute | solution.py:277
  78.3 85.3 %collective-permute-start.20 = (bf16[2,2,64,384]{3,2,1,0:T(8,128)(2,1)S(1)}, bf16[2,2,64,384]{3,2,1,0:T(8,128)(2,1)S(1)}, u32[]{:S(2)}, u32[]{:S(2)}) collective-permute-start(bf16[2,2,64,384]{3,2,1,0:T(8,128)(2,1)S(1)} %pad_maximum_fusion.15), channel_id=1, source_target_pairs={{0,3},{1,0},{2,1},{3,2},{4,7},{5,4},{6,5},{7,6},{8,11},{9,8},{10,9... | collective-permute-start | bytes 589832 | tf_op jit(solution)/shard_map/ppermute | solution.py:277
  135.7 171.2 %collective-permute-start.32 = (f32[128,512]{1,0:T(8,128)}, f32[128,512]{1,0:T(8,128)}, u32[]{:S(2)}, u32[]{:S(2)}) collective-permute-start(f32[128,512]{1,0:T(8,128)} %maximum_select_fusion.7), channel_id=1, source_target_pairs={{0,16},{4,20},{8,24},{12,28},{16,0},{20,4},{24,8},{28,12},{1,17},{... | collective-permute-start | bytes 786440 | tf_op jit(solution)/shard_map/ppermute | solution.py:273
  189.8 7.4 %collective-permute-start.24 = (bf16[192,128]{1,0:T(8,128)(2,1)S(1)}, bf16[192,128]{1,0:T(8,128)(2,1)S(1)}, u32[]{:S(2)}, u32[]{:S(2)}) collective-permute-start(bf16[192,128]{1,0:T(8,128)(2,1)S(1)} %fusion.36), channel_id=1, source_target_pairs={{0,2},{1,3},{2,0},{3,1},{4,6},{5,7},{6,4},{7,5},{8,10},{9,11},{10,... | collective-permute-start | bytes 147464 | tf_op jit(solution)/shard_map/ppermute | solution.py:277
  189.9 7.7 %collective-permute-start.25 = (bf16[192,128]{1,0:T(8,128)(2,1)S(1)}, bf16[192,128]{1,0:T(8,128)(2,1)S(1)}, u32[]{:S(2)}, u32[]{:S(2)}) collective-permute-start(bf16[192,128]{1,0:T(8,128)(2,1)S(1)} %fusion.36), channel_id=1, source_target_pairs={{0,1},{1,2},{2,3},{3,0},{4,5},{5,6},{6,7},{7,4},{8,9},{9,10},{10,1... | collective-permute-start | bytes 147464 | tf_op jit(solution)/shard_map/ppermute | solution.py:277
  192.0 7.8 %collective-permute-start.26 = (bf16[192,128]{1,0:T(8,128)(2,1)S(1)}, bf16[192,128]{1,0:T(8,128)(2,1)S(1)}, u32[]{:S(2)}, u32[]{:S(2)}) collective-permute-start(bf16[192,128]{1,0:T(8,128)(2,1)S(1)} %fusion.36), channel_id=1, source_target_pairs={{0,3},{1,0},{2,1},{3,2},{4,7},{5,4},{6,5},{7,6},{8,11},{9,8},{10,9... | collective-permute-start | bytes 147464 | tf_op jit(solution)/shard_map/ppermute | solution.py:277
  194.3 38.0 %copy-start.28 = (bf16[384,4608]{1,0:T(8,128)(2,1)S(1)}, bf16[384,4608]{1,0:T(8,128)(2,1)}, u32[]{:S(2)}) copy-start(bf16[384,4608]{1,0:T(8,128)(2,1)} %get-tuple-element.69) | copy-start | bytes 10616836
  196.0 31.2 %collective-permute-start.33 = (bf16[192,4608]{1,0:T(8,128)(2,1)S(1)}, bf16[192,4608]{1,0:T(8,128)(2,1)S(1)}, u32[]{:S(2)}, u32[]{:S(2)}) collective-permute-start(bf16[192,4608]{1,0:T(8,128)(2,1)S(1)} %constant_dynamic-slice_fusion.5), channel_id=1, source_target_pairs={{0,4},{4,0},{8,12},{12,8},{16,20},{20,16},{24,28},{28,24},{1,5},{5... | collective-permute-start | bytes 5308424 | tf_op jit(solution)/shard_map/ppermute | solution.py:273
  196.7 29.2 %copy-start.17 = (bf16[2,2,64,384]{3,2,1,0:T(8,128)(2,1)S(1)}, bf16[2,2,64,384]{3,2,1,0:T(8,128)(2,1)}, u32[]{:S(2)}) copy-start(bf16[2,2,64,384]{3,2,1,0:T(8,128)(2,1)} %copy-done.16) | copy-start | bytes 589828
  196.7 30.5 %copy-start.13 = (bf16[2,2,64,384]{3,2,1,0:T(8,128)(2,1)S(1)}, bf16[2,2,64,384]{3,2,1,0:T(8,128)(2,1)}, u32[]{:S(2)}) copy-start(bf16[2,2,64,384]{3,2,1,0:T(8,128)(2,1)} %copy-done.12) | copy-start | bytes 589828
  197.3 12.5 %collective-permute-start.3 = (bf16[2,2,64,384]{3,2,1,0:T(8,128)(2,1)S(1)}, bf16[2,2,64,384]{3,2,1,0:T(8,128)(2,1)S(1)}, u32[]{:S(2)}, u32[]{:S(2)}) collective-permute-start(bf16[2,2,64,384]{3,2,1,0:T(8,128)(2,1)S(1)} %copy-done.27), channel_id=1, source_target_pairs={{0,2},{1,3},{2,0},{3,1},{4,6},{5,7},{6,4},{7,5},{8,10},{9,11},{10,... | collective-permute-start | bytes 589832 | tf_op jit(solution)/shard_map/ppermute | solution.py:277
  197.6 15.8 %collective-permute-start.4 = (bf16[2,2,64,384]{3,2,1,0:T(8,128)(2,1)S(1)}, bf16[2,2,64,384]{3,2,1,0:T(8,128)(2,1)S(1)}, u32[]{:S(2)}, u32[]{:S(2)}) collective-permute-start(bf16[2,2,64,384]{3,2,1,0:T(8,128)(2,1)S(1)} %copy-done.25), channel_id=1, source_target_pairs={{0,3},{1,0},{2,1},{3,2},{4,7},{5,4},{6,5},{7,6},{8,11},{9,8},{10,9... | collective-permute-start | bytes 589832 | tf_op jit(solution)/shard_map/ppermute | solution.py:277
  199.8 16.1 %collective-permute-start.5 = (bf16[2,2,64,384]{3,2,1,0:T(8,128)(2,1)S(1)}, bf16[2,2,64,384]{3,2,1,0:T(8,128)(2,1)S(1)}, u32[]{:S(2)}, u32[]{:S(2)}) collective-permute-start(bf16[2,2,64,384]{3,2,1,0:T(8,128)(2,1)S(1)} %copy-done.23), channel_id=1, source_target_pairs={{0,1},{1,2},{2,3},{3,0},{4,5},{5,6},{6,7},{7,4},{8,9},{9,10},{10,1... | collective-permute-start | bytes 589832 | tf_op jit(solution)/shard_map/ppermute | solution.py:277
  209.8 16.1 %collective-permute-start.9 = (bf16[2,2,64,384]{3,2,1,0:T(8,128)(2,1)S(1)}, bf16[2,2,64,384]{3,2,1,0:T(8,128)(2,1)S(1)}, u32[]{:S(2)}, u32[]{:S(2)}) collective-permute-start(bf16[2,2,64,384]{3,2,1,0:T(8,128)(2,1)S(1)} %copy-done.21), channel_id=1, source_target_pairs={{0,2},{1,3},{2,0},{3,1},{4,6},{5,7},{6,4},{7,5},{8,10},{9,11},{10,... | collective-permute-start | bytes 589832 | tf_op jit(solution)/shard_map/ppermute | solution.py:277
  213.4 20.8 %collective-permute-start.10 = (bf16[2,2,64,384]{3,2,1,0:T(8,128)(2,1)S(1)}, bf16[2,2,64,384]{3,2,1,0:T(8,128)(2,1)S(1)}, u32[]{:S(2)}, u32[]{:S(2)}) collective-permute-start(bf16[2,2,64,384]{3,2,1,0:T(8,128)(2,1)S(1)} %copy-done.19), channel_id=1, source_target_pairs={{0,3},{1,0},{2,1},{3,2},{4,7},{5,4},{6,5},{7,6},{8,11},{9,8},{10,9... | collective-permute-start | bytes 589832 | tf_op jit(solution)/shard_map/ppermute | solution.py:277
  215.9 18.9 %collective-permute-start.11 = (bf16[2,2,64,384]{3,2,1,0:T(8,128)(2,1)S(1)}, bf16[2,2,64,384]{3,2,1,0:T(8,128)(2,1)S(1)}, u32[]{:S(2)}, u32[]{:S(2)}) collective-permute-start(bf16[2,2,64,384]{3,2,1,0:T(8,128)(2,1)S(1)} %copy-done.15), channel_id=1, source_target_pairs={{0,1},{1,2},{2,3},{3,0},{4,5},{5,6},{6,7},{7,4},{8,9},{9,10},{10,1... | collective-permute-start | bytes 589832 | tf_op jit(solution)/shard_map/ppermute | solution.py:277
  225.8 21.1 %collective-permute-start.15 = (bf16[2,2,64,384]{3,2,1,0:T(8,128)(2,1)S(1)}, bf16[2,2,64,384]{3,2,1,0:T(8,128)(2,1)S(1)}, u32[]{:S(2)}, u32[]{:S(2)}) collective-permute-start(bf16[2,2,64,384]{3,2,1,0:T(8,128)(2,1)S(1)} %copy-done.17), channel_id=1, source_target_pairs={{0,2},{1,3},{2,0},{3,1},{4,6},{5,7},{6,4},{7,5},{8,10},{9,11},{10,... | collective-permute-start | bytes 589832 | tf_op jit(solution)/shard_map/ppermute | solution.py:277
  227.2 20.9 %collective-permute-start.16 = (bf16[2,2,64,384]{3,2,1,0:T(8,128)(2,1)S(1)}, bf16[2,2,64,384]{3,2,1,0:T(8,128)(2,1)S(1)}, u32[]{:S(2)}, u32[]{:S(2)}) collective-permute-start(bf16[2,2,64,384]{3,2,1,0:T(8,128)(2,1)S(1)} %copy-done.13), channel_id=1, source_target_pairs={{0,3},{1,0},{2,1},{3,2},{4,7},{5,4},{6,5},{7,6},{8,11},{9,8},{10,9... | collective-permute-start | bytes 589832 | tf_op jit(solution)/shard_map/ppermute | solution.py:277
  234.2 13.0 %collective-permute-start.34 = (bf16[96,4608]{1,0:T(8,128)(2,1)S(1)}, bf16[96,4608]{1,0:T(8,128)(2,1)S(1)}, u32[]{:S(2)}, u32[]{:S(2)}) collective-permute-start(bf16[96,4608]{1,0:T(8,128)(2,1)S(1)} %constant_dynamic-slice_fusion.4), channel_id=1, source_target_pairs={{0,8},{4,20},{8,0},{12,28},{16,24},{20,4},{24,16},{28,12},{1,9},{5... | collective-permute-start | bytes 2654216 | tf_op jit(solution)/shard_map/ppermute | solution.py:273
  234.8 13.3 %collective-permute-start.17 = (bf16[2,2,64,384]{3,2,1,0:T(8,128)(2,1)S(1)}, bf16[2,2,64,384]{3,2,1,0:T(8,128)(2,1)S(1)}, u32[]{:S(2)}, u32[]{:S(2)}) collective-permute-start(bf16[2,2,64,384]{3,2,1,0:T(8,128)(2,1)S(1)} %copy-done.11), channel_id=1, source_target_pairs={{0,1},{1,2},{2,3},{3,0},{4,5},{5,6},{6,7},{7,4},{8,9},{9,10},{10,1... | collective-permute-start | bytes 589832 | tf_op jit(solution)/shard_map/ppermute | solution.py:277
  246.9 26.3 %collective-permute-start.21 = (bf16[2,2,64,384]{3,2,1,0:T(8,128)(2,1)S(1)}, bf16[2,2,64,384]{3,2,1,0:T(8,128)(2,1)S(1)}, u32[]{:S(2)}, u32[]{:S(2)}) collective-permute-start(bf16[2,2,64,384]{3,2,1,0:T(8,128)(2,1)S(1)} %copy-done.9), channel_id=1, source_target_pairs={{0,2},{1,3},{2,0},{3,1},{4,6},{5,7},{6,4},{7,5},{8,10},{9,11},{10,... | collective-permute-start | bytes 589832 | tf_op jit(solution)/shard_map/ppermute | solution.py:277
  247.5 8.4 %collective-permute-start.35 = (bf16[48,4608]{1,0:T(8,128)(2,1)S(1)}, bf16[48,4608]{1,0:T(8,128)(2,1)S(1)}, u32[]{:S(2)}, u32[]{:S(2)}) collective-permute-start(bf16[48,4608]{1,0:T(8,128)(2,1)S(1)} %constant_dynamic-slice_fusion.3), channel_id=1, source_target_pairs={{0,16},{4,12},{8,24},{12,4},{16,0},{20,28},{24,8},{28,20},{1,17},{... | collective-permute-start | bytes 1327112 | tf_op jit(solution)/shard_map/ppermute | solution.py:273
  256.0 9.8 %collective-permute-start.36 = (bf16[48,1152]{1,0:T(8,128)(2,1)S(1)}, bf16[48,1152]{1,0:T(8,128)(2,1)S(1)}, u32[]{:S(2)}, u32[]{:S(2)}) collective-permute-start(bf16[48,1152]{1,0:T(8,128)(2,1)S(1)} %get-tuple-element.162), channel_id=1, source_target_pairs={{0,2},{1,3},{2,0},{3,1},{4,6},{5,7},{6,4},{7,5},{8,10},{9,11},{10,... | collective-permute-start | bytes 331784 | tf_op jit(solution)/shard_map/ppermute | solution.py:277
  259.9 13.1 %collective-permute-start.37 = (bf16[48,1152]{1,0:T(8,128)(2,1)S(1)}, bf16[48,1152]{1,0:T(8,128)(2,1)S(1)}, u32[]{:S(2)}, u32[]{:S(2)}) collective-permute-start(bf16[48,1152]{1,0:T(8,128)(2,1)S(1)} %get-tuple-element.164), channel_id=1, source_target_pairs={{0,1},{1,2},{2,3},{3,0},{4,5},{5,6},{6,7},{7,4},{8,9},{9,10},{10,1... | collective-permute-start | bytes 331784 | tf_op jit(solution)/shard_map/ppermute | solution.py:277
  261.0 12.0 %collective-permute-start.38 = (bf16[48,1152]{1,0:T(8,128)(2,1)S(1)}, bf16[48,1152]{1,0:T(8,128)(2,1)S(1)}, u32[]{:S(2)}, u32[]{:S(2)}) collective-permute-start(bf16[48,1152]{1,0:T(8,128)(2,1)S(1)} %get-tuple-element.163), channel_id=1, source_target_pairs={{0,3},{1,0},{2,1},{3,2},{4,7},{5,4},{6,5},{7,6},{8,11},{9,8},{10,9... | collective-permute-start | bytes 331784 | tf_op jit(solution)/shard_map/ppermute | solution.py:277
  265.9 30.9 %collective-permute-start.22 = (bf16[2,2,64,384]{3,2,1,0:T(8,128)(2,1)S(1)}, bf16[2,2,64,384]{3,2,1,0:T(8,128)(2,1)S(1)}, u32[]{:S(2)}, u32[]{:S(2)}) collective-permute-start(bf16[2,2,64,384]{3,2,1,0:T(8,128)(2,1)S(1)} %get-tuple-element.62), channel_id=1, source_target_pairs={{0,3},{1,0},{2,1},{3,2},{4,7},{5,4},{6,5},{7,6},{8,11},{9,8},{10,9... | collective-permute-start | bytes 589832 | tf_op jit(solution)/shard_map/ppermute | solution.py:277
  273.0 33.8 %collective-permute-start.23 = (bf16[2,2,64,384]{3,2,1,0:T(8,128)(2,1)S(1)}, bf16[2,2,64,384]{3,2,1,0:T(8,128)(2,1)S(1)}, u32[]{:S(2)}, u32[]{:S(2)}) collective-permute-start(bf16[2,2,64,384]{3,2,1,0:T(8,128)(2,1)S(1)} %get-tuple-element.63), channel_id=1, source_target_pairs={{0,1},{1,2},{2,3},{3,0},{4,5},{5,6},{6,7},{7,4},{8,9},{9,10},{10,1... | collective-permute-start | bytes 589832 | tf_op jit(solution)/shard_map/ppermute | solution.py:277
  273.0 23.8 %collective-permute-start.27 = (bf16[768,128]{1,0:T(8,128)(2,1)S(1)}, bf16[768,128]{1,0:T(8,128)(2,1)S(1)}, u32[]{:S(2)}, u32[]{:S(2)}) collective-permute-start(bf16[768,128]{1,0:T(8,128)(2,1)S(1)} %constant_dynamic-update-slice_fusion.4), channel_id=1, source_target_pairs={{0,4},{4,0},{8,12},{12,8},{16,20},{20,16},{24,28},{28,24},{1,5},{5... | collective-permute-start | bytes 589832 | tf_op jit(solution)/shard_map/ppermute | solution.py:273
  273.2 10.9 %collective-permute-start.39 = (bf16[48,1152]{1,0:T(8,128)(2,1)S(1)}, bf16[48,1152]{1,0:T(8,128)(2,1)S(1)}, u32[]{:S(2)}, u32[]{:S(2)}) collective-permute-start(bf16[48,1152]{1,0:T(8,128)(2,1)S(1)} %get-tuple-element.127), channel_id=1, source_target_pairs={{0,2},{1,3},{2,0},{3,1},{4,6},{5,7},{6,4},{7,5},{8,10},{9,11},{10,... | collective-permute-start | bytes 331784 | tf_op jit(solution)/shard_map/ppermute | solution.py:277
  284.1 7.3 %collective-permute-start.40 = (bf16[48,1152]{1,0:T(8,128)(2,1)S(1)}, bf16[48,1152]{1,0:T(8,128)(2,1)S(1)}, u32[]{:S(2)}, u32[]{:S(2)}) collective-permute-start(bf16[48,1152]{1,0:T(8,128)(2,1)S(1)} %get-tuple-element.127), channel_id=1, source_target_pairs={{0,1},{1,2},{2,3},{3,0},{4,5},{5,6},{6,7},{7,4},{8,9},{9,10},{10,1... | collective-permute-start | bytes 331784 | tf_op jit(solution)/shard_map/ppermute | solution.py:277
  291.4 4.7 %collective-permute-start.41 = (bf16[48,1152]{1,0:T(8,128)(2,1)S(1)}, bf16[48,1152]{1,0:T(8,128)(2,1)S(1)}, u32[]{:S(2)}, u32[]{:S(2)}) collective-permute-start(bf16[48,1152]{1,0:T(8,128)(2,1)S(1)} %get-tuple-element.127), channel_id=1, source_target_pairs={{0,3},{1,0},{2,1},{3,2},{4,7},{5,4},{6,5},{7,6},{8,11},{9,8},{10,9... | collective-permute-start | bytes 331784 | tf_op jit(solution)/shard_map/ppermute | solution.py:277
  296.2 9.8 %collective-permute-start.42 = (bf16[48,4608]{1,0:T(8,128)(2,1)S(1)}, bf16[48,4608]{1,0:T(8,128)(2,1)S(1)}, u32[]{:S(2)}, u32[]{:S(2)}) collective-permute-start(bf16[48,4608]{1,0:T(8,128)(2,1)S(1)} %constant_dynamic-update-slice_fusion.3), channel_id=1, source_target_pairs={{0,16},{4,12},{8,24},{12,4},{16,0},{20,28},{24,8},{28,20},{1,17},{... | collective-permute-start | bytes 1327112 | tf_op jit(solution)/shard_map/ppermute | solution.py:273
  296.9 12.8 %collective-permute-start.28 = (bf16[1536,128]{1,0:T(8,128)(2,1)S(1)}, bf16[1536,128]{1,0:T(8,128)(2,1)S(1)}, u32[]{:S(2)}, u32[]{:S(2)}) collective-permute-start(bf16[1536,128]{1,0:T(8,128)(2,1)S(1)} %maximum_select_fusion.6), channel_id=1, source_target_pairs={{0,8},{4,12},{8,0},{12,4},{16,24},{20,28},{24,16},{28,20},{1,9},{5... | collective-permute-start | bytes 1179656 | tf_op jit(solution)/shard_map/ppermute | solution.py:273
  306.2 13.1 %collective-permute-start.43 = (bf16[96,4608]{1,0:T(8,128)(2,1)S(1)}, bf16[96,4608]{1,0:T(8,128)(2,1)S(1)}, u32[]{:S(2)}, u32[]{:S(2)}) collective-permute-start(bf16[96,4608]{1,0:T(8,128)(2,1)S(1)} %maximum_select_fusion.3), channel_id=1, source_target_pairs={{0,8},{4,20},{8,0},{12,28},{16,24},{20,4},{24,16},{28,12},{1,9},{5... | collective-permute-start | bytes 2654216 | tf_op jit(solution)/shard_map/ppermute | solution.py:273
  309.9 20.5 %collective-permute-start.29 = (bf16[3072,128]{1,0:T(8,128)(2,1)S(1)}, bf16[3072,128]{1,0:T(8,128)(2,1)S(1)}, u32[]{:S(2)}, u32[]{:S(2)}) collective-permute-start(bf16[3072,128]{1,0:T(8,128)(2,1)S(1)} %maximum_select_fusion.4), channel_id=1, source_target_pairs={{0,16},{4,20},{8,24},{12,28},{16,0},{20,4},{24,8},{28,12},{1,17},{... | collective-permute-start | bytes 2359304 | tf_op jit(solution)/shard_map/ppermute | solution.py:273
  320.8 26.1 %collective-permute-start.44 = (bf16[192,4608]{1,0:T(8,128)(2,1)}, bf16[192,4608]{1,0:T(8,128)(2,1)}, u32[]{:S(2)}, u32[]{:S(2)}) collective-permute-start(bf16[192,4608]{1,0:T(8,128)(2,1)} %maximum_select_fusion.1), channel_id=1, source_target_pairs={{0,4},{4,0},{8,12},{12,8},{16,20},{20,16},{24,28},{28,24},{1,5},{5... | collective-permute-start | bytes 5308424 | tf_op jit(solution)/shard_map/ppermute | solution.py:273
  (45 other events, 450.7 us)

commit v2 on v1

v2 whole, which is shorter than its diff:
```python
import functools
import math

import jax
import jax.numpy as jnp
from jax import lax
from jax.experimental import pallas as pl
from jax.experimental.pallas import tpu as pltpu
from jax.sharding import PartitionSpec as P

D = 384
HEADS = 6
HEAD_DIM = 64
FF = 1536
SEQ_LEN = 256
KEEP = 128
LEVELS = 64
EPSILON = 1e-06
highest = lax.Precision.HIGHEST

UP, DOWN, QKV, OUT, WIDE = 0, FF, 2 * FF, 2 * FF + 3 * D, 2 * FF + 4 * D
FF_TILE = 1536
CHUNKS = (2, 3, 3)
GROUPS = ((0, 1), (2,))
PAD = 8
KERNEL_FLOPS = 30_000_000_000


def dot_nn(a, b):
    return lax.dot_general(a, b, (((1,), (0,)), ((), ())), preferred_element_type=jnp.float32)


def dot_nt(a, b):
    return lax.dot_general(a, b, (((1,), (1,)), ((), ())), preferred_element_type=jnp.float32)


def dot_tn(a, b):
    return lax.dot_general(a, b, (((0,), (0,)), ((), ())), preferred_element_type=jnp.float32)


def row_mean(values):
    return jnp.mean(values, -1, keepdims=True)


def layer_norm(values):
    centered = values - row_mean(values)
    rstd = lax.rsqrt(row_mean(centered * centered) + EPSILON)
    return centered * rstd, rstd


def norm_back(grad, normed, rstd):
    return rstd * (grad - row_mean(grad) - normed * row_mean(grad * normed))


def col_sum(values):
    return jnp.sum(values, 0, keepdims=True)


def layer_kernel(parts, first, last, placed, *refs):
    live_ref = refs[0]
    ins = refs[1 : 1 + parts]
    (mod_ref, wqkv, wout, wup, wdown, bqkv, bout, bup, bdown) = refs[1 + parts : 10 + parts]
    rest = refs[10 + parts :]
    if not first:
        acc_in, bias_in = rest[:2]
        rest = rest[2:]
    if placed:
        rest = rest[parts:]
    outs = rest[:parts]
    gmod_ref, acc_out, bias_acc, acc, probs_ref, sem = rest[parts : parts + 6]
    acc_low = rest[parts + 6] if last else acc
    step = pl.program_id(0)
    steps = pl.num_programs(0)

    def send(start, stop, slot):
        @pl.when(step == steps - 1)
        def _():
            if last:
                acc_low[:, start:stop] = acc[:, start:stop].astype(jnp.bfloat16)
            sent(start, stop, slot).start()

    def sent(start, stop, slot):
        return pltpu.make_async_copy(acc_low.at[:, start:stop], acc_out.at[:, start:stop], sem.at[slot])

    @pl.when(step == 0)
    def _():
        if first:
            acc[...] = jnp.zeros_like(acc)
            bias_acc[...] = jnp.zeros_like(bias_acc)
        else:
            pltpu.make_async_copy(acc_in, acc, sem.at[0]).start()
            bias_acc[...] = bias_in[...]

    rows = ins[0].shape[2]
    full = parts * rows
    tokens = jnp.concatenate([ref[0, 0] for ref in ins], 0).astype(jnp.float32)
    live_parts = [live_ref[step, p] for p in range(parts)]
    live = jnp.concatenate([jnp.full((rows, 1), flag, jnp.float32) for flag in live_parts], 0)
    key_part = lax.broadcasted_iota(jnp.int32, (1, full), 1) // rows
    live_keys = jnp.zeros((1, full), jnp.float32)
    for p in range(parts):
        live_keys = jnp.where(key_part == p, live_parts[p], live_keys)
    live_keys = live_keys > 0.5
    mod = mod_ref[0]
    shift_one, scale_one, gate_one = mod[0:1], 1.0 + mod[1:2], mod[2:3]
    shift_two, scale_two, gate_two = mod[3:4], 1.0 + mod[4:5], mod[5:6]

    norm_one, rstd_one = layer_norm(tokens)
    in_one = (norm_one * scale_one + shift_one).astype(jnp.bfloat16)
    projected = dot_nn(in_one, wqkv[...]) + bqkv[...]
    inv_root = 1.0 / math.sqrt(HEAD_DIM)
    queries = (projected[:, :D].astype(jnp.bfloat16) * jnp.bfloat16(inv_root)).astype(jnp.bfloat16)
    keys = projected[:, D : 2 * D].astype(jnp.bfloat16)
    values = projected[:, 2 * D :].astype(jnp.bfloat16)
    lanes = lax.broadcasted_iota(jnp.int32, (1, 2 * HEAD_DIM), 1)
    halves = (lanes < HEAD_DIM, lanes >= HEAD_DIM)

    def pair(array, j):
        return array[:, j * 2 * HEAD_DIM : (j + 1) * 2 * HEAD_DIM]

    def half(array, h):
        return jnp.where(halves[h], array, jnp.zeros_like(array))

    def head_scores(n):
        j, h = divmod(n, 2)
        return jnp.where(live_keys, dot_nt(pair(queries, j), half(pair(keys, j), h)), -1e30)

    attended = []
    every = [head_scores(n) for n in range(HEADS)]
    for n in range(HEADS):
        scores, ahead = every[n], None
        j, h = divmod(n, 2)
        exps = jnp.exp(scores - jnp.max(scores, -1, keepdims=True))
        probs = exps * (1.0 / jnp.sum(exps, -1, keepdims=True))
        probs_ref[n] = probs
        term = dot_nn(probs.astype(jnp.bfloat16), half(pair(values, j), h))
        if h == 0:
            total = term
        else:
            attended.append((total + term).astype(jnp.bfloat16))
        scores = ahead
    attended = jnp.concatenate(attended, 1)
    attn_branch = dot_nn(attended, wout[...]) + bout[...]
    live_gate_one = live * gate_one
    residual = tokens + live_gate_one * attn_branch
    norm_two, rstd_two = layer_norm(residual)
    in_two = (norm_two * scale_two + shift_two).astype(jnp.bfloat16)

    g_output = jnp.concatenate([ref[1, 0] for ref in ins], 0).astype(jnp.float32)
    live_out = live * g_output
    g_ffn = (live_out * gate_two).astype(jnp.bfloat16)
    if not first:

        @pl.when(step == 0)
        def _():
            pltpu.make_async_copy(acc_in, acc, sem.at[0]).wait()

    in_two_t = in_two.T
    g_ffn_t = g_ffn.T
    ffn = None
    g_in_two = None
    root = math.sqrt(2.0 / math.pi)
    for tile in range(FF // FF_TILE):
        cols = slice(tile * FF_TILE, (tile + 1) * FF_TILE)
        pre = dot_nn(in_two, wup[:, cols]) + bup[:, cols]
        square = pre * pre
        gate = 0.5 + 0.5 * jnp.tanh(pre * (root + (root * 0.044715) * square))
        hidden_wide = pre * gate
        slope = gate + hidden_wide * (1.0 - gate) * (2.0 * root + (6.0 * root * 0.044715) * square)
        hidden = hidden_wide.astype(jnp.bfloat16)
        term = dot_nn(hidden, wdown[cols, :])
        ffn = term if ffn is None else ffn + term
        g_pre_wide = dot_nt(g_ffn, wdown[cols, :]) * slope
        g_pre = g_pre_wide.astype(jnp.bfloat16)
        acc[:, DOWN + tile * FF_TILE : DOWN + (tile + 1) * FF_TILE] += dot_nn(g_ffn_t, hidden)
        acc[:, UP + tile * FF_TILE : UP + (tile + 1) * FF_TILE] += dot_nn(in_two_t, g_pre)
        bias_acc[:, UP + tile * FF_TILE : UP + (tile + 1) * FF_TILE] += col_sum(g_pre.astype(jnp.float32))
        term = dot_nt(g_pre, wup[:, cols])
        g_in_two = term if g_in_two is None else g_in_two + term
    send(UP, QKV, 0)
    bias_acc[:, DOWN : DOWN + D] += col_sum(g_ffn.astype(jnp.float32))
    ffn = ffn + bdown[...]
    layer_out = (residual + live * gate_two * ffn).astype(jnp.bfloat16)
    for p in range(parts):
        outs[p][0, 0] = layer_out[p * rows : (p + 1) * rows]
    gmod_ref[0, 5:6] = col_sum(live_out * ffn)
    gmod_ref[0, 4:5] = col_sum(g_in_two * norm_two)
    gmod_ref[0, 3:4] = col_sum(g_in_two)
    g_residual = g_output + norm_back(g_in_two * scale_two, norm_two, rstd_two)
    g_attn = (live_gate_one * g_residual).astype(jnp.bfloat16)
    gmod_ref[0, 2:3] = col_sum(live * g_residual * attn_branch)
    acc[:, OUT : OUT + D] += dot_tn(attended, g_attn)
    bias_acc[:, OUT : OUT + D] += col_sum(g_attn.astype(jnp.float32))
    g_attended = dot_nt(g_attn, wout[...]).astype(jnp.bfloat16)

    g_queries, g_keys, g_values = [], [], []

    def head_probs(n):
        j, h = divmod(n, 2)
        return dot_nt(pair(g_attended, j), half(pair(values, j), h))

    queries_t = queries.T
    g_attended_t = g_attended.T
    every = [head_probs(n) for n in range(HEADS)]
    for n in range(HEADS):
        j, h = divmod(n, 2)
        head = slice(n * HEAD_DIM, (n + 1) * HEAD_DIM)
        probs = probs_ref[n]
        weighted = probs * every[n]
        g_scores = (weighted - probs * jnp.sum(weighted, -1, keepdims=True)).astype(jnp.bfloat16)
        tq = dot_nn(g_scores, half(pair(keys, j), h))
        g_keys.append(dot_nn(queries_t[head], g_scores).astype(jnp.bfloat16))
        g_values.append(dot_nn(g_attended_t[head], probs.astype(jnp.bfloat16)).astype(jnp.bfloat16))
        if h == 0:
            gq = tq
        else:
            g_queries.append(((gq + tq) * inv_root).astype(jnp.bfloat16))
    g_keys = [jnp.concatenate(g_keys, 0).T]
    g_values = [jnp.concatenate(g_values, 0).T]
    g_projected = jnp.concatenate(g_queries + g_keys + g_values, 1)
    acc[:, QKV : QKV + 3 * D] += dot_tn(in_one, g_projected)
    send(QKV, WIDE, 1)
    bias_acc[:, QKV : QKV + 3 * D] += col_sum(g_projected.astype(jnp.float32))
    g_in_one = dot_nt(g_projected, wqkv[...])
    gmod_ref[0, 1:2] = col_sum(g_in_one * norm_one)
    gmod_ref[0, 0:1] = col_sum(g_in_one)
    g_tokens = (g_residual + norm_back(g_in_one * scale_one, norm_one, rstd_one)).astype(jnp.bfloat16)
    for p in range(parts):
        outs[p][1, 0] = g_tokens[p * rows : (p + 1) * rows]

    @pl.when(step == steps - 1)
    def _():
        sent(UP, QKV, 0).wait()
        sent(QKV, WIDE, 1).wait()


def layer_call(live, blocks, mod, weights, carried, buffers, place, size, last):
    parts = len(blocks)
    images, rows = blocks[0].shape[1:3]
    first = carried is None
    resident = [pl.BlockSpec(w.shape, lambda i: (0, 0), pipeline_mode=pl.Buffered(1)) for w in weights]
    block_spec = pl.BlockSpec((2, 1, rows, D), lambda i: (0, i, 0, 0))
    out_spec = pl.BlockSpec((2, 1, rows, D), lambda i: (0, i + place, 0, 0))
    mod_spec = pl.BlockSpec((1, 6, D), lambda i: (i, 0, 0))
    any_spec = pl.BlockSpec(memory_space=pl.ANY)
    bias_spec = pl.BlockSpec((1, WIDE), lambda i: (0, 0))
    in_specs = (
        [pl.BlockSpec(memory_space=pltpu.SMEM)] + [block_spec] * parts + [mod_spec] + resident
    )
    args = [live, *blocks, mod, *weights]
    aliases = {}
    if not first:
        in_specs += [any_spec, bias_spec]
        if not last:
            aliases[len(args)] = parts + 1
        args += list(carried)
    if buffers is not None:
        in_specs += [any_spec] * parts
        aliases.update({len(args) + p: p for p in range(parts)})
        args += list(buffers)
    acc_type = jnp.bfloat16 if last else jnp.float32
    scratch = [
        pltpu.VMEM((D, WIDE), jnp.float32),
        pltpu.VMEM((HEADS, parts * rows, parts * rows), jnp.float32),
        pltpu.SemaphoreType.DMA((2,)),
    ]
    if last:
        scratch.append(pltpu.VMEM((D, WIDE), jnp.bfloat16))
    result = pl.pallas_call(
        functools.partial(layer_kernel, parts, first, last, buffers is not None),
        grid=(images,),
        in_specs=in_specs,
        out_specs=[out_spec] * parts + [mod_spec, any_spec, bias_spec],
        out_shape=[jax.ShapeDtypeStruct((2, size, rows, D), jnp.bfloat16)] * parts
        + [
            jax.ShapeDtypeStruct((images, 6, D), jnp.float32),
            jax.ShapeDtypeStruct((D, WIDE), acc_type),
            jax.ShapeDtypeStruct((1, WIDE), jnp.float32),
        ],
        scratch_shapes=scratch,
        input_output_aliases=aliases,
        cost_estimate=pl.CostEstimate(
            flops=KERNEL_FLOPS * images, transcendentals=0, bytes_accessed=8 * images * parts * rows * D
        ),
        compiler_params=pltpu.CompilerParams(vmem_limit_bytes=52 * 1024 * 1024),
    )(*args)
    return result[:parts], result[parts], (result[parts + 1], result[parts + 2])


def finish_kernel(bit_ref, mine_ref, other_ref, up_ref, down_ref, qkv_ref, out_ref):
    low = bit_ref[0] == 0
    size = mine_ref.shape[0]
    mine, other = mine_ref[...], other_ref[...]
    down = []
    for k in range(2):
        part = jnp.where(low, mine, other) if k == 0 else jnp.where(low, other, mine)
        span = slice(k * size, (k + 1) * size)
        up_ref[span] = part[:, UP : UP + FF].astype(jnp.float32)
        qkv_ref[span] = part[:, QKV : QKV + 3 * D].astype(jnp.float32)
        out_ref[span] = part[:, OUT : OUT + D].astype(jnp.float32)
        down.append(part[:, DOWN : DOWN + FF])
    down_ref[...] = jnp.concatenate(down, 0).T.astype(jnp.float32)


def finish(bit, mine, other):
    full = pl.BlockSpec(memory_space=pltpu.VMEM)
    rows = 2 * mine.shape[0]
    shapes = [(rows, FF), (FF, rows), (rows, 3 * D), (rows, D)]
    return pl.pallas_call(
        finish_kernel,
        in_specs=[pl.BlockSpec(memory_space=pltpu.SMEM), full, full],
        out_specs=[full] * 4,
        out_shape=[jax.ShapeDtypeStruct(shape, jnp.float32) for shape in shapes],
        compiler_params=pltpu.CompilerParams(vmem_limit_bytes=52 * 1024 * 1024),
    )(bit.reshape(1), mine, other)


def cut(array, start, size, axis=0):
    return lax.dynamic_slice_in_dim(array, start, size, axis)


def group_stages(size):
    bits = [1 << k for k in range(size.bit_length() - 1)]
    if size == 8:
        table = [[1] * 8, [2 if i % 2 == 0 else 4 for i in range(8)], [4 if i % 2 == 0 else 2 for i in range(8)]]
    else:
        table = [[bit] * size for bit in bits]
    return table


def stage_bit(stage, index):
    masks = jnp.asarray(stage, jnp.int32)[index] if len(set(stage)) > 1 else stage[0]
    return jnp.where((index & masks) != 0, 1, 0)


def swap(array, stage):
    return lax.ppermute(array, "grp", [(i, i ^ bit) for i, bit in enumerate(stage)])


def seq_shift(array, shift, size):
    return lax.ppermute(array, "seq", [(i, (i + shift) % size) for i in range(size)])


def scatter_sum(array, index, place, stages, seq):
    for stage in stages:
        size = array.shape[0] // 2
        bit = stage_bit(stage, index)
        got = swap(cut(array, (1 - bit) * size, size), stage)
        array = (cut(array, bit * size, size).astype(jnp.float32) + got.astype(jnp.float32)).astype(jnp.bfloat16)
    size = array.shape[1] // seq
    total = cut(array, place * size, size, 1).astype(jnp.float32)
    for shift in seq_shifts(seq)[1:]:
        total = total + seq_shift(cut(array, ((place + shift) % seq) * size, size, 1), shift, seq).astype(jnp.float32)
    return total.astype(jnp.bfloat16)


def gather_seq(array, place, seq, axis):
    size = array.shape[axis]
    shape = list(array.shape)
    shape[axis] = size * seq
    whole = lax.dynamic_update_slice_in_dim(jnp.zeros(shape, array.dtype), array, place * size, axis)
    for shift in seq_shifts(seq)[1:]:
        got = seq_shift(array, shift, seq)
        whole = lax.dynamic_update_slice_in_dim(whole, got, ((place - shift) % seq) * size, axis)
    return whole


def join(array, index, stage):
    got = swap(array, stage)
    low = stage_bit(stage, index) == 0
    return jnp.where(low, jnp.concatenate([array, got], 0), jnp.concatenate([got, array], 0))


def gather_group(array, index, group):
    bit = 1
    while bit < group:
        array = join(array, index, [bit] * group)
        bit *= 2
    return array


def seq_shifts(seq):
    return (0, 2, 1, 3) if seq == 4 else tuple(range(seq))


def tied(values, after):
    return lax.optimization_barrier((values, after))[0]


def level_rows(levels):
    return (levels[:, None] == jnp.arange(LEVELS, dtype=levels.dtype)[None, :]).astype(jnp.float32)


def shards(
    group,
    seq,
    tokens,
    cotangent,
    condition,
    mask_flags,
    noise_levels,
    level_table,
    ada_weight,
    ada_bias,
    qkv_weight,
    query_value_bias,
    output_weight,
    output_bias,
    up_weight,
    up_bias,
    down_weight,
    down_bias,
):
    batches, images, rows = tokens.shape[:3]
    count = batches * images
    own = count // seq
    place = lax.axis_index("seq")
    index = lax.axis_index("grp")
    stages = group_stages(group)
    shifts = seq_shifts(seq)
    chunks, groups = (CHUNKS, GROUPS) if sum(CHUNKS) == own else ((own,), ((0,),))
    starts = [sum(chunks[:c]) for c in range(len(chunks))]
    whole = (tokens.reshape(count, rows, D), cotangent.reshape(count, rows, D))
    condition = condition.reshape(count, D)
    noise_levels = noise_levels.reshape(count)

    def fetch(chunk, after):
        source = whole if after is None else tied(whole, after)
        blocks = []
        for shift in shifts:
            start = ((place + shift) % seq) * own + starts[chunk]
            block = jnp.stack([cut(array, start, chunks[chunk]) for array in source])
            blocks.append(block if shift == 0 else seq_shift(block, shift, seq))
        return blocks

    blocks = fetch(0, None)

    flags = cut(mask_flags.reshape(count), place * own, own)
    sources = jnp.stack([(place - shift) % seq for shift in shifts])
    live = jnp.logical_or(flags[:, None] == 0, sources[None, :] * rows < KEEP).astype(jnp.float32)

    mine = cut(condition, place * own, own) + jnp.dot(
        level_rows(cut(noise_levels, place * own, own)), level_table, precision=highest
    )
    modulation = (
        jnp.dot(jax.nn.silu(mine).astype(jnp.bfloat16), ada_weight, preferred_element_type=jnp.float32) + ada_bias
    ).reshape(own, 6, D)

    bias_full = jnp.concatenate([query_value_bias[:D], jnp.zeros((D,), jnp.float32), query_value_bias[D:]])
    weights = (
        qkv_weight,
        output_weight,
        up_weight,
        down_weight,
        bias_full[None],
        output_bias[None],
        up_bias[None],
        down_bias[None],
    )
    table = jnp.concatenate(
        [condition, jnp.broadcast_to(noise_levels[:, None].astype(jnp.float32), (count, 128))], 1
    )
    table = gather_group(table, index, group).reshape(group * seq, own, D + 128)
    table = jnp.pad(table, ((0, 0), (0, PAD), (0, 0)), constant_values=-1.0).reshape(-1, D + 128)
    real = table[:, D : D + 1] >= 0.0
    onehot = level_rows(table[:, D].astype(jnp.int32))
    cond_full = jnp.where(real, table[:, :D] + jnp.dot(onehot, level_table, precision=highest), 0.0)
    activated = jax.nn.silu(cond_full).astype(jnp.bfloat16)
    slot = jnp.arange(own + PAD, dtype=jnp.int32)
    picks = jnp.stack([slot < own] + [slot == own + k for k in range(2)] + [slot < 0] * 5)
    picks = jnp.tile(picks.astype(jnp.bfloat16), (1, group * seq))
    live = tied(live, table)

    carried = None
    g_mods = []
    held = []
    for members in groups:
        buffers = None
        total = sum(chunks[c] for c in members)
        for chunk in members:
            following = fetch(chunk + 1, blocks) if chunk + 1 < len(chunks) else None
            span = slice(starts[chunk], starts[chunk] + chunks[chunk])
            buffers, g_mod, carried = layer_call(
                live[span],
                blocks,
                modulation[span],
                weights,
                carried,
                buffers,
                starts[chunk] - starts[members[0]],
                total,
                chunk + 1 == len(chunks),
            )
            g_mods.append(g_mod)
            arrived = blocks
            blocks = following
        held.append(buffers)

    out_rows = jnp.zeros((count, rows, D), jnp.bfloat16)
    grad_rows = jnp.zeros((count, rows, D), jnp.bfloat16)

    def give(targets, members, buffers, after):
        for shift, buffer in zip(shifts, buffers):
            if shift != 0:
                after = back = seq_shift(tied(buffer, after), -shift, seq)
            else:
                back = buffer
            start = ((place + shift) % seq) * own + starts[members[0]]
            targets = [lax.dynamic_update_slice_in_dim(t, back[k], start, 0) for k, t in enumerate(targets)]
        return targets, after

    summed, bias_sums = carried
    small = jnp.concatenate(
        [g.reshape(-1, 6 * D) for g in g_mods]
        + [bias_sums.reshape(2, 6 * D), jnp.zeros((PAD - 2, 6 * D), jnp.float32)]
    ).astype(jnp.bfloat16)
    small = gather_seq(small, place, seq, 0)
    small = gather_group(small, index, group)
    sums = dot_nn(picks, small)
    grad_ada_bias = sums[0]
    bias_all = sums[1:3].reshape(WIDE)
    grad_ada = dot_tn(activated, small)
    g_activated = dot_nt(small, ada_weight)
    g_cond = jax.vjp(jax.nn.silu, cond_full)[1](g_activated)[0]
    grad_level = lax.dot_general(
        onehot, g_cond, (((0,), (0,)), ((), ())), precision=highest, preferred_element_type=jnp.float32
    )
    grad_condition = cut(g_cond, index * seq * (own + PAD), seq * (own + PAD)).reshape(seq, own + PAD, D)[:, :own]

    part = scatter_sum(summed, index, place, stages, seq)
    targets, after = give([out_rows, grad_rows], groups[0], held[0], arrived)
    part = gather_seq(part, place, seq, 1)
    if len(groups) > 1:
        targets, after = give(targets, groups[1], held[1], after)
    for stage in reversed(stages[1:]):
        part = join(part, index, stage)
    grad_up, grad_down, grad_qkv, grad_out = finish(
        stage_bit(stages[0], index), part, swap(part, stages[0])
    )
    return (
        targets[0].reshape(batches, images, rows, D),
        targets[1].reshape(batches, images, rows, D),
        grad_condition.reshape(batches, images, D),
        grad_level,
        grad_ada,
        grad_ada_bias,
        grad_qkv,
        jnp.concatenate([bias_all[QKV : QKV + D], bias_all[QKV + 2 * D : QKV + 3 * D]]),
        grad_out,
        bias_all[OUT : OUT + D],
        grad_up,
        bias_all[UP : UP + FF],
        grad_down,
        bias_all[DOWN : DOWN + D],
    )


def solution(mesh):
    rows = P(None, "grp", "seq", None)
    in_specs = (rows, rows, P(None, "grp", None), P(None, "grp"), P(None, "grp")) + (P(),) * 11
    out_specs = (rows, rows, P(None, "grp", None)) + (P(),) * 11
    body = functools.partial(shards, mesh.shape["grp"], mesh.shape["seq"])
    return jax.shard_map(body, mesh=mesh, in_specs=in_specs, out_specs=out_specs, check_vma=False)
```

time: 364 us -> 255 us (0.70)
  other arithmetic: 37.9 us -> 7.91 us
  Pallas kernels: 101 us -> 73.3 us
  waiting for transfers between devices: 88.9 us -> 61.6 us
  starting transfers between devices: 78.5 us -> 56.8 us
  local copies, waits for them, and re-layouts: 41.5 us -> 34.7 us
  matrix products: 7.67 us -> 12.4 us
    pallas_call x4, Pallas kernels: 101 us -> 73.3 us  [the longest x3 68.5 us: layer_call(): pl.pallas_call(functools.partial(layer_kernel, parts, first, last, buffer...]
    ppermute x33 -> x24, starting transfers between devices: 71.9 us -> 45.2 us  [seq_shift(): lax.ppermute(array, 'seq', [(i, (i + shift) % size) for i in range(size)])]
    ppermute x12, waiting for transfers between devices: 33.9 us -> 15.6 us  [swap(): lax.ppermute(array, 'grp', [(i, i ^ bit) for i, bit in enumerate(stage)])]
    unnamed x103 -> x61, local copies, waits for them, and re-layouts: 19.1 us -> 2.04 us
    another operation x21 -> x13, other arithmetic: 16.4 us -> 0.46 us  [the longest x12 0.4 us: fetch(): block = jnp.stack([cut(array, start, chunks[chunk]) for array in source])]
    ppermute x33 -> x24, waiting for transfers between devices: 55 us -> 45.9 us  [seq_shift(): lax.ppermute(array, 'seq', [(i, (i + shift) % size) for i in range(size)])]
    select_n x9 -> x7, other arithmetic: 11.5 us -> 2.77 us  [join(): jnp.where(low, jnp.concatenate([array, got], 0), jnp.concatenate([got, ar...]
    dynamic_update_slice x17 -> x10, local copies, waits for them, and re-layouts: 0.54 us -> 8.78 us  [the longest x9 7.85 us: give(): lax.dynamic_update_slice_in_dim(t, back[k], start, 0)]
  transfers between devices with their start and end apart: 45 -> 36, of which waited for: 17 -> 13; matrix products, arithmetic and copies ran while one was open for 18% -> 19% of each run, Pallas kernels for 28% -> 17%
where the time goes in v2:
time: 255 us; the launch traced here: 250 us
  Pallas kernels  73.3 us (29%)
  waiting for transfers between devices  61.6 us (24%)
  starting transfers between devices  56.8 us (22%)
  local copies, waits for them, and re-layouts  34.7 us (14%)
  matrix products  12.4 us (5%)
  other arithmetic  7.91 us (3%)
  between operations  3.06 us (1%)
    pallas_call x3, Pallas kernels, layer_call(): pl.pallas_call(functools.partial(layer_kernel, parts, first, last, buffer...  68.5 us
    ppermute x24, waiting for transfers between devices, seq_shift(): lax.ppermute(array, 'seq', [(i, (i + shift) % size) for i in range(size)])  45.9 us
    ppermute x24, starting transfers between devices, seq_shift(): lax.ppermute(array, 'seq', [(i, (i + shift) % size) for i in range(size)])  45.2 us
    ppermute x12, waiting for transfers between devices, swap(): lax.ppermute(array, 'grp', [(i, i ^ bit) for i, bit in enumerate(stage)])  15.6 us
    ppermute x12, starting transfers between devices, swap(): lax.ppermute(array, 'grp', [(i, i ^ bit) for i, bit in enumerate(stage)])  11.6 us
    dynamic_update_slice x9, local copies, waits for them, and re-layouts, give(): lax.dynamic_update_slice_in_dim(t, back[k], start, 0)  7.85 us
    dot_general x1, matrix products, dot_tn(): lax.dot_general(a, b, (((0,), (0,)), ((), ())), preferred_element_type=jn...  5.71 us
  transfers between devices with their start and end apart: 36, of which 13 were waited for; matrix products, arithmetic and copies ran while one was open for 19% of the time, Pallas kernels for 17%

profile of v2, /device:TPU:0, one launch (start us, length us, event | category | flops | bytes accessed | tf_op | source)
XLA Modules:
  0.0 249.6 jit_solution(8474097320628385693)
XLA Ops:
  0.8 1.5 dynamic-slice_bitcast_fusion.16
  2.3 4.1 %collective-permute-start.3 = (bf16[2,2,64,384]{3,2,1,0:T(8,128)(2,1)S(1)}, bf16[2,2,64,384]{3,2,1,0:T(8,128)(2,1)S(1)}, u32[]{:S(2)}, u32[]{:S(2)}) collective-permute-start(bf16[2,2,64,384]{3,2,1,0:T(8,128)(2,1)S(1)} %pad_maximum_fusion.9), channel_id=1, source_target_pairs={{0,2},{1,3},{2,0},{3,1},{4,6},{5,7},{6,4},{7,5},{8,10},{9,11},{10,... | collective-permute-start | bytes 589832 | tf_op jit(solution)/shard_map/ppermute | solution.py:341
  6.5 1.6 collective-permute-start.4
  8.2 2.3 collective-permute-start.5
  13.1 1.6 collective-permute-start.1
  20.0 1.6 collective-permute-start.2
  22.9 1.9 collective-permute-start.8
  26.2 4.0 %collective-permute-start.6 = (bf16[2,3,64,384]{3,2,1,0:T(8,128)(2,1)S(1)}, bf16[2,3,64,384]{3,2,1,0:T(8,128)(2,1)S(1)}, u32[]{:S(2)}, u32[]{:S(2)}) collective-permute-start(bf16[2,3,64,384]{3,2,1,0:T(8,128)(2,1)S(1)} %pad_maximum_fusion.1), channel_id=1, source_target_pairs={{0,2},{1,3},{2,0},{3,1},{4,6},{5,7},{6,4},{7,5},{8,10},{9,11},{10,... | collective-permute-start | bytes 884744 | tf_op jit(solution)/shard_map/ppermute | solution.py:341
  31.4 17.3 %shard_map.299 = (bf16[2,5,64,384]{3,2,1,0:T(8,128)(2,1)S(1)}, bf16[2,5,64,384]{3,2,1,0:T(8,128)(2,1)}, bf16[2,5,64,384]{3,2,1,0:T(8,128)(2,1)}, bf16[2,5,64,384...) custom-call(f32[2,4]{1,0:T(2,128)S(1)} %slice.117.refs_0_, ...), custom_call_target="tpu_custom_call" | custom-call | flops 60000002048 | bytes 1572864 | tf_op jit(solution)/shard_map/pallas_call | solution.py:269
  49.4 4.7 %collective-permute-done.6.refs_2_ = bf16[2,3,64,384]{3,2,1,0:T(8,128)(2,1)S(1)} collective-permute-done((bf16[2,3,64,384]{3,2,1,0:T(8,128)(2,1)S(1)}, bf16[2,3,64,384]{3,2,1,0:T(8,128)(2,1)S(1)}, u32[]{:S(2)}, u32[]{:S(2)}) %collective-permute-start.6) | collective-permute-done | bytes 294944 | tf_op jit(solution)/shard_map/ppermute | solution.py:341
  55.6 2.2 collective-permute-start.10
  57.9 25.0 %shard_map.300 = (bf16[2,5,64,384]{3,2,1,0:T(8,128)(2,1)}, bf16[2,5,64,384]{3,2,1,0:T(8,128)(2,1)}, bf16[2,5,64,384]{3,2,1,0:T(8,128)(2,1)}, bf16[2,5,64,384]{3,...) custom-call(f32[3,4]{1,0:T(4,128)S(1)} %get-tuple-element.136.refs_0, ...), custom_call_target="tpu_custom_call", output_to_operand_aliasing={{5}: (14, {}), {0}: (16, {}), {1}: (17, {}), {2}: (18, {}),... | custom-call | flops 89999998976 | bytes 2359296 | tf_op jit(solution)/shard_map/pallas_call | solution.py:269
  83.8 26.3 %shard_map.301 = (bf16[2,3,64,384]{3,2,1,0:T(8,128)(2,1)S(1)}, bf16[2,3,64,384]{3,2,1,0:T(8,128)(2,1)S(1)}, bf16[2,3,64,384]{3,2,1,0:T(8,128)(2,1)S(1)}, bf16[2,...) custom-call(f32[3,4]{1,0:T(4,128)S(1)} %get-tuple-element.135.refs_0_, ...), custom_call_target="tpu_custom_call" | custom-call | flops 89999998976 | bytes 2359296 | tf_op jit(solution)/shard_map/pallas_call | solution.py:269
  110.1 2.9 %constant_dynamic-slice_fusion.5 = bf16[192,4608]{1,0:T(8,128)(2,1)} fusion(bf16[384,4608]{1,0:T(8,128)(2,1)} %get-tuple-element.81, s32[]{:T(128)S(6)} %select_n.360), kind=kLoop, calls=%fused_computation.107 | loop fusion | bytes 3538948 | tf_op jit(solution)/shard_map/dynamic_slice | solution.py:319
  113.9 1.4 broadcast.104.clone.1
  116.0 1.4 broadcast.104.clone
  119.6 2.9 %collective-permute-start.18 = (bf16[16,2304]{1,0:T(8,128)(2,1)}, bf16[16,2304]{1,0:T(8,128)(2,1)S(1)}, u32[]{:S(2)}, u32[]{:S(2)}) collective-permute-start(bf16[16,2304]{1,0:T(8,128)(2,1)} %concatenate.77), channel_id=1, source_target_pairs={{0,2},{1,3},{2,0},{3,1},{4,6},{5,7},{6,4},{7,5},{8,10},{9,11},{10,... | collective-permute-start | bytes 221192 | tf_op jit(solution)/shard_map/ppermute | solution.py:341
  122.5 3.8 %collective-permute-start.20 = (bf16[16,2304]{1,0:T(8,128)(2,1)}, bf16[16,2304]{1,0:T(8,128)(2,1)S(1)}, u32[]{:S(2)}, u32[]{:S(2)}) collective-permute-start(bf16[16,2304]{1,0:T(8,128)(2,1)} %concatenate.77), channel_id=1, source_target_pairs={{0,3},{1,0},{2,1},{3,2},{4,7},{5,4},{6,5},{7,6},{8,11},{9,8},{10,9... | collective-permute-start | bytes 221192 | tf_op jit(solution)/shard_map/ppermute | solution.py:341
  127.3 2.4 add_convert_fusion
  129.8 1.5 collective-permute-start.25
  131.5 11.4 %collective-permute-done.25 = bf16[96,4608]{1,0:T(8,128)(2,1)S(1)} collective-permute-done((bf16[96,4608]{1,0:T(8,128)(2,1)S(1)}, bf16[96,4608]{1,0:T(8,128)(2,1)S(1)}, u32[]{:S(2)}, u32[]{:S(2)}) %collective-permute-start.25) | collective-permute-done | bytes 884768 | tf_op jit(solution)/shard_map/ppermute | solution.py:337
  143.2 1.6 collective-permute-start.26
  144.9 1.5 collective-permute-start.22
  146.4 5.1 %collective-permute-done.12 = bf16[2,5,64,384]{3,2,1,0:T(8,128)(2,1)S(1)} collective-permute-done((bf16[2,5,64,384]{3,2,1,0:T(8,128)(2,1)}, bf16[2,5,64,384]{3,2,1,0:T(8,128)(2,1)S(1)}, u32[]{:S(2)}, u32[]{:S(2)}) %collective-permute-start.12) | collective-permute-done | bytes 491552 | tf_op jit(solution)/shard_map/ppermute | solution.py:341
  151.5 2.1 collective-permute-start.13
  155.2 3.3 %collective-permute-start.29 = (bf16[48,1152]{1,0:T(8,128)(2,1)S(1)}, bf16[48,1152]{1,0:T(8,128)(2,1)S(1)}, u32[]{:S(2)}, u32[]{:S(2)}) collective-permute-start(bf16[48,1152]{1,0:T(8,128)(2,1)S(1)} %get-tuple-element.119), channel_id=1, source_target_pairs={{0,3},{1,0},{2,1},{3,2},{4,7},{5,4},{6,5},{7,6},{8,11},{9,8},{10,9... | collective-permute-start | bytes 331784 | tf_op jit(solution)/shard_map/ppermute | solution.py:341
  158.5 2.6 %collective-permute-done.22 = bf16[128,2304]{1,0:T(8,128)(2,1)S(1)} collective-permute-done((bf16[128,2304]{1,0:T(8,128)(2,1)S(1)}, bf16[128,2304]{1,0:T(8,128)(2,1)S(1)}, u32[]{:S(2)}, u32[]{:S(2)}) %collective-permute-start.22) | collective-permute-done | bytes 589856 | tf_op jit(solution)/shard_map/ppermute | solution.py:337
  162.0 5.8 %collective-permute-done.13 = bf16[2,5,64,384]{3,2,1,0:T(8,128)(2,1)S(1)} collective-permute-done((bf16[2,5,64,384]{3,2,1,0:T(8,128)(2,1)S(1)}, bf16[2,5,64,384]{3,2,1,0:T(8,128)(2,1)S(1)}, u32[]{:S(2)}, u32[]{:S(2)}) %collective-permute-start.13) | collective-permute-done | bytes 491552 | tf_op jit(solution)/shard_map/ppermute | solution.py:341
  167.8 4.2 %collective-permute-done.27 = bf16[48,1152]{1,0:T(8,128)(2,1)S(1)} collective-permute-done((bf16[48,1152]{1,0:T(8,128)(2,1)S(1)}, bf16[48,1152]{1,0:T(8,128)(2,1)S(1)}, u32[]{:S(2)}, u32[]{:S(2)}) %collective-permute-start.27) | collective-permute-done | bytes 110624 | tf_op jit(solution)/shard_map/ppermute | solution.py:341
  172.0 9.0 %collective-permute-done.29 = bf16[48,1152]{1,0:T(8,128)(2,1)S(1)} collective-permute-done((bf16[48,1152]{1,0:T(8,128)(2,1)S(1)}, bf16[48,1152]{1,0:T(8,128)(2,1)S(1)}, u32[]{:S(2)}, u32[]{:S(2)}) %collective-permute-start.29) | collective-permute-done | bytes 110624 | tf_op jit(solution)/shard_map/ppermute | solution.py:341
  181.1 3.7 %collective-permute-start.30 = (bf16[48,1152]{1,0:T(8,128)(2,1)S(1)}, bf16[48,1152]{1,0:T(8,128)(2,1)S(1)}, u32[]{:S(2)}, u32[]{:S(2)}) collective-permute-start(bf16[48,1152]{1,0:T(8,128)(2,1)S(1)} %get-tuple-element.87), channel_id=1, source_target_pairs={{0,2},{1,3},{2,0},{3,1},{4,6},{5,7},{6,4},{7,5},{8,10},{9,11},{10,... | collective-permute-start | bytes 331784 | tf_op jit(solution)/shard_map/ppermute | solution.py:341
  185.6 3.0 %collective-permute-start.15 = (bf16[2,3,64,384]{3,2,1,0:T(8,128)(2,1)S(1)}, bf16[2,3,64,384]{3,2,1,0:T(8,128)(2,1)S(1)}, u32[]{:S(2)}, u32[]{:S(2)}) collective-permute-start(bf16[2,3,64,384]{3,2,1,0:T(8,128)(2,1)S(1)} %get-tuple-element.72), channel_id=1, source_target_pairs={{0,2},{1,3},{2,0},{3,1},{4,6},{5,7},{6,4},{7,5},{8,10},{9,11},{10,... | collective-permute-start | bytes 884744 | tf_op jit(solution)/shard_map/ppermute | solution.py:341
  189.6 2.8 %collective-permute-start.32 = (bf16[48,1152]{1,0:T(8,128)(2,1)S(1)}, bf16[48,1152]{1,0:T(8,128)(2,1)S(1)}, u32[]{:S(2)}, u32[]{:S(2)}) collective-permute-start(bf16[48,1152]{1,0:T(8,128)(2,1)S(1)} %get-tuple-element.87), channel_id=1, source_target_pairs={{0,3},{1,0},{2,1},{3,2},{4,7},{5,4},{6,5},{7,6},{8,11},{9,8},{10,9... | collective-permute-start | bytes 331784 | tf_op jit(solution)/shard_map/ppermute | solution.py:341
  192.4 8.2 %collective-permute-done.31 = bf16[48,1152]{1,0:T(8,128)(2,1)S(1)} collective-permute-done((bf16[48,1152]{1,0:T(8,128)(2,1)S(1)}, bf16[48,1152]{1,0:T(8,128)(2,1)S(1)}, u32[]{:S(2)}, u32[]{:S(2)}) %collective-permute-start.31) | collective-permute-done | bytes 110624 | tf_op jit(solution)/shard_map/ppermute | solution.py:341
  200.7 1.6 collective-permute-start.33
  203.8 2.0 collective-permute-done.15
  205.8 2.5 %collective-permute-start.16 = (bf16[2,3,64,384]{3,2,1,0:T(8,128)(2,1)S(1)}, bf16[2,3,64,384]{3,2,1,0:T(8,128)(2,1)S(1)}, u32[]{:S(2)}, u32[]{:S(2)}) collective-permute-start(bf16[2,3,64,384]{3,2,1,0:T(8,128)(2,1)S(1)} %get-tuple-element.74), channel_id=1, source_target_pairs={{0,3},{1,0},{2,1},{3,2},{4,7},{5,4},{6,5},{7,6},{8,11},{9,8},{10,9... | collective-permute-start | bytes 884744 | tf_op jit(solution)/shard_map/ppermute | solution.py:341
  209.2 1.6 collective-permute-start.34
  211.5 6.9 %collective-permute-done.16 = bf16[2,3,64,384]{3,2,1,0:T(8,128)(2,1)S(1)} collective-permute-done((bf16[2,3,64,384]{3,2,1,0:T(8,128)(2,1)S(1)}, bf16[2,3,64,384]{3,2,1,0:T(8,128)(2,1)S(1)}, u32[]{:S(2)}, u32[]{:S(2)}) %collective-permute-start.16) | collective-permute-done | bytes 294944 | tf_op jit(solution)/shard_map/ppermute | solution.py:341
  218.4 1.7 collective-permute-start.17
  220.8 2.4 fusion.2
  228.3 1.5 slice_reduce_fusion
  229.8 1.4 fusion.27
  231.2 5.7 %fusion.4 = f32[384,2304]{1,0:T(8,128)} fusion(f32[512,384]{1,0:T(8,128)} %copy-done.7, bf16[256,2304]{1,0:T(8,128)(2,1)} %copy-done.21, bf16[256,2304]{1,0:T(8,128)(2,1)} %copy-done.6, pred[]{:T(512)S(6)} %eq.109), kind=kOutput, calls=%fused_computation.19 | convolution fusion | flops 917569536 | bytes 6684673 | tf_op jit(solution)/shard_map/dot_general | solution.py:38
  239.4 1.4 reshape.209
  240.9 2.3 fusion.6
  243.1 1.7 fusion.13
  244.9 4.8 %shard_map.302 = (f32[384,1536]{1,0:T(8,128)}, f32[1536,384]{1,0:T(8,128)}, f32[384,1152]{1,0:T(8,128)}, f32[384,384]{1,0:T(8,128)}) custom-call(s32[1]{0:T(128)} %bitcast.51.bit_ref, bf16[192,4608]{1,0:T(8,128)(2,1)S(1)} %maximum_select_fusion.1.mine_ref, bf16[192,4608]{1,0:T(8,128)(2,1)} %collective-permute-done.35.other_ref), custom_call_target="tpu_custom_call" | custom-call | tf_op jit(solution)/shard_map/pallas_call | solution.py:309
  (200 shorter events, 34.5 us)
Async XLA Ops:
  0.6 10.8 %copy-start = (bf16[384,2304]{1,0:T(8,128)(2,1)S(1)}, bf16[384,2304]{1,0:T(8,128)(2,1)}, u32[]{:S(2)}) copy-start(bf16[384,2304]{1,0:T(8,128)(2,1)} %param.26) | copy-start | bytes 5308420
  0.7 10.2 %copy-start.20 = (s32[16,2]{0,1:T(2,128)S(1)}, s32[16,2]{0,1:T(2,128)}, u32[]{:S(2)}) copy-start(s32[16,2]{0,1:T(2,128)} %param.23) | copy-start | bytes 388
  0.7 10.5 %copy-start.16 = (f32[768]{0:T(1024)S(1)}, f32[768]{0:T(1024)}, u32[]{:S(2)}) copy-start(f32[768]{0:T(1024)} %param.29) | copy-start | bytes 9220
  0.7 10.5 %copy-start.8 = (f32[64,384]{1,0:T(8,128)S(1)}, f32[64,384]{1,0:T(8,128)}, u32[]{:S(2)}) copy-start(f32[64,384]{1,0:T(8,128)} %param.25) | copy-start | bytes 294916
  0.7 10.7 %copy-start.12 = (f32[2304]{0:T(1024)S(1)}, f32[2304]{0:T(1024)}, u32[]{:S(2)}) copy-start(f32[2304]{0:T(1024)} %param.27) | copy-start | bytes 27652
  2.3 19.3 %collective-permute-start.3 = (bf16[2,2,64,384]{3,2,1,0:T(8,128)(2,1)S(1)}, bf16[2,2,64,384]{3,2,1,0:T(8,128)(2,1)S(1)}, u32[]{:S(2)}, u32[]{:S(2)}) collective-permute-start(bf16[2,2,64,384]{3,2,1,0:T(8,128)(2,1)S(1)} %pad_maximum_fusion.9), channel_id=1, source_target_pairs={{0,2},{1,3},{2,0},{3,1},{4,6},{5,7},{6,4},{7,5},{8,10},{9,11},{10,... | collective-permute-start | bytes 589832 | tf_op jit(solution)/shard_map/ppermute | solution.py:341
  6.5 10.9 %copy-start.15 = (f32[1536]{0:T(1024)S(1)}, f32[1536]{0:T(1024)}, u32[]{:S(2)}) copy-start(f32[1536]{0:T(1024)} %param.33) | copy-start | bytes 18436
  6.5 10.9 %copy-start.17 = (f32[384]{0:T(512)S(1)}, f32[384]{0:T(512)}, u32[]{:S(2)}) copy-start(f32[384]{0:T(512)} %param.31) | copy-start | bytes 4612
  6.5 10.9 %copy-start.18 = (f32[384]{0:T(512)S(1)}, f32[384]{0:T(512)}, u32[]{:S(2)}) copy-start(f32[384]{0:T(512)} %param.35) | copy-start | bytes 4612
  6.5 15.1 %collective-permute-start.4 = (bf16[2,2,64,384]{3,2,1,0:T(8,128)(2,1)S(1)}, bf16[2,2,64,384]{3,2,1,0:T(8,128)(2,1)S(1)}, u32[]{:S(2)}, u32[]{:S(2)}) collective-permute-start(bf16[2,2,64,384]{3,2,1,0:T(8,128)(2,1)S(1)} %pad_maximum_fusion.10), channel_id=1, source_target_pairs={{0,1},{1,2},{2,3},{3,0},{4,5},{5,6},{6,7},{7,4},{8,9},{9,10},{10,1... | collective-permute-start | bytes 589832 | tf_op jit(solution)/shard_map/ppermute | solution.py:341
  8.2 13.5 %collective-permute-start.5 = (bf16[2,2,64,384]{3,2,1,0:T(8,128)(2,1)S(1)}, bf16[2,2,64,384]{3,2,1,0:T(8,128)(2,1)S(1)}, u32[]{:S(2)}, u32[]{:S(2)}) collective-permute-start(bf16[2,2,64,384]{3,2,1,0:T(8,128)(2,1)S(1)} %pad_maximum_fusion.11), channel_id=1, source_target_pairs={{0,3},{1,0},{2,1},{3,2},{4,7},{5,4},{6,5},{7,6},{8,11},{9,8},{10,9... | collective-permute-start | bytes 589832 | tf_op jit(solution)/shard_map/ppermute | solution.py:341
  10.8 1.4 collective-permute-start
  13.1 5.9 %collective-permute-start.1 = (f32[64,512]{1,0:T(8,128)S(1)}, f32[64,512]{1,0:T(8,128)}, u32[]{:S(2)}, u32[]{:S(2)}) collective-permute-start(f32[64,512]{1,0:T(8,128)S(1)} %maximum_select_fusion.7), channel_id=1, source_target_pairs={{0,8},{4,12},{8,0},{12,4},{16,24},{20,28},{24,16},{28,20},{1,9},{5... | collective-permute-start | bytes 393224 | tf_op jit(solution)/shard_map/ppermute | solution.py:337
  20.0 10.2 %collective-permute-start.2 = (f32[128,512]{1,0:T(8,128)S(1)}, f32[128,512]{1,0:T(8,128)S(1)}, u32[]{:S(2)}, u32[]{:S(2)}) collective-permute-start(f32[128,512]{1,0:T(8,128)S(1)} %maximum_select_fusion.6), channel_id=1, source_target_pairs={{0,16},{4,20},{8,24},{12,28},{16,0},{20,4},{24,8},{28,12},{1,17},{... | collective-permute-start | bytes 786440 | tf_op jit(solution)/shard_map/ppermute | solution.py:337
  22.9 26.4 %collective-permute-start.8 = (bf16[2,3,64,384]{3,2,1,0:T(8,128)(2,1)S(1)}, bf16[2,3,64,384]{3,2,1,0:T(8,128)(2,1)S(1)}, u32[]{:S(2)}, u32[]{:S(2)}) collective-permute-start(bf16[2,3,64,384]{3,2,1,0:T(8,128)(2,1)S(1)} %pad_maximum_fusion.3), channel_id=1, source_target_pairs={{0,3},{1,0},{2,1},{3,2},{4,7},{5,4},{6,5},{7,6},{8,11},{9,8},{10,9... | collective-permute-start | bytes 884744 | tf_op jit(solution)/shard_map/ppermute | solution.py:341
  24.8 24.5 %collective-permute-start.7 = (bf16[2,3,64,384]{3,2,1,0:T(8,128)(2,1)S(1)}, bf16[2,3,64,384]{3,2,1,0:T(8,128)(2,1)S(1)}, u32[]{:S(2)}, u32[]{:S(2)}) collective-permute-start(bf16[2,3,64,384]{3,2,1,0:T(8,128)(2,1)S(1)} %pad_maximum_fusion.2), channel_id=1, source_target_pairs={{0,1},{1,2},{2,3},{3,0},{4,5},{5,6},{6,7},{7,4},{8,9},{9,10},{10,1... | collective-permute-start | bytes 884744 | tf_op jit(solution)/shard_map/ppermute | solution.py:341
  26.2 27.9 %collective-permute-start.6 = (bf16[2,3,64,384]{3,2,1,0:T(8,128)(2,1)S(1)}, bf16[2,3,64,384]{3,2,1,0:T(8,128)(2,1)S(1)}, u32[]{:S(2)}, u32[]{:S(2)}) collective-permute-start(bf16[2,3,64,384]{3,2,1,0:T(8,128)(2,1)S(1)} %pad_maximum_fusion.1), channel_id=1, source_target_pairs={{0,2},{1,3},{2,0},{3,1},{4,6},{5,7},{6,4},{7,5},{8,10},{9,11},{10,... | collective-permute-start | bytes 884744 | tf_op jit(solution)/shard_map/ppermute | solution.py:341
  55.4 27.5 %collective-permute-start.11 = (bf16[2,3,64,384]{3,2,1,0:T(8,128)(2,1)S(1)}, bf16[2,3,64,384]{3,2,1,0:T(8,128)(2,1)S(1)}, u32[]{:S(2)}, u32[]{:S(2)}) collective-permute-start(bf16[2,3,64,384]{3,2,1,0:T(8,128)(2,1)S(1)} %pad_maximum_fusion.7), channel_id=1, source_target_pairs={{0,3},{1,0},{2,1},{3,2},{4,7},{5,4},{6,5},{7,6},{8,11},{9,8},{10,9... | collective-permute-start | bytes 884744 | tf_op jit(solution)/shard_map/ppermute | solution.py:341
  55.6 27.4 %collective-permute-start.10 = (bf16[2,3,64,384]{3,2,1,0:T(8,128)(2,1)S(1)}, bf16[2,3,64,384]{3,2,1,0:T(8,128)(2,1)S(1)}, u32[]{:S(2)}, u32[]{:S(2)}) collective-permute-start(bf16[2,3,64,384]{3,2,1,0:T(8,128)(2,1)S(1)} %pad_maximum_fusion.6), channel_id=1, source_target_pairs={{0,1},{1,2},{2,3},{3,0},{4,5},{5,6},{6,7},{7,4},{8,9},{9,10},{10,1... | collective-permute-start | bytes 884744 | tf_op jit(solution)/shard_map/ppermute | solution.py:341
  57.8 25.1 %collective-permute-start.9 = (bf16[2,3,64,384]{3,2,1,0:T(8,128)(2,1)S(1)}, bf16[2,3,64,384]{3,2,1,0:T(8,128)(2,1)S(1)}, u32[]{:S(2)}, u32[]{:S(2)}) collective-permute-start(bf16[2,3,64,384]{3,2,1,0:T(8,128)(2,1)S(1)} %pad_maximum_fusion.5), channel_id=1, source_target_pairs={{0,2},{1,3},{2,0},{3,1},{4,6},{5,7},{6,4},{7,5},{8,10},{9,11},{10,... | collective-permute-start | bytes 884744 | tf_op jit(solution)/shard_map/ppermute | solution.py:341
  113.0 14.3 %collective-permute-start.24 = (bf16[192,4608]{1,0:T(8,128)(2,1)}, bf16[192,4608]{1,0:T(8,128)(2,1)}, u32[]{:S(2)}, u32[]{:S(2)}) collective-permute-start(bf16[192,4608]{1,0:T(8,128)(2,1)} %constant_dynamic-slice_fusion.5), channel_id=1, source_target_pairs={{0,4},{4,0},{8,12},{12,8},{16,20},{20,16},{24,28},{28,24},{1,5},{5... | collective-permute-start | bytes 5308424 | tf_op jit(solution)/shard_map/ppermute | solution.py:337
  113.9 107.0 %copy-start.7 = (f32[512,384]{1,0:T(8,128)}, f32[512,384]{1,0:T(8,128)S(1)}, u32[]{:S(2)}) copy-start(f32[512,384]{1,0:T(8,128)S(1)} %fusion) | copy-start | bytes 2359300
  119.6 11.8 %collective-permute-start.18 = (bf16[16,2304]{1,0:T(8,128)(2,1)}, bf16[16,2304]{1,0:T(8,128)(2,1)S(1)}, u32[]{:S(2)}, u32[]{:S(2)}) collective-permute-start(bf16[16,2304]{1,0:T(8,128)(2,1)} %concatenate.77), channel_id=1, source_target_pairs={{0,2},{1,3},{2,0},{3,1},{4,6},{5,7},{6,4},{7,5},{8,10},{9,11},{10,... | collective-permute-start | bytes 221192 | tf_op jit(solution)/shard_map/ppermute | solution.py:341
  122.5 8.8 %collective-permute-start.19 = (bf16[16,2304]{1,0:T(8,128)(2,1)}, bf16[16,2304]{1,0:T(8,128)(2,1)S(1)}, u32[]{:S(2)}, u32[]{:S(2)}) collective-permute-start(bf16[16,2304]{1,0:T(8,128)(2,1)} %concatenate.77), channel_id=1, source_target_pairs={{0,1},{1,2},{2,3},{3,0},{4,5},{5,6},{6,7},{7,4},{8,9},{9,10},{10,1... | collective-permute-start | bytes 221192 | tf_op jit(solution)/shard_map/ppermute | solution.py:341
  122.5 8.8 %collective-permute-start.20 = (bf16[16,2304]{1,0:T(8,128)(2,1)}, bf16[16,2304]{1,0:T(8,128)(2,1)S(1)}, u32[]{:S(2)}, u32[]{:S(2)}) collective-permute-start(bf16[16,2304]{1,0:T(8,128)(2,1)} %concatenate.77), channel_id=1, source_target_pairs={{0,3},{1,0},{2,1},{3,2},{4,7},{5,4},{6,5},{7,6},{8,11},{9,8},{10,9... | collective-permute-start | bytes 221192 | tf_op jit(solution)/shard_map/ppermute | solution.py:341
  126.3 25.1 %collective-permute-start.12 = (bf16[2,5,64,384]{3,2,1,0:T(8,128)(2,1)}, bf16[2,5,64,384]{3,2,1,0:T(8,128)(2,1)S(1)}, u32[]{:S(2)}, u32[]{:S(2)}) collective-permute-start(bf16[2,5,64,384]{3,2,1,0:T(8,128)(2,1)} %get-tuple-element.63), channel_id=1, source_target_pairs={{0,2},{1,3},{2,0},{3,1},{4,6},{5,7},{6,4},{7,5},{8,10},{9,11},{10,... | collective-permute-start | bytes 1474568 | tf_op jit(solution)/shard_map/ppermute | solution.py:341
  129.8 13.1 %collective-permute-start.25 = (bf16[96,4608]{1,0:T(8,128)(2,1)S(1)}, bf16[96,4608]{1,0:T(8,128)(2,1)S(1)}, u32[]{:S(2)}, u32[]{:S(2)}) collective-permute-start(bf16[96,4608]{1,0:T(8,128)(2,1)S(1)} %constant_dynamic-slice_fusion.4), channel_id=1, source_target_pairs={{0,8},{4,20},{8,0},{12,28},{16,24},{20,4},{24,16},{28,12},{1,9},{5... | collective-permute-start | bytes 2654216 | tf_op jit(solution)/shard_map/ppermute | solution.py:337
  131.4 20.1 %copy-start.22 = (bf16[2,5,64,384]{3,2,1,0:T(8,128)(2,1)S(1)}, bf16[2,5,64,384]{3,2,1,0:T(8,128)(2,1)}, u32[]{:S(2)}) copy-start(bf16[2,5,64,384]{3,2,1,0:T(8,128)(2,1)} %get-tuple-element.65) | copy-start | bytes 1474564
  131.4 13.4 %collective-permute-start.21 = (bf16[64,2304]{1,0:T(8,128)(2,1)S(1)}, bf16[64,2304]{1,0:T(8,128)(2,1)S(1)}, u32[]{:S(2)}, u32[]{:S(2)}) collective-permute-start(bf16[64,2304]{1,0:T(8,128)(2,1)S(1)} %constant_dynamic-update-slice_fusion.4), channel_id=1, source_target_pairs={{0,4},{4,0},{8,12},{12,8},{16,20},{20,16},{24,28},{28,24},{1,5},{5... | collective-permute-start | bytes 884744 | tf_op jit(solution)/shard_map/ppermute | solution.py:337
  143.2 11.2 %collective-permute-start.26 = (bf16[48,4608]{1,0:T(8,128)(2,1)S(1)}, bf16[48,4608]{1,0:T(8,128)(2,1)S(1)}, u32[]{:S(2)}, u32[]{:S(2)}) collective-permute-start(bf16[48,4608]{1,0:T(8,128)(2,1)S(1)} %constant_dynamic-slice_fusion.3), channel_id=1, source_target_pairs={{0,16},{4,12},{8,24},{12,4},{16,0},{20,28},{24,8},{28,20},{1,17},{... | collective-permute-start | bytes 1327112 | tf_op jit(solution)/shard_map/ppermute | solution.py:337
  144.9 16.3 %collective-permute-start.22 = (bf16[128,2304]{1,0:T(8,128)(2,1)S(1)}, bf16[128,2304]{1,0:T(8,128)(2,1)S(1)}, u32[]{:S(2)}, u32[]{:S(2)}) collective-permute-start(bf16[128,2304]{1,0:T(8,128)(2,1)S(1)} %maximum_select_fusion.4), channel_id=1, source_target_pairs={{0,8},{4,12},{8,0},{12,4},{16,24},{20,28},{24,16},{28,20},{1,9},{5... | collective-permute-start | bytes 1769480 | tf_op jit(solution)/shard_map/ppermute | solution.py:337
  151.5 16.3 %collective-permute-start.13 = (bf16[2,5,64,384]{3,2,1,0:T(8,128)(2,1)S(1)}, bf16[2,5,64,384]{3,2,1,0:T(8,128)(2,1)S(1)}, u32[]{:S(2)}, u32[]{:S(2)}) collective-permute-start(bf16[2,5,64,384]{3,2,1,0:T(8,128)(2,1)S(1)} %copy-done.22), channel_id=1, source_target_pairs={{0,3},{1,0},{2,1},{3,2},{4,7},{5,4},{6,5},{7,6},{8,11},{9,8},{10,9... | collective-permute-start | bytes 1474568 | tf_op jit(solution)/shard_map/ppermute | solution.py:341
  154.5 13.3 %copy-start.23 = (bf16[2,5,64,384]{3,2,1,0:T(8,128)(2,1)S(1)}, bf16[2,5,64,384]{3,2,1,0:T(8,128)(2,1)}, u32[]{:S(2)}) copy-start(bf16[2,5,64,384]{3,2,1,0:T(8,128)(2,1)} %get-tuple-element.67) | copy-start | bytes 1474564
  154.6 17.4 %collective-permute-start.27 = (bf16[48,1152]{1,0:T(8,128)(2,1)S(1)}, bf16[48,1152]{1,0:T(8,128)(2,1)S(1)}, u32[]{:S(2)}, u32[]{:S(2)}) collective-permute-start(bf16[48,1152]{1,0:T(8,128)(2,1)S(1)} %get-tuple-element.118), channel_id=1, source_target_pairs={{0,2},{1,3},{2,0},{3,1},{4,6},{5,7},{6,4},{7,5},{8,10},{9,11},{10,... | collective-permute-start | bytes 331784 | tf_op jit(solution)/shard_map/ppermute | solution.py:341
  154.7 17.3 %collective-permute-start.28 = (bf16[48,1152]{1,0:T(8,128)(2,1)S(1)}, bf16[48,1152]{1,0:T(8,128)(2,1)S(1)}, u32[]{:S(2)}, u32[]{:S(2)}) collective-permute-start(bf16[48,1152]{1,0:T(8,128)(2,1)S(1)} %get-tuple-element.120), channel_id=1, source_target_pairs={{0,1},{1,2},{2,3},{3,0},{4,5},{5,6},{6,7},{7,4},{8,9},{9,10},{10,1... | collective-permute-start | bytes 331784 | tf_op jit(solution)/shard_map/ppermute | solution.py:341
  155.2 25.8 %collective-permute-start.29 = (bf16[48,1152]{1,0:T(8,128)(2,1)S(1)}, bf16[48,1152]{1,0:T(8,128)(2,1)S(1)}, u32[]{:S(2)}, u32[]{:S(2)}) collective-permute-start(bf16[48,1152]{1,0:T(8,128)(2,1)S(1)} %get-tuple-element.119), channel_id=1, source_target_pairs={{0,3},{1,0},{2,1},{3,2},{4,7},{5,4},{6,5},{7,6},{8,11},{9,8},{10,9... | collective-permute-start | bytes 331784 | tf_op jit(solution)/shard_map/ppermute | solution.py:341
  161.4 62.2 %copy-start.6 = (bf16[256,2304]{1,0:T(8,128)(2,1)}, bf16[256,2304]{1,0:T(8,128)(2,1)S(1)}, u32[]{:S(2)}) copy-start(bf16[256,2304]{1,0:T(8,128)(2,1)S(1)} %maximum_select_fusion.2) | copy-start | bytes 3538948
  161.4 59.4 %collective-permute-start.23 = (bf16[256,2304]{1,0:T(8,128)(2,1)S(1)}, bf16[256,2304]{1,0:T(8,128)(2,1)S(1)}, u32[]{:S(2)}, u32[]{:S(2)}) collective-permute-start(bf16[256,2304]{1,0:T(8,128)(2,1)S(1)} %maximum_select_fusion.2), channel_id=1, source_target_pairs={{0,16},{4,20},{8,24},{12,28},{16,0},{20,4},{24,8},{28,12},{1,17},{... | collective-permute-start | bytes 3538952 | tf_op jit(solution)/shard_map/ppermute | solution.py:337
  167.8 17.8 %collective-permute-start.14 = (bf16[2,5,64,384]{3,2,1,0:T(8,128)(2,1)S(1)}, bf16[2,5,64,384]{3,2,1,0:T(8,128)(2,1)S(1)}, u32[]{:S(2)}, u32[]{:S(2)}) collective-permute-start(bf16[2,5,64,384]{3,2,1,0:T(8,128)(2,1)S(1)} %copy-done.23), channel_id=1, source_target_pairs={{0,1},{1,2},{2,3},{3,0},{4,5},{5,6},{6,7},{7,4},{8,9},{9,10},{10,1... | collective-permute-start | bytes 1474568 | tf_op jit(solution)/shard_map/ppermute | solution.py:341
  181.1 11.3 %collective-permute-start.30 = (bf16[48,1152]{1,0:T(8,128)(2,1)S(1)}, bf16[48,1152]{1,0:T(8,128)(2,1)S(1)}, u32[]{:S(2)}, u32[]{:S(2)}) collective-permute-start(bf16[48,1152]{1,0:T(8,128)(2,1)S(1)} %get-tuple-element.87), channel_id=1, source_target_pairs={{0,2},{1,3},{2,0},{3,1},{4,6},{5,7},{6,4},{7,5},{8,10},{9,11},{10,... | collective-permute-start | bytes 331784 | tf_op jit(solution)/shard_map/ppermute | solution.py:341
  185.6 20.2 %collective-permute-start.15 = (bf16[2,3,64,384]{3,2,1,0:T(8,128)(2,1)S(1)}, bf16[2,3,64,384]{3,2,1,0:T(8,128)(2,1)S(1)}, u32[]{:S(2)}, u32[]{:S(2)}) collective-permute-start(bf16[2,3,64,384]{3,2,1,0:T(8,128)(2,1)S(1)} %get-tuple-element.72), channel_id=1, source_target_pairs={{0,2},{1,3},{2,0},{3,1},{4,6},{5,7},{6,4},{7,5},{8,10},{9,11},{10,... | collective-permute-start | bytes 884744 | tf_op jit(solution)/shard_map/ppermute | solution.py:341
  188.6 12.0 %collective-permute-start.31 = (bf16[48,1152]{1,0:T(8,128)(2,1)S(1)}, bf16[48,1152]{1,0:T(8,128)(2,1)S(1)}, u32[]{:S(2)}, u32[]{:S(2)}) collective-permute-start(bf16[48,1152]{1,0:T(8,128)(2,1)S(1)} %get-tuple-element.87), channel_id=1, source_target_pairs={{0,1},{1,2},{2,3},{3,0},{4,5},{5,6},{6,7},{7,4},{8,9},{9,10},{10,1... | collective-permute-start | bytes 331784 | tf_op jit(solution)/shard_map/ppermute | solution.py:341
  189.6 11.1 %collective-permute-start.32 = (bf16[48,1152]{1,0:T(8,128)(2,1)S(1)}, bf16[48,1152]{1,0:T(8,128)(2,1)S(1)}, u32[]{:S(2)}, u32[]{:S(2)}) collective-permute-start(bf16[48,1152]{1,0:T(8,128)(2,1)S(1)} %get-tuple-element.87), channel_id=1, source_target_pairs={{0,3},{1,0},{2,1},{3,2},{4,7},{5,4},{6,5},{7,6},{8,11},{9,8},{10,9... | collective-permute-start | bytes 331784 | tf_op jit(solution)/shard_map/ppermute | solution.py:341
  200.7 8.4 %collective-permute-start.33 = (bf16[48,4608]{1,0:T(8,128)(2,1)S(1)}, bf16[48,4608]{1,0:T(8,128)(2,1)S(1)}, u32[]{:S(2)}, u32[]{:S(2)}) collective-permute-start(bf16[48,4608]{1,0:T(8,128)(2,1)S(1)} %constant_dynamic-update-slice_fusion.3), channel_id=1, source_target_pairs={{0,16},{4,12},{8,24},{12,4},{16,0},{20,28},{24,8},{28,20},{1,17},{... | collective-permute-start | bytes 1327112 | tf_op jit(solution)/shard_map/ppermute | solution.py:337
  205.8 12.6 %collective-permute-start.16 = (bf16[2,3,64,384]{3,2,1,0:T(8,128)(2,1)S(1)}, bf16[2,3,64,384]{3,2,1,0:T(8,128)(2,1)S(1)}, u32[]{:S(2)}, u32[]{:S(2)}) collective-permute-start(bf16[2,3,64,384]{3,2,1,0:T(8,128)(2,1)S(1)} %get-tuple-element.74), channel_id=1, source_target_pairs={{0,3},{1,0},{2,1},{3,2},{4,7},{5,4},{6,5},{7,6},{8,11},{9,8},{10,9... | collective-permute-start | bytes 884744 | tf_op jit(solution)/shard_map/ppermute | solution.py:341
  209.2 14.1 %collective-permute-start.34 = (bf16[96,4608]{1,0:T(8,128)(2,1)S(1)}, bf16[96,4608]{1,0:T(8,128)(2,1)S(1)}, u32[]{:S(2)}, u32[]{:S(2)}) collective-permute-start(bf16[96,4608]{1,0:T(8,128)(2,1)S(1)} %maximum_select_fusion.3), channel_id=1, source_target_pairs={{0,8},{4,20},{8,0},{12,28},{16,24},{20,4},{24,16},{28,12},{1,9},{5... | collective-permute-start | bytes 2654216 | tf_op jit(solution)/shard_map/ppermute | solution.py:337
  218.4 24.8 %collective-permute-start.17 = (bf16[2,3,64,384]{3,2,1,0:T(8,128)(2,1)}, bf16[2,3,64,384]{3,2,1,0:T(8,128)(2,1)}, u32[]{:S(2)}, u32[]{:S(2)}) collective-permute-start(bf16[2,3,64,384]{3,2,1,0:T(8,128)(2,1)} %get-tuple-element.76), channel_id=1, source_target_pairs={{0,1},{1,2},{2,3},{3,0},{4,5},{5,6},{6,7},{7,4},{8,9},{9,10},{10,1... | collective-permute-start | bytes 884744 | tf_op jit(solution)/shard_map/ppermute | solution.py:341
  223.5 21.3 %collective-permute-start.35 = (bf16[192,4608]{1,0:T(8,128)(2,1)S(1)}, bf16[192,4608]{1,0:T(8,128)(2,1)}, u32[]{:S(2)}, u32[]{:S(2)}) collective-permute-start(bf16[192,4608]{1,0:T(8,128)(2,1)S(1)} %maximum_select_fusion.1.mine_ref), channel_id=1, source_target_pairs={{0,4},{4,0},{8,12},{12,8},{16,20},{20,16},{24,28},{28,24},{1,5},{5... | collective-permute-start | bytes 5308424 | tf_op jit(solution)/shard_map/ppermute | solution.py:337
  (16 other events, 71.1 us)

commit v3 on v2

--- a/solution.py
+++ b/solution.py
@@ -21,8 +21,9 @@
 UP, DOWN, QKV, OUT, WIDE = 0, FF, 2 * FF, 2 * FF + 3 * D, 2 * FF + 4 * D
 FF_TILE = 1536
 CHUNKS = (2, 3, 3)
-GROUPS = ((0, 1), (2,))
-PAD = 8
+SIDE = 640
+COND = 6 * D + SIDE
+LEVEL = COND + 2 * D
 KERNEL_FLOPS = 30_000_000_000
 
 
@@ -57,7 +58,8 @@
 
 
 def layer_kernel(parts, first, last, placed, *refs):
-    live_ref = refs[0]
+    bit_ref, live_ref = refs[:2]
+    refs = refs[1:]
     ins = refs[1 : 1 + parts]
     (mod_ref, wqkv, wout, wup, wdown, bqkv, bout, bup, bdown) = refs[1 + parts : 10 + parts]
     rest = refs[10 + parts :]
@@ -67,7 +69,11 @@
     if placed:
         rest = rest[parts:]
     outs = rest[:parts]
-    gmod_ref, acc_out, bias_acc, acc, probs_ref, sem = rest[parts : parts + 6]
+    gmod_ref, bias_acc, acc_out = rest[parts : parts + 3]
+    if last:
+        give_out = rest[parts + 3]
+        rest = rest[3:]
+    acc, probs_ref, sem = rest[parts + 3 : parts + 6]
     acc_low = rest[parts + 6] if last else acc
     step = pl.program_id(0)
     steps = pl.num_programs(0)
@@ -76,11 +82,23 @@
         @pl.when(step == steps - 1)
         def _():
             if last:
-                acc_low[:, start:stop] = acc[:, start:stop].astype(jnp.bfloat16)
-            sent(start, stop, slot).start()
+                low = bit_ref[0] == 0
+                top = acc[: D // 2, start:stop].astype(jnp.bfloat16)
+                bottom = acc[D // 2 :, start:stop].astype(jnp.bfloat16)
+                acc_low[: D // 2, start:stop] = jnp.where(low, top, bottom)
+                acc_low[D // 2 :, start:stop] = jnp.where(low, bottom, top)
+            for copy in sent(start, stop, slot):
+                copy.start()
 
     def sent(start, stop, slot):
-        return pltpu.make_async_copy(acc_low.at[:, start:stop], acc_out.at[:, start:stop], sem.at[slot])
+        if not last:
+            return [pltpu.make_async_copy(acc.at[:, start:stop], acc_out.at[:, start:stop], sem.at[slot])]
+        return [
+            pltpu.make_async_copy(
+                acc_low.at[k * (D // 2) : (k + 1) * (D // 2), start:stop], out.at[:, start:stop], sem.at[2 * k + slot]
+            )
+            for k, out in enumerate((acc_out, give_out))
+        ]
 
     @pl.when(step == 0)
     def _():
@@ -230,11 +248,11 @@
 
     @pl.when(step == steps - 1)
     def _():
-        sent(UP, QKV, 0).wait()
-        sent(QKV, WIDE, 1).wait()
-
-
-def layer_call(live, blocks, mod, weights, carried, buffers, place, size, last):
+        for copy in sent(UP, QKV, 0) + sent(QKV, WIDE, 1):
+            copy.wait()
+
+
+def layer_call(bit, live, blocks, mod, weights, carried, buffers, place, size, last, room):
     parts = len(blocks)
     images, rows = blocks[0].shape[1:3]
     first = carried is None
@@ -245,24 +263,28 @@
     any_spec = pl.BlockSpec(memory_space=pl.ANY)
     bias_spec = pl.BlockSpec((1, WIDE), lambda i: (0, 0))
     in_specs = (
-        [pl.BlockSpec(memory_space=pltpu.SMEM)] + [block_spec] * parts + [mod_spec] + resident
+        [pl.BlockSpec(memory_space=pltpu.SMEM)] * 2 + [block_spec] * parts + [mod_spec] + resident
     )
-    args = [live, *blocks, mod, *weights]
+    args = [bit.reshape(1), live, *blocks, mod, *weights]
     aliases = {}
     if not first:
         in_specs += [any_spec, bias_spec]
         if not last:
-            aliases[len(args)] = parts + 1
+            aliases[len(args)] = parts + 2
         args += list(carried)
     if buffers is not None:
         in_specs += [any_spec] * parts
         aliases.update({len(args) + p: p for p in range(parts)})
         args += list(buffers)
-    acc_type = jnp.bfloat16 if last else jnp.float32
+    if last:
+        sums = [jax.ShapeDtypeStruct((D // 2, WIDE), jnp.bfloat16)] * 2
+        sums += [jax.ShapeDtypeStruct((room, rows, D), jnp.bfloat16)] * 2
+    else:
+        sums = [jax.ShapeDtypeStruct((D, WIDE), jnp.float32)]
     scratch = [
         pltpu.VMEM((D, WIDE), jnp.float32),
         pltpu.VMEM((HEADS, parts * rows, parts * rows), jnp.float32),
-        pltpu.SemaphoreType.DMA((2,)),
+        pltpu.SemaphoreType.DMA((4,)),
     ]
     if last:
         scratch.append(pltpu.VMEM((D, WIDE), jnp.bfloat16))
@@ -270,13 +292,13 @@
         functools.partial(layer_kernel, parts, first, last, buffers is not None),
         grid=(images,),
         in_specs=in_specs,
-        out_specs=[out_spec] * parts + [mod_spec, any_spec, bias_spec],
+        out_specs=[out_spec] * parts + [mod_spec, bias_spec] + [any_spec] * len(sums),
         out_shape=[jax.ShapeDtypeStruct((2, size, rows, D), jnp.bfloat16)] * parts
         + [
             jax.ShapeDtypeStruct((images, 6, D), jnp.float32),
-            jax.ShapeDtypeStruct((D, WIDE), acc_type),
             jax.ShapeDtypeStruct((1, WIDE), jnp.float32),
-        ],
+        ]
+        + sums,
         scratch_shapes=scratch,
         input_output_aliases=aliases,
         cost_estimate=pl.CostEstimate(
@@ -284,7 +306,7 @@
         ),
         compiler_params=pltpu.CompilerParams(vmem_limit_bytes=52 * 1024 * 1024),
     )(*args)
-    return result[:parts], result[parts], (result[parts + 1], result[parts + 2])
+    return result[:parts], result[parts], (*result[parts + 2 :], result[parts + 1])
 
 
 def finish_kernel(bit_ref, mine_ref, other_ref, up_ref, down_ref, qkv_ref, out_ref):
@@ -315,6 +337,40 @@
     )(bit.reshape(1), mine, other)
 
 
+def ada_kernel(small_ref, weight_ref, grad_ref, bias_ref, side_ref, cond_out, level_ref):
+    rows = small_ref.shape[0]
+    small = small_ref[:, : 6 * D]
+    slot = lax.broadcasted_iota(jnp.int32, (side_ref.shape[0], rows), 0)
+    row = lax.broadcasted_iota(jnp.int32, (side_ref.shape[0], rows), 1)
+    picks = (row % side_ref.shape[0] == slot).astype(jnp.bfloat16)
+    bias_ref[...] = col_sum(dot_nn(picks, small))
+    side_ref[...] = dot_nn(picks, small_ref[:, 6 * D : COND])
+    cond = small_ref[:, COND : COND + D].astype(jnp.float32) + small_ref[:, COND + D : LEVEL].astype(jnp.float32)
+    gate = jax.nn.sigmoid(cond)
+    g_cond = dot_nt(small, weight_ref[...]) * (gate * (1.0 + cond * (1.0 - gate)))
+    cond_out[...] = g_cond
+    levels = small_ref[:, LEVEL : LEVEL + 128].astype(jnp.float32)
+    onehot = (levels == lax.broadcasted_iota(jnp.int32, (rows, 128), 1).astype(jnp.float32)).astype(jnp.float32)
+    level_ref[...] = lax.dot_general(
+        onehot, g_cond, (((0,), (0,)), ((), ())), precision=highest, preferred_element_type=jnp.float32
+    )[:LEVELS]
+    grad_ref[...] = dot_tn((cond * gate).astype(jnp.bfloat16), small)
+
+
+def ada_call(small, weight, own):
+    full = pl.BlockSpec(memory_space=pltpu.VMEM)
+    rows = small.shape[0]
+    shapes = [(D, 6 * D), (1, 6 * D), (own, SIDE), (rows, D), (LEVELS, D)]
+    return pl.pallas_call(
+        ada_kernel,
+        in_specs=[full] * 2,
+        out_specs=[full] * 5,
+        out_shape=[jax.ShapeDtypeStruct(shape, jnp.float32) for shape in shapes],
+        cost_estimate=pl.CostEstimate(flops=6_000_000_000, transcendentals=0, bytes_accessed=8_000_000),
+        compiler_params=pltpu.CompilerParams(vmem_limit_bytes=52 * 1024 * 1024),
+    )(small, weight)
+
+
 def cut(array, start, size, axis=0):
     return lax.dynamic_slice_in_dim(array, start, size, axis)
 
@@ -341,12 +397,26 @@
     return lax.ppermute(array, "seq", [(i, (i + shift) % size) for i in range(size)])
 
 
-def scatter_sum(array, index, place, stages, seq):
-    for stage in stages:
-        size = array.shape[0] // 2
-        bit = stage_bit(stage, index)
-        got = swap(cut(array, (1 - bit) * size, size), stage)
-        array = (cut(array, bit * size, size).astype(jnp.float32) + got.astype(jnp.float32)).astype(jnp.bfloat16)
+def scatter_grp(keep, give, index, stages, after):
+    given = []
+    for k, stage in enumerate(stages):
+        if k in after:
+            give = tied(give, after[k])
+        given.append(give)
+        got = swap(give, stage)
+        if k + 1 < len(stages):
+            size = keep.shape[0] // 2
+            bit = stage_bit(stages[k + 1], index)
+            keep, give = [
+                (cut(keep, b * size, size).astype(jnp.float32) + cut(got, b * size, size).astype(jnp.float32)).astype(
+                    jnp.bfloat16
+                )
+                for b in (bit, 1 - bit)
+            ]
+    return (keep.astype(jnp.float32) + got.astype(jnp.float32)).astype(jnp.bfloat16), given
+
+
+def scatter_seq(array, place, seq):
     size = array.shape[1] // seq
     total = cut(array, place * size, size, 1).astype(jnp.float32)
     for shift in seq_shifts(seq)[1:]:
@@ -371,12 +441,37 @@
     return jnp.where(low, jnp.concatenate([array, got], 0), jnp.concatenate([got, array], 0))
 
 
-def gather_group(array, index, group):
-    bit = 1
-    while bit < group:
-        array = join(array, index, [bit] * group)
-        bit *= 2
-    return array
+def join_seq(array, place, bit, seq):
+    got = lax.ppermute(array, "seq", [(i, i ^ bit) for i in range(seq)])
+    low = (place & bit) == 0
+    return jnp.where(low, jnp.concatenate([array, got], 0), jnp.concatenate([got, array], 0))
+
+
+def join_last(array, index, stage):
+    got = swap(array, stage)
+    low = stage_bit(stage, index) == 0
+    first, second = jnp.where(low, array, got), jnp.where(low, got, array)
+    half = first.shape[0] // 2
+    odd = (index & 1) == 0
+    return jnp.concatenate(
+        [
+            first[:half],
+            jnp.where(odd, second[:half], first[half:]),
+            jnp.where(odd, first[half:], second[:half]),
+            second[half:],
+        ],
+        0,
+    )
+
+
+def group_steps(index, group):
+    stages = group_stages(group)
+    if group == 8:
+        stages[1:] = stages[:0:-1]
+    steps = [functools.partial(join, index=index, stage=stage) for stage in stages]
+    if group == 8:
+        steps[-1] = functools.partial(join_last, index=index, stage=stages[-1])
+    return steps
 
 
 def seq_shifts(seq):
@@ -418,22 +513,23 @@
     index = lax.axis_index("grp")
     stages = group_stages(group)
     shifts = seq_shifts(seq)
-    chunks, groups = (CHUNKS, GROUPS) if sum(CHUNKS) == own else ((own,), ((0,),))
+    chunks = CHUNKS if sum(CHUNKS) == own else (own,)
     starts = [sum(chunks[:c]) for c in range(len(chunks))]
     whole = (tokens.reshape(count, rows, D), cotangent.reshape(count, rows, D))
     condition = condition.reshape(count, D)
     noise_levels = noise_levels.reshape(count)
 
-    def fetch(chunk, after):
-        source = whole if after is None else tied(whole, after)
-        blocks = []
-        for shift in shifts:
-            start = ((place + shift) % seq) * own + starts[chunk]
-            block = jnp.stack([cut(array, start, chunks[chunk]) for array in source])
-            blocks.append(block if shift == 0 else seq_shift(block, shift, seq))
-        return blocks
-
-    blocks = fetch(0, None)
+    def pieces(chunk):
+        return [
+            jnp.stack([cut(array, ((place + shift) % seq) * own + starts[chunk], chunks[chunk]) for array in whole])
+            for shift in shifts
+        ]
+
+    def fetch(sources):
+        return [block if shift == 0 else seq_shift(block, shift, seq) for shift, block in zip(shifts, sources)]
+
+    blocks = fetch(pieces(0))
+    later = [pieces(chunk) for chunk in range(1, len(chunks))]
 
     flags = cut(mask_flags.reshape(count), place * own, own)
     sources = jnp.stack([(place - shift) % seq for shift in shifts])
@@ -457,86 +553,97 @@
         up_bias[None],
         down_bias[None],
     )
-    table = jnp.concatenate(
-        [condition, jnp.broadcast_to(noise_levels[:, None].astype(jnp.float32), (count, 128))], 1
+    high = mine.astype(jnp.bfloat16)
+    own_levels = cut(noise_levels, place * own, own).astype(jnp.bfloat16)
+    side = jnp.concatenate(
+        [high, (mine - high.astype(jnp.float32)).astype(jnp.bfloat16), jnp.broadcast_to(own_levels[:, None], (own, 128))],
+        1,
     )
-    table = gather_group(table, index, group).reshape(group * seq, own, D + 128)
-    table = jnp.pad(table, ((0, 0), (0, PAD), (0, 0)), constant_values=-1.0).reshape(-1, D + 128)
-    real = table[:, D : D + 1] >= 0.0
-    onehot = level_rows(table[:, D].astype(jnp.int32))
-    cond_full = jnp.where(real, table[:, :D] + jnp.dot(onehot, level_table, precision=highest), 0.0)
-    activated = jax.nn.silu(cond_full).astype(jnp.bfloat16)
-    slot = jnp.arange(own + PAD, dtype=jnp.int32)
-    picks = jnp.stack([slot < own] + [slot == own + k for k in range(2)] + [slot < 0] * 5)
-    picks = jnp.tile(picks.astype(jnp.bfloat16), (1, group * seq))
-    live = tied(live, table)
-
+    bit = stage_bit(stages[0], index)
     carried = None
     g_mods = []
+
+    def give(buffer, shift, start, after, source=None):
+        if shift != 0:
+            buffer = seq_shift(tied(buffer, after), -shift, seq)
+        start = ((place + (shift if source is None else source)) % seq) * own + start
+        for k in range(2):
+            targets[k] = lax.dynamic_update_slice_in_dim(targets[k], buffer[k], start, 0)
+        return buffer
+
+    def back(buffers, k, after):
+        return seq_shift(tied(buffers[k], after), -shifts[k], seq) if k else buffers[0]
+
+    def put(buffer, k, chunk):
+        for which in range(2):
+            targets[which] = lax.dynamic_update_slice_in_dim(
+                targets[which], buffer[which], ((place + shifts[k]) % seq) * own + starts[chunk], 0
+            )
+
     held = []
-    for members in groups:
-        buffers = None
-        total = sum(chunks[c] for c in members)
-        for chunk in members:
-            following = fetch(chunk + 1, blocks) if chunk + 1 < len(chunks) else None
-            span = slice(starts[chunk], starts[chunk] + chunks[chunk])
-            buffers, g_mod, carried = layer_call(
-                live[span],
-                blocks,
-                modulation[span],
-                weights,
-                carried,
-                buffers,
-                starts[chunk] - starts[members[0]],
-                total,
-                chunk + 1 == len(chunks),
-            )
-            g_mods.append(g_mod)
-            arrived = blocks
-            blocks = following
+    released = None
+    for chunk in range(len(chunks)):
+        final = chunk + 1 == len(chunks)
+        if chunk == 0:
+            live, later = lax.optimization_barrier((live, later))
+        following = None if final else fetch(tied(later[chunk], blocks))
+        span = slice(starts[chunk], starts[chunk] + chunks[chunk])
+        if final:
+            early = [[back(buffers, k, (blocks, released)) for k in range(len(shifts))] for buffers in held[:-1]]
+            ahead = [back(buffers, 2, (blocks, released)) for buffers in held[-1:]]
+        buffers, g_mod, carried = layer_call(
+            bit, live[span], blocks, modulation[span], weights, carried, None, 0, chunks[chunk], final, count
+        )
         held.append(buffers)
-
-    out_rows = jnp.zeros((count, rows, D), jnp.bfloat16)
-    grad_rows = jnp.zeros((count, rows, D), jnp.bfloat16)
-
-    def give(targets, members, buffers, after):
-        for shift, buffer in zip(shifts, buffers):
-            if shift != 0:
-                after = back = seq_shift(tied(buffer, after), -shift, seq)
-            else:
-                back = buffer
-            start = ((place + shift) % seq) * own + starts[members[0]]
-            targets = [lax.dynamic_update_slice_in_dim(t, back[k], start, 0) for k, t in enumerate(targets)]
-        return targets, after
-
-    summed, bias_sums = carried
+        released = g_mod
+        g_mods.append(g_mod)
+        blocks = following
+
+    keep, send, *targets, bias_sums = carried
+    send = tied(send, (early, ahead))
+    for chunk, buffers in enumerate(early):
+        for k, buffer in enumerate(buffers):
+            put(buffer, k, chunk)
+    after = {}
+    if len(chunks) > 1:
+        middle = [ahead[0] if k == 2 else back(held[-2], k, early) for k in range(len(shifts))]
+        after = {1: middle[3], len(stages): middle[1]}
+        for k, buffer in enumerate(middle):
+            put(buffer, k, len(chunks) - 2)
+    part, given = scatter_grp(keep, send, index, stages, after)
+    if len(stages) in after:
+        part = tied(part, after[len(stages)])
+    quarter = scatter_seq(part, place, seq)
+    given += [part, quarter]
+    part = gather_seq(quarter, place, seq, 1)
+    bias_side = jnp.pad(bias_sums, ((0, 0), (0, own * SIDE - WIDE))).reshape(own, SIDE)
     small = jnp.concatenate(
-        [g.reshape(-1, 6 * D) for g in g_mods]
-        + [bias_sums.reshape(2, 6 * D), jnp.zeros((PAD - 2, 6 * D), jnp.float32)]
-    ).astype(jnp.bfloat16)
-    small = gather_seq(small, place, seq, 0)
-    small = gather_group(small, index, group)
-    sums = dot_nn(picks, small)
-    grad_ada_bias = sums[0]
-    bias_all = sums[1:3].reshape(WIDE)
-    grad_ada = dot_tn(activated, small)
-    g_activated = dot_nt(small, ada_weight)
-    g_cond = jax.vjp(jax.nn.silu, cond_full)[1](g_activated)[0]
-    grad_level = lax.dot_general(
-        onehot, g_cond, (((0,), (0,)), ((), ())), precision=highest, preferred_element_type=jnp.float32
+        [jnp.concatenate([g.reshape(-1, 6 * D) for g in g_mods]).astype(jnp.bfloat16), bias_side.astype(jnp.bfloat16), side],
+        1,
     )
-    grad_condition = cut(g_cond, index * seq * (own + PAD), seq * (own + PAD)).reshape(seq, own + PAD, D)[:, :own]
-
-    part = scatter_sum(summed, index, place, stages, seq)
-    targets, after = give([out_rows, grad_rows], groups[0], held[0], arrived)
-    part = gather_seq(part, place, seq, 1)
-    if len(groups) > 1:
-        targets, after = give(targets, groups[1], held[1], after)
-    for stage in reversed(stages[1:]):
+    small = tied(small, given[1])
+    given = iter(given[-1:] * (len(stages) - 1) + [part])
+    for k in range(seq.bit_length() - 1):
+        small = join_seq(small, place, 1 << k, seq)
+    for step in group_steps(index, group):
+        small = step(tied(small, next(given, part)))
+    grad_ada, grad_ada_bias, bias_side, g_cond, grad_level = ada_call(small, ada_weight, own)
+    final_rows = [back(held[-1], k, part) for k in range(len(shifts))]
+    joins = list(reversed(stages[1:]))
+    for k, stage in enumerate(joins):
+        if k + 1 == len(joins):
+            part = tied(part, (final_rows[1], final_rows[2], small))
         part = join(part, index, stage)
-    grad_up, grad_down, grad_qkv, grad_out = finish(
-        stage_bit(stages[0], index), part, swap(part, stages[0])
-    )
+    part, grad_ada = lax.optimization_barrier((part, grad_ada))
+    part = tied(part, final_rows[3])
+    other = swap(part, stages[0])
+    for k, buffer in enumerate(final_rows):
+        put(buffer, k, len(chunks) - 1)
+    grad_up, grad_down, grad_qkv, grad_out = finish(bit, part, other)
+
+    grad_ada_bias = grad_ada_bias[0]
+    bias_all = bias_side.reshape(own * SIDE)
+    grad_condition = cut(g_cond, index * count, count)
     return (
         targets[0].reshape(batches, images, rows, D),
         targets[1].reshape(batches, images, rows, D),

time: 255 us -> 227 us (0.89)
  local copies, waits for them, and re-layouts: 34.7 us -> 17.4 us
  matrix products: 12.4 us -> 0.54 us
  other arithmetic: 7.91 us -> 15.5 us
  waiting for transfers between devices: 61.6 us -> 56.7 us
  Pallas kernels: 73.3 us -> 77.4 us
  starting transfers between devices: 56.8 us -> 53.8 us
    ppermute x24, waiting for transfers between devices: 45.9 us -> 28.4 us  [seq_shift(): lax.ppermute(array, 'seq', [(i, (i + shift) % size) for i in range(size)])]
    ppermute x12 -> x9, waiting for transfers between devices: 15.6 us -> 28.2 us  [swap(): lax.ppermute(array, 'grp', [(i, i ^ bit) for i, bit in enumerate(stage)])]
    dot_general x5 -> x0, matrix products: 11.8 us -> none  [the longest x1 5.71 us: dot_tn(): lax.dot_general(a, b, (((0,), (0,)), ((), ())), preferred_element_type=jn...]
    pallas_call x0 -> x1, Pallas kernels: none -> 5.72 us  [ada_call(): pl.pallas_call(ada_kernel, in_specs=[full] * 2, out_specs=[full] * 5, out...]
    another operation x13, other arithmetic: 0.46 us -> 5.29 us  [the longest x12 5.28 us: pieces(): jnp.stack([cut(array, (place + shift) % seq * own + starts[chunk], chunks...]
    another operation x12 -> x2, local copies, waits for them, and re-layouts: 7.62 us -> 3.42 us  [pieces(): jnp.stack([cut(array, (place + shift) % seq * own + starts[chunk], chunks...]
    dynamic_slice x6 -> x2, local copies, waits for them, and re-layouts: 4.01 us -> 0.04 us  [cut(): return lax.dynamic_slice_in_dim(array, start, size, axis)]
    convert_element_type x6 -> x4, other arithmetic: 2.91 us -> 6.18 us  [the longest x2 4.42 us: scatter_grp(): (cut(keep, b * size, size).astype(jnp.float32) + cut(got, b * size, size)...]
  transfers between devices with their start and end apart: 36 -> 35, of which waited for: 13 -> 17; matrix products, arithmetic and copies ran while one was open for 19% -> 13% of each run, Pallas kernels for 17% -> 32%
where the time goes in v3:
time: 227 us; the launch traced here: 224 us
  Pallas kernels  77.4 us (34%)
  waiting for transfers between devices  56.7 us (25%)
  starting transfers between devices  53.8 us (24%)
  local copies, waits for them, and re-layouts  17.4 us (8%)
  other arithmetic  15.5 us (7%)
  between operations  2.87 us (1%)
    pallas_call x3, Pallas kernels, layer_call(): pl.pallas_call(functools.partial(layer_kernel, parts, first, last, buffer...  66.9 us
    ppermute x24, starting transfers between devices, seq_shift(): lax.ppermute(array, 'seq', [(i, (i + shift) % size) for i in range(size)])  45.1 us
    ppermute x24, waiting for transfers between devices, seq_shift(): lax.ppermute(array, 'seq', [(i, (i + shift) % size) for i in range(size)])  28.4 us
    ppermute x9, waiting for transfers between devices, swap(): lax.ppermute(array, 'grp', [(i, i ^ bit) for i, bit in enumerate(stage)])  28.2 us
    ppermute x9, starting transfers between devices, swap(): lax.ppermute(array, 'grp', [(i, i ^ bit) for i, bit in enumerate(stage)])  8.54 us
    dynamic_update_slice x12, local copies, waits for them, and re-layouts, put(): lax.dynamic_update_slice_in_dim(targets[which], buffer[which], (place + s...  8.2 us
    pallas_call x1, Pallas kernels, ada_call(): pl.pallas_call(ada_kernel, in_specs=[full] * 2, out_specs=[full] * 5, out...  5.72 us
    another operation x12, other arithmetic, pieces(): jnp.stack([cut(array, (place + shift) % seq * own + starts[chunk], chunks...  5.28 us
  transfers between devices with their start and end apart: 35, of which 17 were waited for; matrix products, arithmetic and copies ran while one was open for 13% of the time, Pallas kernels for 32%

profile of v3, /device:TPU:0, one launch (start us, length us, event | category | flops | bytes accessed | tf_op | source)
XLA Modules:
  0.0 224.2 jit_solution(13057218180199766277)
XLA Ops:
  0.8 1.4 dynamic-slice_bitcast_fusion.16
  2.9 4.1 %collective-permute-start = (bf16[2,2,64,384]{3,2,1,0:T(8,128)(2,1)}, bf16[2,2,64,384]{3,2,1,0:T(8,128)(2,1)S(1)}, u32[]{:S(2)}, u32[]{:S(2)}) collective-permute-start(bf16[2,2,64,384]{3,2,1,0:T(8,128)(2,1)} %pad_maximum_fusion.10), channel_id=1, source_target_pairs={{0,2},{1,3},{2,0},{3,1},{4,6},{5,7},{6,4},{7,5},{8,10},{9,11},{10,... | collective-permute-start | bytes 589832 | tf_op jit(solution)/shard_map/ppermute | solution.py:397
  7.7 1.6 collective-permute-start.1
  10.0 2.2 %collective-permute-start.2 = (bf16[2,2,64,384]{3,2,1,0:T(8,128)(2,1)}, bf16[2,2,64,384]{3,2,1,0:T(8,128)(2,1)S(1)}, u32[]{:S(2)}, u32[]{:S(2)}) collective-permute-start(bf16[2,2,64,384]{3,2,1,0:T(8,128)(2,1)} %pad_maximum_fusion.12), channel_id=1, source_target_pairs={{0,3},{1,0},{2,1},{3,2},{4,7},{5,4},{6,5},{7,6},{8,11},{9,8},{10,9... | collective-permute-start | bytes 589832 | tf_op jit(solution)/shard_map/ppermute | solution.py:397
  14.1 2.0 dynamic-slice_bitcast_fusion
  19.5 1.9 collective-permute-done.refs_3_
  21.4 2.1 collective-permute-done.2.refs_5_
  23.5 3.9 %collective-permute-start.3 = (bf16[2,3,64,384]{3,2,1,0:T(8,128)(2,1)}, bf16[2,3,64,384]{3,2,1,0:T(8,128)(2,1)S(1)}, u32[]{:S(2)}, u32[]{:S(2)}) collective-permute-start(bf16[2,3,64,384]{3,2,1,0:T(8,128)(2,1)} %pad_maximum_fusion.2), channel_id=1, source_target_pairs={{0,2},{1,3},{2,0},{3,1},{4,6},{5,7},{6,4},{7,5},{8,10},{9,11},{10,... | collective-permute-start | bytes 884744 | tf_op jit(solution)/shard_map/ppermute | solution.py:397
  27.4 3.8 %collective-permute-start.5 = (bf16[2,3,64,384]{3,2,1,0:T(8,128)(2,1)S(1)}, bf16[2,3,64,384]{3,2,1,0:T(8,128)(2,1)S(1)}, u32[]{:S(2)}, u32[]{:S(2)}) collective-permute-start(bf16[2,3,64,384]{3,2,1,0:T(8,128)(2,1)S(1)} %copy-done.6), channel_id=1, source_target_pairs={{0,3},{1,0},{2,1},{3,2},{4,7},{5,4},{6,5},{7,6},{8,11},{9,8},{10,9... | collective-permute-start | bytes 884744 | tf_op jit(solution)/shard_map/ppermute | solution.py:397
  31.2 16.6 %shard_map.317 = (bf16[2,2,64,384]{3,2,1,0:T(8,128)(2,1)S(1)}, bf16[2,2,64,384]{3,2,1,0:T(8,128)(2,1)S(1)}, bf16[2,2,64,384]{3,2,1,0:T(8,128)(2,1)S(1)}, bf16[2,...) custom-call(s32[1]{0:T(128)} %bitcast.refs_0_.bit_ref, ...), custom_call_target="tpu_custom_call" | custom-call | flops 60000002048 | bytes 1572864 | tf_op jit(solution)/shard_map/pallas_call | solution.py:291
  48.3 5.2 %collective-permute-start.6 = (bf16[2,3,64,384]{3,2,1,0:T(8,128)(2,1)S(1)}, bf16[2,3,64,384]{3,2,1,0:T(8,128)(2,1)S(1)}, u32[]{:S(2)}, u32[]{:S(2)}) collective-permute-start(bf16[2,3,64,384]{3,2,1,0:T(8,128)(2,1)S(1)} %copy-done.5), channel_id=1, source_target_pairs={{0,2},{1,3},{2,0},{3,1},{4,6},{5,7},{6,4},{7,5},{8,10},{9,11},{10,... | collective-permute-start | bytes 884744 | tf_op jit(solution)/shard_map/ppermute | solution.py:397
  53.5 0.9 collective-permute-start.7
  54.4 2.9 %collective-permute-start.8 = (bf16[2,3,64,384]{3,2,1,0:T(8,128)(2,1)S(1)}, bf16[2,3,64,384]{3,2,1,0:T(8,128)(2,1)S(1)}, u32[]{:S(2)}, u32[]{:S(2)}) collective-permute-start(bf16[2,3,64,384]{3,2,1,0:T(8,128)(2,1)S(1)} %pad_maximum_fusion.8), channel_id=1, source_target_pairs={{0,3},{1,0},{2,1},{3,2},{4,7},{5,4},{6,5},{7,6},{8,11},{9,8},{10,9... | collective-permute-start | bytes 884744 | tf_op jit(solution)/shard_map/ppermute | solution.py:397
  57.3 24.4 %shard_map.318 = (bf16[2,3,64,384]{3,2,1,0:T(8,128)(2,1)S(1)}, bf16[2,3,64,384]{3,2,1,0:T(8,128)(2,1)S(1)}, bf16[2,3,64,384]{3,2,1,0:T(8,128)(2,1)S(1)}, bf16[2,...) custom-call(s32[1]{0:T(128)} %bitcast.refs_0_.bit_ref, ...), custom_call_target="tpu_custom_call", output_to_operand_aliasing={{6}: (15, {})} | custom-call | flops 89999998976 | bytes 2359296 | tf_op jit(solution)/shard_map/pallas_call | solution.py:291
  81.9 1.5 collective-permute-start.10
  84.0 3.2 %collective-permute-start.13 = (bf16[2,3,64,384]{3,2,1,0:T(8,128)(2,1)S(1)}, bf16[2,3,64,384]{3,2,1,0:T(8,128)(2,1)S(1)}, u32[]{:S(2)}, u32[]{:S(2)}) collective-permute-start(bf16[2,3,64,384]{3,2,1,0:T(8,128)(2,1)S(1)} %get-tuple-element.118), channel_id=1, source_target_pairs={{0,3},{1,0},{2,1},{3,2},{4,7},{5,4},{6,5},{7,6},{8,11},{9,8},{10,9... | collective-permute-start | bytes 884744 | tf_op jit(solution)/shard_map/ppermute | solution.py:397
  87.2 25.8 %shard_map.319 = (bf16[2,3,64,384]{3,2,1,0:T(8,128)(2,1)S(1)}, bf16[2,3,64,384]{3,2,1,0:T(8,128)(2,1)S(1)}, bf16[2,3,64,384]{3,2,1,0:T(8,128)(2,1)S(1)}, bf16[2,...) custom-call(s32[1]{0:T(128)} %bitcast.refs_0_.bit_ref, ...), custom_call_target="tpu_custom_call" | custom-call | flops 89999998976 | bytes 2359296 | tf_op jit(solution)/shard_map/pallas_call | solution.py:291
  116.5 1.3 collective-permute-done.15
  117.8 3.3 %add_convert_fusion.1 = (bf16[96,4608]{1,0:T(8,128)(2,1)S(1)}, bf16[96,4608]{1,0:T(8,128)(2,1)}) fusion(bf16[192,4608]{1,0:T(8,128)(2,1)} %collective-permute-done.15, s32[]{:T(128)S(6)} %select_n.376, bf16[192,4608]{1,0:T(8,128)(2,1)} %get-tuple-element.123, s32[]{:T(128)S(6)} %select_n.379), kind=kLoop, calls=%fused_computation.4 | loop fusion | flops 3538944 | bytes 5308424 | tf_op jit(solution)/shard_map/convert_element_type | solution.py:411
  121.1 6.6 %collective-permute-done.14 = bf16[2,3,64,384]{3,2,1,0:T(8,128)(2,1)S(1)} collective-permute-done((bf16[2,3,64,384]{3,2,1,0:T(8,128)(2,1)S(1)}, bf16[2,3,64,384]{3,2,1,0:T(8,128)(2,1)S(1)}, u32[]{:S(2)}, u32[]{:S(2)}) %collective-permute-start.14) | collective-permute-done | bytes 294944 | tf_op jit(solution)/shard_map/ppermute | solution.py:397
  127.7 1.5 collective-permute-start.16
  129.6 11.4 %collective-permute-done.16 = bf16[96,4608]{1,0:T(8,128)(2,1)} collective-permute-done((bf16[96,4608]{1,0:T(8,128)(2,1)}, bf16[96,4608]{1,0:T(8,128)(2,1)}, u32[]{:S(2)}, u32[]{:S(2)}) %collective-permute-start.16) | collective-permute-done | bytes 884768 | tf_op jit(solution)/shard_map/ppermute | solution.py:393
  141.0 1.1 add_convert_fusion.3
  142.1 1.6 collective-permute-start.17
  143.9 6.6 %collective-permute-done.17 = bf16[48,4608]{1,0:T(8,128)(2,1)S(1)} collective-permute-done((bf16[48,4608]{1,0:T(8,128)(2,1)S(1)}, bf16[48,4608]{1,0:T(8,128)(2,1)S(1)}, u32[]{:S(2)}, u32[]{:S(2)}) %collective-permute-start.17) | collective-permute-done | bytes 442400 | tf_op jit(solution)/shard_map/ppermute | solution.py:393
  150.5 1.2 add_convert_fusion.2
  151.8 2.0 collective-permute-start.19
  153.9 2.9 %collective-permute-done.20 = bf16[48,1152]{1,0:T(8,128)(2,1)S(1)} collective-permute-done((bf16[48,1152]{1,0:T(8,128)(2,1)S(1)}, bf16[48,1152]{1,0:T(8,128)(2,1)S(1)}, u32[]{:S(2)}, u32[]{:S(2)}) %collective-permute-start.20) | collective-permute-done | bytes 110624 | tf_op jit(solution)/shard_map/ppermute | solution.py:397
  156.8 1.6 collective-permute-done.19
  158.4 3.2 %collective-permute-done.18 = bf16[48,1152]{1,0:T(8,128)(2,1)S(1)} collective-permute-done((bf16[48,1152]{1,0:T(8,128)(2,1)S(1)}, bf16[48,1152]{1,0:T(8,128)(2,1)S(1)}, u32[]{:S(2)}, u32[]{:S(2)}) %collective-permute-start.18) | collective-permute-done | bytes 110624 | tf_op jit(solution)/shard_map/ppermute | solution.py:397
  163.4 2.6 %collective-permute-start.22 = (bf16[48,1152]{1,0:T(8,128)(2,1)S(1)}, bf16[48,1152]{1,0:T(8,128)(2,1)S(1)}, u32[]{:S(2)}, u32[]{:S(2)}) collective-permute-start(bf16[48,1152]{1,0:T(8,128)(2,1)S(1)} %get-tuple-element.157), channel_id=1, source_target_pairs={{0,1},{1,2},{2,3},{3,0},{4,5},{5,6},{6,7},{7,4},{8,9},{9,10},{10,1... | collective-permute-start | bytes 331784 | tf_op jit(solution)/shard_map/ppermute | solution.py:397
  166.1 1.2 collective-permute-start.23
  167.4 1.6 collective-permute-start.30
  169.0 5.1 %collective-permute-done.21 = bf16[48,1152]{1,0:T(8,128)(2,1)S(1)} collective-permute-done((bf16[48,1152]{1,0:T(8,128)(2,1)S(1)}, bf16[48,1152]{1,0:T(8,128)(2,1)S(1)}, u32[]{:S(2)}, u32[]{:S(2)}) %collective-permute-start.21) | collective-permute-done | bytes 110624 | tf_op jit(solution)/shard_map/ppermute | solution.py:397
  174.1 1.5 collective-permute-done.23
  175.6 1.6 collective-permute-start.32
  177.4 1.5 collective-permute-start.31
  180.3 1.4 collective-permute-start.24
  181.6 2.3 %collective-permute-start.25 = (bf16[2,3,64,384]{3,2,1,0:T(8,128)(2,1)S(1)}, bf16[2,3,64,384]{3,2,1,0:T(8,128)(2,1)S(1)}, u32[]{:S(2)}, u32[]{:S(2)}) collective-permute-start(bf16[2,3,64,384]{3,2,1,0:T(8,128)(2,1)S(1)} %get-tuple-element.130), channel_id=1, source_target_pairs={{0,3},{1,0},{2,1},{3,2},{4,7},{5,4},{6,5},{7,6},{8,11},{9,8},{10,9... | collective-permute-start | bytes 884744 | tf_op jit(solution)/shard_map/ppermute | solution.py:397
  184.0 4.8 %collective-permute-done.32 = bf16[48,4608]{1,0:T(8,128)(2,1)S(1)} collective-permute-done((bf16[48,4608]{1,0:T(8,128)(2,1)S(1)}, bf16[48,4608]{1,0:T(8,128)(2,1)S(1)}, u32[]{:S(2)}, u32[]{:S(2)}) %collective-permute-start.32) | collective-permute-done | bytes 442400 | tf_op jit(solution)/shard_map/ppermute | solution.py:393
  188.9 3.9 %collective-permute-done.31 = bf16[128,3840]{1,0:T(8,128)(2,1)S(1)} collective-permute-done((bf16[128,3840]{1,0:T(8,128)(2,1)S(1)}, bf16[128,3840]{1,0:T(8,128)(2,1)S(1)}, u32[]{:S(2)}, u32[]{:S(2)}) %collective-permute-start.31) | collective-permute-done | bytes 983072 | tf_op jit(solution)/shard_map/ppermute | solution.py:393
  193.1 1.4 pad_maximum_fusion.small_ref
  194.5 2.2 %collective-permute-done.24 = bf16[2,3,64,384]{3,2,1,0:T(8,128)(2,1)S(1)} collective-permute-done((bf16[2,3,64,384]{3,2,1,0:T(8,128)(2,1)S(1)}, bf16[2,3,64,384]{3,2,1,0:T(8,128)(2,1)S(1)}, u32[]{:S(2)}, u32[]{:S(2)}) %collective-permute-start.24) | collective-permute-done | bytes 294944 | tf_op jit(solution)/shard_map/ppermute | solution.py:397
  198.7 5.2 %collective-permute-start.26 = (bf16[2,3,64,384]{3,2,1,0:T(8,128)(2,1)S(1)}, bf16[2,3,64,384]{3,2,1,0:T(8,128)(2,1)S(1)}, u32[]{:S(2)}, u32[]{:S(2)}) collective-permute-start(bf16[2,3,64,384]{3,2,1,0:T(8,128)(2,1)S(1)} %get-tuple-element.132), channel_id=1, source_target_pairs={{0,1},{1,2},{2,3},{3,0},{4,5},{5,6},{6,7},{7,4},{8,9},{9,10},{10,1... | collective-permute-start | bytes 884744 | tf_op jit(solution)/shard_map/ppermute | solution.py:397
  204.0 5.7 %shard_map.320 = (f32[384,2304]{1,0:T(8,128)}, f32[1,2304]{1,0:T(1,128)S(1)}, f32[8,640]{1,0:T(8,128)S(1)}, f32[256,384]{1,0:T(8,128)S(1)}, f32[64,384]{1,0:T(8,128)}) custom-call(bf16[256,3840]{1,0:T(8,128)(2,1)} %pad_maximum_fusion.small_ref, bf16[384,2304]{1,0:T(8,128)(2,1)} %weight_ref.1), custom_call_target="tpu_custom_call" | custom-call | flops 6000000000 | bytes 8000000 | tf_op jit(solution)/shard_map/pallas_call | solution.py:364
  210.1 0.9 collective-permute-done.26
  215.2 1.1 copy-done.27
  219.4 4.8 %shard_map.321 = (f32[384,1536]{1,0:T(8,128)}, f32[1536,384]{1,0:T(8,128)}, f32[384,1152]{1,0:T(8,128)}, f32[384,384]{1,0:T(8,128)}) custom-call(s32[1]{0:T(128)} %bitcast.refs_0_.bit_ref, bf16[192,4608]{1,0:T(8,128)(2,1)S(1)} %maximum_select_fusion.mine_ref, bf16[192,4608]{1,0:T(8,128)(2,1)} %collective-permute-done.34.other_ref), custom_call_target="tpu_custom_call" | custom-call | tf_op jit(solution)/shard_map/pallas_call | solution.py:331
  (188 shorter events, 24.4 us)
Async XLA Ops:
  0.6 12.4 %copy-start = (f32[64,384]{1,0:T(8,128)S(1)}, f32[64,384]{1,0:T(8,128)}, u32[]{:S(2)}) copy-start(f32[64,384]{1,0:T(8,128)} %param.27) | copy-start | bytes 294916
  0.7 11.6 %copy-start.17 = (f32[16,2,384]{2,1,0:T(2,128)S(1)}, f32[16,2,384]{2,1,0:T(2,128)}, u32[]{:S(2)}) copy-start(f32[16,2,384]{2,1,0:T(2,128)} %param.24) | copy-start | bytes 147460
  0.7 11.6 %copy-start.24 = (s32[16,2]{0,1:T(2,128)S(1)}, s32[16,2]{0,1:T(2,128)}, u32[]{:S(2)}) copy-start(s32[16,2]{0,1:T(2,128)} %param.26) | copy-start | bytes 388
  0.7 12.5 %copy-start.3 = (bf16[384,2304]{1,0:T(8,128)(2,1)S(1)}, bf16[384,2304]{1,0:T(8,128)(2,1)}, u32[]{:S(2)}) copy-start(bf16[384,2304]{1,0:T(8,128)(2,1)} %weight_ref.1) | copy-start | bytes 5308420
  0.7 12.5 %copy-start.18 = (f32[2304]{0:T(1024)S(1)}, f32[2304]{0:T(1024)}, u32[]{:S(2)}) copy-start(f32[2304]{0:T(1024)} %param.29) | copy-start | bytes 27652
  2.9 18.5 %collective-permute-start = (bf16[2,2,64,384]{3,2,1,0:T(8,128)(2,1)}, bf16[2,2,64,384]{3,2,1,0:T(8,128)(2,1)S(1)}, u32[]{:S(2)}, u32[]{:S(2)}) collective-permute-start(bf16[2,2,64,384]{3,2,1,0:T(8,128)(2,1)} %pad_maximum_fusion.10), channel_id=1, source_target_pairs={{0,2},{1,3},{2,0},{3,1},{4,6},{5,7},{6,4},{7,5},{8,10},{9,11},{10,... | collective-permute-start | bytes 589832 | tf_op jit(solution)/shard_map/ppermute | solution.py:397
  7.7 13.7 %collective-permute-start.1 = (bf16[2,2,64,384]{3,2,1,0:T(8,128)(2,1)}, bf16[2,2,64,384]{3,2,1,0:T(8,128)(2,1)S(1)}, u32[]{:S(2)}, u32[]{:S(2)}) collective-permute-start(bf16[2,2,64,384]{3,2,1,0:T(8,128)(2,1)} %pad_maximum_fusion.11), channel_id=1, source_target_pairs={{0,1},{1,2},{2,3},{3,0},{4,5},{5,6},{6,7},{7,4},{8,9},{9,10},{10,1... | collective-permute-start | bytes 589832 | tf_op jit(solution)/shard_map/ppermute | solution.py:397
  10.0 13.6 %collective-permute-start.2 = (bf16[2,2,64,384]{3,2,1,0:T(8,128)(2,1)}, bf16[2,2,64,384]{3,2,1,0:T(8,128)(2,1)S(1)}, u32[]{:S(2)}, u32[]{:S(2)}) collective-permute-start(bf16[2,2,64,384]{3,2,1,0:T(8,128)(2,1)} %pad_maximum_fusion.12), channel_id=1, source_target_pairs={{0,3},{1,0},{2,1},{3,2},{4,7},{5,4},{6,5},{7,6},{8,11},{9,8},{10,9... | collective-permute-start | bytes 589832 | tf_op jit(solution)/shard_map/ppermute | solution.py:397
  18.4 12.8 %copy-start.2 = (bf16[384,384]{1,0:T(8,128)(2,1)S(1)}, bf16[384,384]{1,0:T(8,128)(2,1)}, u32[]{:S(2)}) copy-start(bf16[384,384]{1,0:T(8,128)(2,1)} %refs_8_.5) | copy-start | bytes 884740
  23.5 24.3 %collective-permute-start.3 = (bf16[2,3,64,384]{3,2,1,0:T(8,128)(2,1)}, bf16[2,3,64,384]{3,2,1,0:T(8,128)(2,1)S(1)}, u32[]{:S(2)}, u32[]{:S(2)}) collective-permute-start(bf16[2,3,64,384]{3,2,1,0:T(8,128)(2,1)} %pad_maximum_fusion.2), channel_id=1, source_target_pairs={{0,2},{1,3},{2,0},{3,1},{4,6},{5,7},{6,4},{7,5},{8,10},{9,11},{10,... | collective-permute-start | bytes 884744 | tf_op jit(solution)/shard_map/ppermute | solution.py:397
  27.4 20.5 %collective-permute-start.4 = (bf16[2,3,64,384]{3,2,1,0:T(8,128)(2,1)}, bf16[2,3,64,384]{3,2,1,0:T(8,128)(2,1)S(1)}, u32[]{:S(2)}, u32[]{:S(2)}) collective-permute-start(bf16[2,3,64,384]{3,2,1,0:T(8,128)(2,1)} %pad_maximum_fusion.3), channel_id=1, source_target_pairs={{0,1},{1,2},{2,3},{3,0},{4,5},{5,6},{6,7},{7,4},{8,9},{9,10},{10,1... | collective-permute-start | bytes 884744 | tf_op jit(solution)/shard_map/ppermute | solution.py:397
  27.4 20.9 %collective-permute-start.5 = (bf16[2,3,64,384]{3,2,1,0:T(8,128)(2,1)S(1)}, bf16[2,3,64,384]{3,2,1,0:T(8,128)(2,1)S(1)}, u32[]{:S(2)}, u32[]{:S(2)}) collective-permute-start(bf16[2,3,64,384]{3,2,1,0:T(8,128)(2,1)S(1)} %copy-done.6), channel_id=1, source_target_pairs={{0,3},{1,0},{2,1},{3,2},{4,7},{5,4},{6,5},{7,6},{8,11},{9,8},{10,9... | collective-permute-start | bytes 884744 | tf_op jit(solution)/shard_map/ppermute | solution.py:397
  31.2 17.1 %copy-start.5 = (bf16[2,3,64,384]{3,2,1,0:T(8,128)(2,1)S(1)}, bf16[2,3,64,384]{3,2,1,0:T(8,128)(2,1)}, u32[]{:S(2)}) copy-start(bf16[2,3,64,384]{3,2,1,0:T(8,128)(2,1)} %pad_maximum_fusion.6) | copy-start | bytes 884740
  48.3 33.5 %collective-permute-start.6 = (bf16[2,3,64,384]{3,2,1,0:T(8,128)(2,1)S(1)}, bf16[2,3,64,384]{3,2,1,0:T(8,128)(2,1)S(1)}, u32[]{:S(2)}, u32[]{:S(2)}) collective-permute-start(bf16[2,3,64,384]{3,2,1,0:T(8,128)(2,1)S(1)} %copy-done.5), channel_id=1, source_target_pairs={{0,2},{1,3},{2,0},{3,1},{4,6},{5,7},{6,4},{7,5},{8,10},{9,11},{10,... | collective-permute-start | bytes 884744 | tf_op jit(solution)/shard_map/ppermute | solution.py:397
  53.5 28.3 %collective-permute-start.7 = (bf16[2,3,64,384]{3,2,1,0:T(8,128)(2,1)S(1)}, bf16[2,3,64,384]{3,2,1,0:T(8,128)(2,1)S(1)}, u32[]{:S(2)}, u32[]{:S(2)}) collective-permute-start(bf16[2,3,64,384]{3,2,1,0:T(8,128)(2,1)S(1)} %pad_maximum_fusion.7), channel_id=1, source_target_pairs={{0,1},{1,2},{2,3},{3,0},{4,5},{5,6},{6,7},{7,4},{8,9},{9,10},{10,1... | collective-permute-start | bytes 884744 | tf_op jit(solution)/shard_map/ppermute | solution.py:397
  54.4 27.4 %collective-permute-start.8 = (bf16[2,3,64,384]{3,2,1,0:T(8,128)(2,1)S(1)}, bf16[2,3,64,384]{3,2,1,0:T(8,128)(2,1)S(1)}, u32[]{:S(2)}, u32[]{:S(2)}) collective-permute-start(bf16[2,3,64,384]{3,2,1,0:T(8,128)(2,1)S(1)} %pad_maximum_fusion.8), channel_id=1, source_target_pairs={{0,3},{1,0},{2,1},{3,2},{4,7},{5,4},{6,5},{7,6},{8,11},{9,8},{10,9... | collective-permute-start | bytes 884744 | tf_op jit(solution)/shard_map/ppermute | solution.py:397
  81.8 31.2 %collective-permute-start.9 = (bf16[2,2,64,384]{3,2,1,0:T(8,128)(2,1)S(1)}, bf16[2,2,64,384]{3,2,1,0:T(8,128)(2,1)S(1)}, u32[]{:S(2)}, u32[]{:S(2)}) collective-permute-start(bf16[2,2,64,384]{3,2,1,0:T(8,128)(2,1)S(1)} %get-tuple-element.109), channel_id=1, source_target_pairs={{0,2},{1,3},{2,0},{3,1},{4,6},{5,7},{6,4},{7,5},{8,10},{9,11},{10,... | collective-permute-start | bytes 589832 | tf_op jit(solution)/shard_map/ppermute | solution.py:397
  81.9 31.1 %collective-permute-start.10 = (bf16[2,2,64,384]{3,2,1,0:T(8,128)(2,1)S(1)}, bf16[2,2,64,384]{3,2,1,0:T(8,128)(2,1)S(1)}, u32[]{:S(2)}, u32[]{:S(2)}) collective-permute-start(bf16[2,2,64,384]{3,2,1,0:T(8,128)(2,1)S(1)} %get-tuple-element.111), channel_id=1, source_target_pairs={{0,3},{1,0},{2,1},{3,2},{4,7},{5,4},{6,5},{7,6},{8,11},{9,8},{10,9... | collective-permute-start | bytes 589832 | tf_op jit(solution)/shard_map/ppermute | solution.py:397
  83.4 29.7 %collective-permute-start.11 = (bf16[2,2,64,384]{3,2,1,0:T(8,128)(2,1)S(1)}, bf16[2,2,64,384]{3,2,1,0:T(8,128)(2,1)S(1)}, u32[]{:S(2)}, u32[]{:S(2)}) collective-permute-start(bf16[2,2,64,384]{3,2,1,0:T(8,128)(2,1)S(1)} %get-tuple-element.113), channel_id=1, source_target_pairs={{0,1},{1,2},{2,3},{3,0},{4,5},{5,6},{6,7},{7,4},{8,9},{9,10},{10,1... | collective-permute-start | bytes 589832 | tf_op jit(solution)/shard_map/ppermute | solution.py:397
  84.0 29.1 %collective-permute-start.13 = (bf16[2,3,64,384]{3,2,1,0:T(8,128)(2,1)S(1)}, bf16[2,3,64,384]{3,2,1,0:T(8,128)(2,1)S(1)}, u32[]{:S(2)}, u32[]{:S(2)}) collective-permute-start(bf16[2,3,64,384]{3,2,1,0:T(8,128)(2,1)S(1)} %get-tuple-element.118), channel_id=1, source_target_pairs={{0,3},{1,0},{2,1},{3,2},{4,7},{5,4},{6,5},{7,6},{8,11},{9,8},{10,9... | collective-permute-start | bytes 884744 | tf_op jit(solution)/shard_map/ppermute | solution.py:397
  87.2 26.5 %copy-start.33 = (s32[8]{0:T(128)S(1)}, s32[8]{0:T(128)}, u32[]{:S(2)}) copy-start(s32[8]{0:T(128)} %constant.206.clone) | copy-start | bytes 100
  87.2 27.8 %copy-start.32 = (s32[8]{0:T(128)S(1)}, s32[8]{0:T(128)}, u32[]{:S(2)}) copy-start(s32[8]{0:T(128)} %constant.207.clone) | copy-start | bytes 100
  113.7 4.0 %collective-permute-start.15 = (bf16[192,4608]{1,0:T(8,128)(2,1)}, bf16[192,4608]{1,0:T(8,128)(2,1)}, u32[]{:S(2)}, u32[]{:S(2)}) collective-permute-start(bf16[192,4608]{1,0:T(8,128)(2,1)} %get-tuple-element.125), channel_id=1, source_target_pairs={{0,4},{4,0},{8,12},{12,8},{16,20},{20,16},{24,28},{28,24},{1,5},{5... | collective-permute-start | bytes 5308424 | tf_op jit(solution)/shard_map/ppermute | solution.py:393
  116.4 11.3 %collective-permute-start.14 = (bf16[2,3,64,384]{3,2,1,0:T(8,128)(2,1)S(1)}, bf16[2,3,64,384]{3,2,1,0:T(8,128)(2,1)S(1)}, u32[]{:S(2)}, u32[]{:S(2)}) collective-permute-start(bf16[2,3,64,384]{3,2,1,0:T(8,128)(2,1)S(1)} %get-tuple-element.120), channel_id=1, source_target_pairs={{0,1},{1,2},{2,3},{3,0},{4,5},{5,6},{6,7},{7,4},{8,9},{9,10},{10,1... | collective-permute-start | bytes 884744 | tf_op jit(solution)/shard_map/ppermute | solution.py:397
  117.8 11.6 %copy-start.10 = (f32[8,384]{1,0:T(8,128)S(1)}, f32[8,384]{1,0:T(8,128)}, u32[]{:S(2)}) copy-start(f32[8,384]{1,0:T(8,128)} %copy-done.9) | copy-start | bytes 36868
  117.8 11.6 %copy-start.23 = (bf16[8]{0:T(256)(128)(2,1)S(1)}, bf16[8]{0:T(256)(128)(2,1)}, u32[]{:S(2)}) copy-start(bf16[8]{0:T(256)(128)(2,1)} %get-tuple-element.154) | copy-start | bytes 52
  127.7 13.4 %collective-permute-start.16 = (bf16[96,4608]{1,0:T(8,128)(2,1)}, bf16[96,4608]{1,0:T(8,128)(2,1)}, u32[]{:S(2)}, u32[]{:S(2)}) collective-permute-start(bf16[96,4608]{1,0:T(8,128)(2,1)} %get-tuple-element.126), channel_id=1, source_target_pairs={{0,8},{4,20},{8,0},{12,28},{16,24},{20,4},{24,16},{28,12},{1,9},{5... | collective-permute-start | bytes 2654216 | tf_op jit(solution)/shard_map/ppermute | solution.py:393
  129.5 22.2 %collective-permute-start.12 = (bf16[2,3,64,384]{3,2,1,0:T(8,128)(2,1)S(1)}, bf16[2,3,64,384]{3,2,1,0:T(8,128)(2,1)S(1)}, u32[]{:S(2)}, u32[]{:S(2)}) collective-permute-start(bf16[2,3,64,384]{3,2,1,0:T(8,128)(2,1)S(1)} %get-tuple-element.116), channel_id=1, source_target_pairs={{0,2},{1,3},{2,0},{3,1},{4,6},{5,7},{6,4},{7,5},{8,10},{9,11},{10,... | collective-permute-start | bytes 884744 | tf_op jit(solution)/shard_map/ppermute | solution.py:397
  129.5 14.3 %collective-permute-start.27 = (bf16[8,3840]{1,0:T(8,128)(2,1)S(1)}, bf16[8,3840]{1,0:T(8,128)(2,1)S(1)}, u32[]{:S(2)}, u32[]{:S(2)}) collective-permute-start(bf16[8,3840]{1,0:T(8,128)(2,1)S(1)} %constant_dynamic-update-slice_fusion.4), channel_id=1, source_target_pairs={{0,1},{1,0},{2,3},{3,2},{4,5},{5,4},{6,7},{7,6},{8,9},{9,8},{10,11... | collective-permute-start | bytes 184328 | tf_op jit(solution)/shard_map/ppermute | solution.py:445
  142.1 8.4 %collective-permute-start.17 = (bf16[48,4608]{1,0:T(8,128)(2,1)S(1)}, bf16[48,4608]{1,0:T(8,128)(2,1)S(1)}, u32[]{:S(2)}, u32[]{:S(2)}) collective-permute-start(bf16[48,4608]{1,0:T(8,128)(2,1)S(1)} %add_convert_fusion.3), channel_id=1, source_target_pairs={{0,16},{4,12},{8,24},{12,4},{16,0},{20,28},{24,8},{28,20},{1,17},{... | collective-permute-start | bytes 1327112 | tf_op jit(solution)/shard_map/ppermute | solution.py:393
  143.8 10.1 %collective-permute-start.28 = (bf16[16,3840]{1,0:T(8,128)(2,1)S(1)}, bf16[16,3840]{1,0:T(8,128)(2,1)S(1)}, u32[]{:S(2)}, u32[]{:S(2)}) collective-permute-start(bf16[16,3840]{1,0:T(8,128)(2,1)S(1)} %maximum_select_fusion.5), channel_id=1, source_target_pairs={{0,2},{1,3},{2,0},{3,1},{4,6},{5,7},{6,4},{7,5},{8,10},{9,11},{10,... | collective-permute-start | bytes 368648 | tf_op jit(solution)/shard_map/ppermute | solution.py:445
  151.8 5.1 %collective-permute-start.20 = (bf16[48,1152]{1,0:T(8,128)(2,1)S(1)}, bf16[48,1152]{1,0:T(8,128)(2,1)S(1)}, u32[]{:S(2)}, u32[]{:S(2)}) collective-permute-start(bf16[48,1152]{1,0:T(8,128)(2,1)S(1)} %get-tuple-element.191), channel_id=1, source_target_pairs={{0,3},{1,0},{2,1},{3,2},{4,7},{5,4},{6,5},{7,6},{8,11},{9,8},{10,9... | collective-permute-start | bytes 331784 | tf_op jit(solution)/shard_map/ppermute | solution.py:397
  151.8 6.6 %collective-permute-start.19 = (bf16[48,1152]{1,0:T(8,128)(2,1)S(1)}, bf16[48,1152]{1,0:T(8,128)(2,1)S(1)}, u32[]{:S(2)}, u32[]{:S(2)}) collective-permute-start(bf16[48,1152]{1,0:T(8,128)(2,1)S(1)} %get-tuple-element.192), channel_id=1, source_target_pairs={{0,1},{1,2},{2,3},{3,0},{4,5},{5,6},{6,7},{7,4},{8,9},{9,10},{10,1... | collective-permute-start | bytes 331784 | tf_op jit(solution)/shard_map/ppermute | solution.py:397
  153.8 7.8 %collective-permute-start.18 = (bf16[48,1152]{1,0:T(8,128)(2,1)S(1)}, bf16[48,1152]{1,0:T(8,128)(2,1)S(1)}, u32[]{:S(2)}, u32[]{:S(2)}) collective-permute-start(bf16[48,1152]{1,0:T(8,128)(2,1)S(1)} %get-tuple-element.190), channel_id=1, source_target_pairs={{0,2},{1,3},{2,0},{3,1},{4,6},{5,7},{6,4},{7,5},{8,10},{9,11},{10,... | collective-permute-start | bytes 331784 | tf_op jit(solution)/shard_map/ppermute | solution.py:397
  161.7 5.5 %collective-permute-start.29 = (bf16[32,3840]{1,0:T(8,128)(2,1)S(1)}, bf16[32,3840]{1,0:T(8,128)(2,1)S(1)}, u32[]{:S(2)}, u32[]{:S(2)}) collective-permute-start(bf16[32,3840]{1,0:T(8,128)(2,1)S(1)} %maximum_select_fusion.4), channel_id=1, source_target_pairs={{0,4},{4,0},{8,12},{12,8},{16,20},{20,16},{24,28},{28,24},{1,5},{5... | collective-permute-start | bytes 737288 | tf_op jit(solution)/shard_map/ppermute | solution.py:393
  163.1 15.8 %copy-start.14 = (bf16[2,2,64,384]{3,2,1,0:T(8,128)(2,1)S(1)}, bf16[2,2,64,384]{3,2,1,0:T(8,128)(2,1)}, u32[]{:S(2)}) copy-start(bf16[2,2,64,384]{3,2,1,0:T(8,128)(2,1)} %copy-done.13) | copy-start | bytes 589828
  163.1 10.9 %collective-permute-start.21 = (bf16[48,1152]{1,0:T(8,128)(2,1)S(1)}, bf16[48,1152]{1,0:T(8,128)(2,1)S(1)}, u32[]{:S(2)}, u32[]{:S(2)}) collective-permute-start(bf16[48,1152]{1,0:T(8,128)(2,1)S(1)} %get-tuple-element.157), channel_id=1, source_target_pairs={{0,2},{1,3},{2,0},{3,1},{4,6},{5,7},{6,4},{7,5},{8,10},{9,11},{10,... | collective-permute-start | bytes 331784 | tf_op jit(solution)/shard_map/ppermute | solution.py:397
  163.4 10.6 %collective-permute-start.22 = (bf16[48,1152]{1,0:T(8,128)(2,1)S(1)}, bf16[48,1152]{1,0:T(8,128)(2,1)S(1)}, u32[]{:S(2)}, u32[]{:S(2)}) collective-permute-start(bf16[48,1152]{1,0:T(8,128)(2,1)S(1)} %get-tuple-element.157), channel_id=1, source_target_pairs={{0,1},{1,2},{2,3},{3,0},{4,5},{5,6},{6,7},{7,4},{8,9},{9,10},{10,1... | collective-permute-start | bytes 331784 | tf_op jit(solution)/shard_map/ppermute | solution.py:397
  166.1 9.5 %collective-permute-start.23 = (bf16[48,1152]{1,0:T(8,128)(2,1)S(1)}, bf16[48,1152]{1,0:T(8,128)(2,1)S(1)}, u32[]{:S(2)}, u32[]{:S(2)}) collective-permute-start(bf16[48,1152]{1,0:T(8,128)(2,1)S(1)} %get-tuple-element.157), channel_id=1, source_target_pairs={{0,3},{1,0},{2,1},{3,2},{4,7},{5,4},{6,5},{7,6},{8,11},{9,8},{10,9... | collective-permute-start | bytes 331784 | tf_op jit(solution)/shard_map/ppermute | solution.py:397
  167.3 12.3 %copy-start.12 = (bf16[2,2,64,384]{3,2,1,0:T(8,128)(2,1)S(1)}, bf16[2,2,64,384]{3,2,1,0:T(8,128)(2,1)}, u32[]{:S(2)}) copy-start(bf16[2,2,64,384]{3,2,1,0:T(8,128)(2,1)} %copy-done.11) | copy-start | bytes 589828
  167.4 9.9 %collective-permute-start.30 = (bf16[64,3840]{1,0:T(8,128)(2,1)S(1)}, bf16[64,3840]{1,0:T(8,128)(2,1)S(1)}, u32[]{:S(2)}, u32[]{:S(2)}) collective-permute-start(bf16[64,3840]{1,0:T(8,128)(2,1)S(1)} %maximum_select_fusion.3), channel_id=1, source_target_pairs={{0,16},{4,12},{8,24},{12,4},{16,0},{20,28},{24,8},{28,20},{1,17},{... | collective-permute-start | bytes 1474568 | tf_op jit(solution)/shard_map/ppermute | solution.py:393
  175.6 13.1 %collective-permute-start.32 = (bf16[48,4608]{1,0:T(8,128)(2,1)S(1)}, bf16[48,4608]{1,0:T(8,128)(2,1)S(1)}, u32[]{:S(2)}, u32[]{:S(2)}) collective-permute-start(bf16[48,4608]{1,0:T(8,128)(2,1)S(1)} %constant_dynamic-update-slice_fusion), channel_id=1, source_target_pairs={{0,16},{4,12},{8,24},{12,4},{16,0},{20,28},{24,8},{28,20},{1,17},{... | collective-permute-start | bytes 1327112 | tf_op jit(solution)/shard_map/ppermute | solution.py:393
  177.4 15.4 %collective-permute-start.31 = (bf16[128,3840]{1,0:T(8,128)(2,1)S(1)}, bf16[128,3840]{1,0:T(8,128)(2,1)S(1)}, u32[]{:S(2)}, u32[]{:S(2)}) collective-permute-start(bf16[128,3840]{1,0:T(8,128)(2,1)S(1)} %maximum_select_fusion.1), channel_id=1, source_target_pairs={{0,8},{4,20},{8,0},{12,28},{16,24},{20,4},{24,16},{28,12},{1,9},{5... | collective-permute-start | bytes 2949128 | tf_op jit(solution)/shard_map/ppermute | solution.py:393
  180.3 16.5 %collective-permute-start.24 = (bf16[2,3,64,384]{3,2,1,0:T(8,128)(2,1)S(1)}, bf16[2,3,64,384]{3,2,1,0:T(8,128)(2,1)S(1)}, u32[]{:S(2)}, u32[]{:S(2)}) collective-permute-start(bf16[2,3,64,384]{3,2,1,0:T(8,128)(2,1)S(1)} %get-tuple-element.128), channel_id=1, source_target_pairs={{0,2},{1,3},{2,0},{3,1},{4,6},{5,7},{6,4},{7,5},{8,10},{9,11},{10,... | collective-permute-start | bytes 884744 | tf_op jit(solution)/shard_map/ppermute | solution.py:397
  181.6 15.1 %collective-permute-start.25 = (bf16[2,3,64,384]{3,2,1,0:T(8,128)(2,1)S(1)}, bf16[2,3,64,384]{3,2,1,0:T(8,128)(2,1)S(1)}, u32[]{:S(2)}, u32[]{:S(2)}) collective-permute-start(bf16[2,3,64,384]{3,2,1,0:T(8,128)(2,1)S(1)} %get-tuple-element.130), channel_id=1, source_target_pairs={{0,3},{1,0},{2,1},{3,2},{4,7},{5,4},{6,5},{7,6},{8,11},{9,8},{10,9... | collective-permute-start | bytes 884744 | tf_op jit(solution)/shard_map/ppermute | solution.py:397
  196.8 13.0 %collective-permute-start.33 = (bf16[96,4608]{1,0:T(8,128)(2,1)S(1)}, bf16[96,4608]{1,0:T(8,128)(2,1)S(1)}, u32[]{:S(2)}, u32[]{:S(2)}) collective-permute-start(bf16[96,4608]{1,0:T(8,128)(2,1)S(1)} %maximum_select_fusion.2), channel_id=1, source_target_pairs={{0,8},{4,20},{8,0},{12,28},{16,24},{20,4},{24,16},{28,12},{1,9},{5... | collective-permute-start | bytes 2654216 | tf_op jit(solution)/shard_map/ppermute | solution.py:393
  198.7 12.3 %collective-permute-start.26 = (bf16[2,3,64,384]{3,2,1,0:T(8,128)(2,1)S(1)}, bf16[2,3,64,384]{3,2,1,0:T(8,128)(2,1)S(1)}, u32[]{:S(2)}, u32[]{:S(2)}) collective-permute-start(bf16[2,3,64,384]{3,2,1,0:T(8,128)(2,1)S(1)} %get-tuple-element.132), channel_id=1, source_target_pairs={{0,1},{1,2},{2,3},{3,0},{4,5},{5,6},{6,7},{7,4},{8,9},{9,10},{10,1... | collective-permute-start | bytes 884744 | tf_op jit(solution)/shard_map/ppermute | solution.py:397
  211.0 8.4 %collective-permute-start.34 = (bf16[192,4608]{1,0:T(8,128)(2,1)S(1)}, bf16[192,4608]{1,0:T(8,128)(2,1)}, u32[]{:S(2)}, u32[]{:S(2)}) collective-permute-start(bf16[192,4608]{1,0:T(8,128)(2,1)S(1)} %maximum_select_fusion.mine_ref), channel_id=1, source_target_pairs={{0,4},{4,0},{8,12},{12,8},{16,20},{20,16},{24,28},{28,24},{1,5},{5... | collective-permute-start | bytes 5308424 | tf_op jit(solution)/shard_map/ppermute | solution.py:393
  (22 other events, 99.2 us)

commit v4 on v3

--- a/solution.py
+++ b/solution.py
@@ -607,7 +607,7 @@
     after = {}
     if len(chunks) > 1:
         middle = [ahead[0] if k == 2 else back(held[-2], k, early) for k in range(len(shifts))]
-        after = {1: middle[3], len(stages): middle[1]}
+        after = {len(stages): (middle[1], middle[3])}
         for k, buffer in enumerate(middle):
             put(buffer, k, len(chunks) - 2)
     part, given = scatter_grp(keep, send, index, stages, after)
@@ -622,7 +622,7 @@
         1,
     )
     small = tied(small, given[1])
-    given = iter(given[-1:] * (len(stages) - 1) + [part])
+    given = iter([given[-2]] + given[-1:] * (len(stages) - 2) + [part])
     for k in range(seq.bit_length() - 1):
         small = join_seq(small, place, 1 << k, seq)
     for step in group_steps(index, group):

time: 227 us -> 220 us (0.969)
  waiting for transfers between devices: 56.7 us -> 46.9 us
  starting transfers between devices: 53.8 us -> 60.1 us
  other arithmetic: 15.5 us -> 12.7 us
    ppermute x9, waiting for transfers between devices: 28.2 us -> 19.9 us  [swap(): lax.ppermute(array, 'grp', [(i, i ^ bit) for i, bit in enumerate(stage)])]
    ppermute x2, starting transfers between devices: 0.17 us -> 4.29 us  [join_seq(): got = lax.ppermute(array, 'seq', [(i, i ^ bit) for i in range(seq)])]
    ppermute x24, starting transfers between devices: 45.1 us -> 48.6 us  [seq_shift(): lax.ppermute(array, 'seq', [(i, (i + shift) % size) for i in range(size)])]
    ppermute x24, waiting for transfers between devices: 28.4 us -> 25.3 us  [seq_shift(): lax.ppermute(array, 'seq', [(i, (i + shift) % size) for i in range(size)])]
  transfers between devices with their start and end apart: 35 -> 35, of which waited for: 17 -> 18; matrix products, arithmetic and copies ran while one was open for 13% -> 11% of each run, Pallas kernels for 32% -> 33%
where the time goes in v4:
time: 220 us; the launch traced here: 218 us
  Pallas kernels  77.4 us (35%)
  starting transfers between devices  60.1 us (27%)
  waiting for transfers between devices  46.9 us (21%)
  local copies, waits for them, and re-layouts  17.3 us (8%)
  other arithmetic  12.7 us (6%)
  between operations  2.79 us (1%)
    pallas_call x3, Pallas kernels, layer_call(): pl.pallas_call(functools.partial(layer_kernel, parts, first, last, buffer...  66.9 us
    ppermute x24, starting transfers between devices, seq_shift(): lax.ppermute(array, 'seq', [(i, (i + shift) % size) for i in range(size)])  48.6 us
    ppermute x24, waiting for transfers between devices, seq_shift(): lax.ppermute(array, 'seq', [(i, (i + shift) % size) for i in range(size)])  25.3 us
    ppermute x9, waiting for transfers between devices, swap(): lax.ppermute(array, 'grp', [(i, i ^ bit) for i, bit in enumerate(stage)])  19.9 us
    dynamic_update_slice x12, local copies, waits for them, and re-layouts, put(): lax.dynamic_update_slice_in_dim(targets[which], buffer[which], (place + s...  8.19 us
    ppermute x9, starting transfers between devices, swap(): lax.ppermute(array, 'grp', [(i, i ^ bit) for i, bit in enumerate(stage)])  7.2 us
    pallas_call x1, Pallas kernels, ada_call(): pl.pallas_call(ada_kernel, in_specs=[full] * 2, out_specs=[full] * 5, out...  5.72 us
    another operation x12, other arithmetic, pieces(): jnp.stack([cut(array, (place + shift) % seq * own + starts[chunk], chunks...  5.28 us
  transfers between devices with their start and end apart: 35, of which 18 were waited for; matrix products, arithmetic and copies ran while one was open for 11% of the time, Pallas kernels for 33%

profile of v4, /device:TPU:0, one launch (start us, length us, event | category | flops | bytes accessed | tf_op | source)
XLA Modules:
  0.0 217.9 jit_solution(14124342898708703085)
XLA Ops:
  0.8 1.4 dynamic-slice_bitcast_fusion.16
  2.9 4.1 %collective-permute-start = (bf16[2,2,64,384]{3,2,1,0:T(8,128)(2,1)}, bf16[2,2,64,384]{3,2,1,0:T(8,128)(2,1)S(1)}, u32[]{:S(2)}, u32[]{:S(2)}) collective-permute-start(bf16[2,2,64,384]{3,2,1,0:T(8,128)(2,1)} %pad_maximum_fusion.10), channel_id=1, source_target_pairs={{0,2},{1,3},{2,0},{3,1},{4,6},{5,7},{6,4},{7,5},{8,10},{9,11},{10,... | collective-permute-start | bytes 589832 | tf_op jit(solution)/shard_map/ppermute | solution.py:397
  7.7 1.6 collective-permute-start.1
  10.0 2.2 %collective-permute-start.2 = (bf16[2,2,64,384]{3,2,1,0:T(8,128)(2,1)}, bf16[2,2,64,384]{3,2,1,0:T(8,128)(2,1)S(1)}, u32[]{:S(2)}, u32[]{:S(2)}) collective-permute-start(bf16[2,2,64,384]{3,2,1,0:T(8,128)(2,1)} %pad_maximum_fusion.12), channel_id=1, source_target_pairs={{0,3},{1,0},{2,1},{3,2},{4,7},{5,4},{6,5},{7,6},{8,11},{9,8},{10,9... | collective-permute-start | bytes 589832 | tf_op jit(solution)/shard_map/ppermute | solution.py:397
  14.1 2.0 dynamic-slice_bitcast_fusion
  19.5 1.9 collective-permute-done.refs_3_
  21.4 2.1 collective-permute-done.2.refs_5_
  23.5 3.9 %collective-permute-start.3 = (bf16[2,3,64,384]{3,2,1,0:T(8,128)(2,1)}, bf16[2,3,64,384]{3,2,1,0:T(8,128)(2,1)S(1)}, u32[]{:S(2)}, u32[]{:S(2)}) collective-permute-start(bf16[2,3,64,384]{3,2,1,0:T(8,128)(2,1)} %pad_maximum_fusion.2), channel_id=1, source_target_pairs={{0,2},{1,3},{2,0},{3,1},{4,6},{5,7},{6,4},{7,5},{8,10},{9,11},{10,... | collective-permute-start | bytes 884744 | tf_op jit(solution)/shard_map/ppermute | solution.py:397
  27.4 3.8 %collective-permute-start.5 = (bf16[2,3,64,384]{3,2,1,0:T(8,128)(2,1)S(1)}, bf16[2,3,64,384]{3,2,1,0:T(8,128)(2,1)S(1)}, u32[]{:S(2)}, u32[]{:S(2)}) collective-permute-start(bf16[2,3,64,384]{3,2,1,0:T(8,128)(2,1)S(1)} %copy-done.6), channel_id=1, source_target_pairs={{0,3},{1,0},{2,1},{3,2},{4,7},{5,4},{6,5},{7,6},{8,11},{9,8},{10,9... | collective-permute-start | bytes 884744 | tf_op jit(solution)/shard_map/ppermute | solution.py:397
  31.2 16.6 %shard_map.317 = (bf16[2,2,64,384]{3,2,1,0:T(8,128)(2,1)S(1)}, bf16[2,2,64,384]{3,2,1,0:T(8,128)(2,1)S(1)}, bf16[2,2,64,384]{3,2,1,0:T(8,128)(2,1)S(1)}, bf16[2,...) custom-call(s32[1]{0:T(128)} %bitcast.refs_0_.bit_ref, ...), custom_call_target="tpu_custom_call" | custom-call | flops 60000002048 | bytes 1572864 | tf_op jit(solution)/shard_map/pallas_call | solution.py:291
  48.3 5.2 %collective-permute-start.6 = (bf16[2,3,64,384]{3,2,1,0:T(8,128)(2,1)S(1)}, bf16[2,3,64,384]{3,2,1,0:T(8,128)(2,1)S(1)}, u32[]{:S(2)}, u32[]{:S(2)}) collective-permute-start(bf16[2,3,64,384]{3,2,1,0:T(8,128)(2,1)S(1)} %copy-done.5), channel_id=1, source_target_pairs={{0,2},{1,3},{2,0},{3,1},{4,6},{5,7},{6,4},{7,5},{8,10},{9,11},{10,... | collective-permute-start | bytes 884744 | tf_op jit(solution)/shard_map/ppermute | solution.py:397
  53.5 0.9 collective-permute-start.7
  54.4 2.9 %collective-permute-start.8 = (bf16[2,3,64,384]{3,2,1,0:T(8,128)(2,1)S(1)}, bf16[2,3,64,384]{3,2,1,0:T(8,128)(2,1)S(1)}, u32[]{:S(2)}, u32[]{:S(2)}) collective-permute-start(bf16[2,3,64,384]{3,2,1,0:T(8,128)(2,1)S(1)} %pad_maximum_fusion.8), channel_id=1, source_target_pairs={{0,3},{1,0},{2,1},{3,2},{4,7},{5,4},{6,5},{7,6},{8,11},{9,8},{10,9... | collective-permute-start | bytes 884744 | tf_op jit(solution)/shard_map/ppermute | solution.py:397
  57.3 24.4 %shard_map.318 = (bf16[2,3,64,384]{3,2,1,0:T(8,128)(2,1)S(1)}, bf16[2,3,64,384]{3,2,1,0:T(8,128)(2,1)S(1)}, bf16[2,3,64,384]{3,2,1,0:T(8,128)(2,1)S(1)}, bf16[2,...) custom-call(s32[1]{0:T(128)} %bitcast.refs_0_.bit_ref, ...), custom_call_target="tpu_custom_call", output_to_operand_aliasing={{6}: (15, {})} | custom-call | flops 89999998976 | bytes 2359296 | tf_op jit(solution)/shard_map/pallas_call | solution.py:291
  81.9 1.5 collective-permute-start.10
  84.0 3.2 %collective-permute-start.13 = (bf16[2,3,64,384]{3,2,1,0:T(8,128)(2,1)S(1)}, bf16[2,3,64,384]{3,2,1,0:T(8,128)(2,1)S(1)}, u32[]{:S(2)}, u32[]{:S(2)}) collective-permute-start(bf16[2,3,64,384]{3,2,1,0:T(8,128)(2,1)S(1)} %get-tuple-element.117), channel_id=1, source_target_pairs={{0,3},{1,0},{2,1},{3,2},{4,7},{5,4},{6,5},{7,6},{8,11},{9,8},{10,9... | collective-permute-start | bytes 884744 | tf_op jit(solution)/shard_map/ppermute | solution.py:397
  87.2 25.8 %shard_map.319 = (bf16[2,3,64,384]{3,2,1,0:T(8,128)(2,1)S(1)}, bf16[2,3,64,384]{3,2,1,0:T(8,128)(2,1)S(1)}, bf16[2,3,64,384]{3,2,1,0:T(8,128)(2,1)S(1)}, bf16[2,...) custom-call(s32[1]{0:T(128)} %bitcast.refs_0_.bit_ref, ...), custom_call_target="tpu_custom_call" | custom-call | flops 89999998976 | bytes 2359296 | tf_op jit(solution)/shard_map/pallas_call | solution.py:291
  116.6 1.2 collective-permute-done.15
  117.8 2.5 %add_convert_fusion.1 = (bf16[96,4608]{1,0:T(8,128)(2,1)S(1)}, bf16[96,4608]{1,0:T(8,128)(2,1)S(1)}) fusion(bf16[192,4608]{1,0:T(8,128)(2,1)} %collective-permute-done.15, s32[]{:T(128)S(6)} %select_n.376, bf16[192,4608]{1,0:T(8,128)(2,1)} %get-tuple-element.122, s32[]{:T(128)S(6)} %select_n.379), kind=kLoop, calls=%fused_computation.4 | loop fusion | flops 3538944 | bytes 5308424 | tf_op jit(solution)/shard_map/convert_element_type | solution.py:411
  120.3 1.6 collective-permute-start.16
  122.8 1.5 collective-permute-start.14
  124.9 1.9 collective-permute-start.27
  126.8 6.6 %collective-permute-done.16 = bf16[96,4608]{1,0:T(8,128)(2,1)S(1)} collective-permute-done((bf16[96,4608]{1,0:T(8,128)(2,1)S(1)}, bf16[96,4608]{1,0:T(8,128)(2,1)S(1)}, u32[]{:S(2)}, u32[]{:S(2)}) %collective-permute-start.16) | collective-permute-done | bytes 884768 | tf_op jit(solution)/shard_map/ppermute | solution.py:393
  133.5 1.6 collective-permute-start.17
  135.2 1.8 collective-permute-done.27
  137.0 2.4 %collective-permute-start.28 = (bf16[16,3840]{1,0:T(8,128)(2,1)S(1)}, bf16[16,3840]{1,0:T(8,128)(2,1)S(1)}, u32[]{:S(2)}, u32[]{:S(2)}) collective-permute-start(bf16[16,3840]{1,0:T(8,128)(2,1)S(1)} %maximum_select_fusion.5), channel_id=1, source_target_pairs={{0,2},{1,3},{2,0},{3,1},{4,6},{5,7},{6,4},{7,5},{8,10},{9,11},{10,... | collective-permute-start | bytes 368648 | tf_op jit(solution)/shard_map/ppermute | solution.py:445
  139.4 2.5 %collective-permute-done.17 = bf16[48,4608]{1,0:T(8,128)(2,1)S(1)} collective-permute-done((bf16[48,4608]{1,0:T(8,128)(2,1)S(1)}, bf16[48,4608]{1,0:T(8,128)(2,1)S(1)}, u32[]{:S(2)}, u32[]{:S(2)}) %collective-permute-start.17) | collective-permute-done | bytes 442400 | tf_op jit(solution)/shard_map/ppermute | solution.py:393
  142.1 4.0 %collective-permute-done.12 = bf16[2,3,64,384]{3,2,1,0:T(8,128)(2,1)S(1)} collective-permute-done((bf16[2,3,64,384]{3,2,1,0:T(8,128)(2,1)S(1)}, bf16[2,3,64,384]{3,2,1,0:T(8,128)(2,1)S(1)}, u32[]{:S(2)}, u32[]{:S(2)}) %collective-permute-start.12) | collective-permute-done | bytes 294944 | tf_op jit(solution)/shard_map/ppermute | solution.py:397
  146.2 2.0 collective-permute-start.19
  148.2 1.9 collective-permute-start.18
  150.3 0.8 collective-permute-done.20
  151.1 4.6 %collective-permute-done.19 = bf16[48,1152]{1,0:T(8,128)(2,1)S(1)} collective-permute-done((bf16[48,1152]{1,0:T(8,128)(2,1)S(1)}, bf16[48,1152]{1,0:T(8,128)(2,1)S(1)}, u32[]{:S(2)}, u32[]{:S(2)}) %collective-permute-start.19) | collective-permute-done | bytes 110624 | tf_op jit(solution)/shard_map/ppermute | solution.py:397
  155.7 2.4 %collective-permute-done.18 = bf16[48,1152]{1,0:T(8,128)(2,1)S(1)} collective-permute-done((bf16[48,1152]{1,0:T(8,128)(2,1)S(1)}, bf16[48,1152]{1,0:T(8,128)(2,1)S(1)}, u32[]{:S(2)}, u32[]{:S(2)}) %collective-permute-start.18) | collective-permute-done | bytes 110624 | tf_op jit(solution)/shard_map/ppermute | solution.py:397
  158.3 3.2 %collective-permute-start.22 = (bf16[48,1152]{1,0:T(8,128)(2,1)S(1)}, bf16[48,1152]{1,0:T(8,128)(2,1)S(1)}, u32[]{:S(2)}, u32[]{:S(2)}) collective-permute-start(bf16[48,1152]{1,0:T(8,128)(2,1)S(1)} %get-tuple-element.155), channel_id=1, source_target_pairs={{0,1},{1,2},{2,3},{3,0},{4,5},{5,6},{6,7},{7,4},{8,9},{9,10},{10,1... | collective-permute-start | bytes 331784 | tf_op jit(solution)/shard_map/ppermute | solution.py:397
  163.0 6.0 %collective-permute-done.21 = bf16[48,1152]{1,0:T(8,128)(2,1)S(1)} collective-permute-done((bf16[48,1152]{1,0:T(8,128)(2,1)S(1)}, bf16[48,1152]{1,0:T(8,128)(2,1)S(1)}, u32[]{:S(2)}, u32[]{:S(2)}) %collective-permute-start.21) | collective-permute-done | bytes 110624 | tf_op jit(solution)/shard_map/ppermute | solution.py:397
  169.0 0.9 collective-permute-done.23
  171.4 1.6 collective-permute-start.31
  174.3 1.1 collective-permute-start.24
  175.4 2.6 %collective-permute-start.25 = (bf16[2,3,64,384]{3,2,1,0:T(8,128)(2,1)S(1)}, bf16[2,3,64,384]{3,2,1,0:T(8,128)(2,1)S(1)}, u32[]{:S(2)}, u32[]{:S(2)}) collective-permute-start(bf16[2,3,64,384]{3,2,1,0:T(8,128)(2,1)S(1)} %get-tuple-element.128), channel_id=1, source_target_pairs={{0,3},{1,0},{2,1},{3,2},{4,7},{5,4},{6,5},{7,6},{8,11},{9,8},{10,9... | collective-permute-start | bytes 884744 | tf_op jit(solution)/shard_map/ppermute | solution.py:397
  178.0 5.0 %collective-permute-done.32 = bf16[48,4608]{1,0:T(8,128)(2,1)S(1)} collective-permute-done((bf16[48,4608]{1,0:T(8,128)(2,1)S(1)}, bf16[48,4608]{1,0:T(8,128)(2,1)S(1)}, u32[]{:S(2)}, u32[]{:S(2)}) %collective-permute-start.32) | collective-permute-done | bytes 442400 | tf_op jit(solution)/shard_map/ppermute | solution.py:393
  183.2 3.9 %collective-permute-done.31 = bf16[128,3840]{1,0:T(8,128)(2,1)S(1)} collective-permute-done((bf16[128,3840]{1,0:T(8,128)(2,1)S(1)}, bf16[128,3840]{1,0:T(8,128)(2,1)S(1)}, u32[]{:S(2)}, u32[]{:S(2)}) %collective-permute-start.31) | collective-permute-done | bytes 983072 | tf_op jit(solution)/shard_map/ppermute | solution.py:393
  187.4 1.4 pad_maximum_fusion.small_ref
  189.4 1.0 collective-permute-start.33
  191.8 5.4 %collective-permute-start.26 = (bf16[2,3,64,384]{3,2,1,0:T(8,128)(2,1)S(1)}, bf16[2,3,64,384]{3,2,1,0:T(8,128)(2,1)S(1)}, u32[]{:S(2)}, u32[]{:S(2)}) collective-permute-start(bf16[2,3,64,384]{3,2,1,0:T(8,128)(2,1)S(1)} %get-tuple-element.130), channel_id=1, source_target_pairs={{0,1},{1,2},{2,3},{3,0},{4,5},{5,6},{6,7},{7,4},{8,9},{9,10},{10,1... | collective-permute-start | bytes 884744 | tf_op jit(solution)/shard_map/ppermute | solution.py:397
  197.3 5.7 %shard_map.320 = (f32[384,2304]{1,0:T(8,128)}, f32[1,2304]{1,0:T(1,128)S(1)}, f32[8,640]{1,0:T(8,128)S(1)}, f32[256,384]{1,0:T(8,128)S(1)}, f32[64,384]{1,0:T(8,128)}) custom-call(bf16[256,3840]{1,0:T(8,128)(2,1)} %pad_maximum_fusion.small_ref, bf16[384,2304]{1,0:T(8,128)(2,1)} %weight_ref.1), custom_call_target="tpu_custom_call" | custom-call | flops 6000000000 | bytes 8000000 | tf_op jit(solution)/shard_map/pallas_call | solution.py:364
  203.3 1.4 collective-permute-done.26
  208.9 1.1 copy-done.21
  213.1 4.8 %shard_map.321 = (f32[384,1536]{1,0:T(8,128)}, f32[1536,384]{1,0:T(8,128)}, f32[384,1152]{1,0:T(8,128)}, f32[384,384]{1,0:T(8,128)}) custom-call(s32[1]{0:T(128)} %bitcast.refs_0_.bit_ref, bf16[192,4608]{1,0:T(8,128)(2,1)S(1)} %maximum_select_fusion.mine_ref, bf16[192,4608]{1,0:T(8,128)(2,1)} %collective-permute-done.34.other_ref), custom_call_target="tpu_custom_call" | custom-call | tf_op jit(solution)/shard_map/pallas_call | solution.py:331
  (176 shorter events, 26.9 us)
Async XLA Ops:
  0.6 12.4 %copy-start = (f32[64,384]{1,0:T(8,128)S(1)}, f32[64,384]{1,0:T(8,128)}, u32[]{:S(2)}) copy-start(f32[64,384]{1,0:T(8,128)} %param.27) | copy-start | bytes 294916
  0.7 11.6 %copy-start.11 = (f32[16,2,384]{2,1,0:T(2,128)S(1)}, f32[16,2,384]{2,1,0:T(2,128)}, u32[]{:S(2)}) copy-start(f32[16,2,384]{2,1,0:T(2,128)} %param.24) | copy-start | bytes 147460
  0.7 11.6 %copy-start.18 = (s32[16,2]{0,1:T(2,128)S(1)}, s32[16,2]{0,1:T(2,128)}, u32[]{:S(2)}) copy-start(s32[16,2]{0,1:T(2,128)} %param.26) | copy-start | bytes 388
  0.7 12.5 %copy-start.3 = (bf16[384,2304]{1,0:T(8,128)(2,1)S(1)}, bf16[384,2304]{1,0:T(8,128)(2,1)}, u32[]{:S(2)}) copy-start(bf16[384,2304]{1,0:T(8,128)(2,1)} %weight_ref.1) | copy-start | bytes 5308420
  0.7 12.5 %copy-start.12 = (f32[2304]{0:T(1024)S(1)}, f32[2304]{0:T(1024)}, u32[]{:S(2)}) copy-start(f32[2304]{0:T(1024)} %param.29) | copy-start | bytes 27652
  2.9 18.5 %collective-permute-start = (bf16[2,2,64,384]{3,2,1,0:T(8,128)(2,1)}, bf16[2,2,64,384]{3,2,1,0:T(8,128)(2,1)S(1)}, u32[]{:S(2)}, u32[]{:S(2)}) collective-permute-start(bf16[2,2,64,384]{3,2,1,0:T(8,128)(2,1)} %pad_maximum_fusion.10), channel_id=1, source_target_pairs={{0,2},{1,3},{2,0},{3,1},{4,6},{5,7},{6,4},{7,5},{8,10},{9,11},{10,... | collective-permute-start | bytes 589832 | tf_op jit(solution)/shard_map/ppermute | solution.py:397
  7.7 13.7 %collective-permute-start.1 = (bf16[2,2,64,384]{3,2,1,0:T(8,128)(2,1)}, bf16[2,2,64,384]{3,2,1,0:T(8,128)(2,1)S(1)}, u32[]{:S(2)}, u32[]{:S(2)}) collective-permute-start(bf16[2,2,64,384]{3,2,1,0:T(8,128)(2,1)} %pad_maximum_fusion.11), channel_id=1, source_target_pairs={{0,1},{1,2},{2,3},{3,0},{4,5},{5,6},{6,7},{7,4},{8,9},{9,10},{10,1... | collective-permute-start | bytes 589832 | tf_op jit(solution)/shard_map/ppermute | solution.py:397
  10.0 13.6 %collective-permute-start.2 = (bf16[2,2,64,384]{3,2,1,0:T(8,128)(2,1)}, bf16[2,2,64,384]{3,2,1,0:T(8,128)(2,1)S(1)}, u32[]{:S(2)}, u32[]{:S(2)}) collective-permute-start(bf16[2,2,64,384]{3,2,1,0:T(8,128)(2,1)} %pad_maximum_fusion.12), channel_id=1, source_target_pairs={{0,3},{1,0},{2,1},{3,2},{4,7},{5,4},{6,5},{7,6},{8,11},{9,8},{10,9... | collective-permute-start | bytes 589832 | tf_op jit(solution)/shard_map/ppermute | solution.py:397
  18.4 12.8 %copy-start.2 = (bf16[384,384]{1,0:T(8,128)(2,1)S(1)}, bf16[384,384]{1,0:T(8,128)(2,1)}, u32[]{:S(2)}) copy-start(bf16[384,384]{1,0:T(8,128)(2,1)} %refs_8_.5) | copy-start | bytes 884740
  19.2 8.2 %copy-start.6 = (bf16[2,3,64,384]{3,2,1,0:T(8,128)(2,1)S(1)}, bf16[2,3,64,384]{3,2,1,0:T(8,128)(2,1)}, u32[]{:S(2)}) copy-start(bf16[2,3,64,384]{3,2,1,0:T(8,128)(2,1)} %pad_maximum_fusion.4) | copy-start | bytes 884740
  23.5 24.3 %collective-permute-start.3 = (bf16[2,3,64,384]{3,2,1,0:T(8,128)(2,1)}, bf16[2,3,64,384]{3,2,1,0:T(8,128)(2,1)S(1)}, u32[]{:S(2)}, u32[]{:S(2)}) collective-permute-start(bf16[2,3,64,384]{3,2,1,0:T(8,128)(2,1)} %pad_maximum_fusion.2), channel_id=1, source_target_pairs={{0,2},{1,3},{2,0},{3,1},{4,6},{5,7},{6,4},{7,5},{8,10},{9,11},{10,... | collective-permute-start | bytes 884744 | tf_op jit(solution)/shard_map/ppermute | solution.py:397
  27.4 20.5 %collective-permute-start.4 = (bf16[2,3,64,384]{3,2,1,0:T(8,128)(2,1)}, bf16[2,3,64,384]{3,2,1,0:T(8,128)(2,1)S(1)}, u32[]{:S(2)}, u32[]{:S(2)}) collective-permute-start(bf16[2,3,64,384]{3,2,1,0:T(8,128)(2,1)} %pad_maximum_fusion.3), channel_id=1, source_target_pairs={{0,1},{1,2},{2,3},{3,0},{4,5},{5,6},{6,7},{7,4},{8,9},{9,10},{10,1... | collective-permute-start | bytes 884744 | tf_op jit(solution)/shard_map/ppermute | solution.py:397
  27.4 20.9 %collective-permute-start.5 = (bf16[2,3,64,384]{3,2,1,0:T(8,128)(2,1)S(1)}, bf16[2,3,64,384]{3,2,1,0:T(8,128)(2,1)S(1)}, u32[]{:S(2)}, u32[]{:S(2)}) collective-permute-start(bf16[2,3,64,384]{3,2,1,0:T(8,128)(2,1)S(1)} %copy-done.6), channel_id=1, source_target_pairs={{0,3},{1,0},{2,1},{3,2},{4,7},{5,4},{6,5},{7,6},{8,11},{9,8},{10,9... | collective-permute-start | bytes 884744 | tf_op jit(solution)/shard_map/ppermute | solution.py:397
  31.2 17.1 %copy-start.5 = (bf16[2,3,64,384]{3,2,1,0:T(8,128)(2,1)S(1)}, bf16[2,3,64,384]{3,2,1,0:T(8,128)(2,1)}, u32[]{:S(2)}) copy-start(bf16[2,3,64,384]{3,2,1,0:T(8,128)(2,1)} %pad_maximum_fusion.6) | copy-start | bytes 884740
  47.9 9.4 %copy-start.24 = (bf16[2,3,64,384]{3,2,1,0:T(8,128)(2,1)}, bf16[2,3,64,384]{3,2,1,0:T(8,128)(2,1)S(1)}, u32[]{:S(2)}) copy-start(bf16[2,3,64,384]{3,2,1,0:T(8,128)(2,1)S(1)} %collective-permute-done.4.refs_4_) | copy-start | bytes 884740
  48.3 9.0 %copy-start.25 = (bf16[2,3,64,384]{3,2,1,0:T(8,128)(2,1)}, bf16[2,3,64,384]{3,2,1,0:T(8,128)(2,1)S(1)}, u32[]{:S(2)}) copy-start(bf16[2,3,64,384]{3,2,1,0:T(8,128)(2,1)S(1)} %collective-permute-done.5.refs_5_) | copy-start | bytes 884740
  48.3 33.5 %collective-permute-start.6 = (bf16[2,3,64,384]{3,2,1,0:T(8,128)(2,1)S(1)}, bf16[2,3,64,384]{3,2,1,0:T(8,128)(2,1)S(1)}, u32[]{:S(2)}, u32[]{:S(2)}) collective-permute-start(bf16[2,3,64,384]{3,2,1,0:T(8,128)(2,1)S(1)} %copy-done.5), channel_id=1, source_target_pairs={{0,2},{1,3},{2,0},{3,1},{4,6},{5,7},{6,4},{7,5},{8,10},{9,11},{10,... | collective-permute-start | bytes 884744 | tf_op jit(solution)/shard_map/ppermute | solution.py:397
  53.5 28.3 %collective-permute-start.7 = (bf16[2,3,64,384]{3,2,1,0:T(8,128)(2,1)S(1)}, bf16[2,3,64,384]{3,2,1,0:T(8,128)(2,1)S(1)}, u32[]{:S(2)}, u32[]{:S(2)}) collective-permute-start(bf16[2,3,64,384]{3,2,1,0:T(8,128)(2,1)S(1)} %pad_maximum_fusion.7), channel_id=1, source_target_pairs={{0,1},{1,2},{2,3},{3,0},{4,5},{5,6},{6,7},{7,4},{8,9},{9,10},{10,1... | collective-permute-start | bytes 884744 | tf_op jit(solution)/shard_map/ppermute | solution.py:397
  54.4 27.4 %collective-permute-start.8 = (bf16[2,3,64,384]{3,2,1,0:T(8,128)(2,1)S(1)}, bf16[2,3,64,384]{3,2,1,0:T(8,128)(2,1)S(1)}, u32[]{:S(2)}, u32[]{:S(2)}) collective-permute-start(bf16[2,3,64,384]{3,2,1,0:T(8,128)(2,1)S(1)} %pad_maximum_fusion.8), channel_id=1, source_target_pairs={{0,3},{1,0},{2,1},{3,2},{4,7},{5,4},{6,5},{7,6},{8,11},{9,8},{10,9... | collective-permute-start | bytes 884744 | tf_op jit(solution)/shard_map/ppermute | solution.py:397
  81.8 31.2 %collective-permute-start.9 = (bf16[2,2,64,384]{3,2,1,0:T(8,128)(2,1)S(1)}, bf16[2,2,64,384]{3,2,1,0:T(8,128)(2,1)S(1)}, u32[]{:S(2)}, u32[]{:S(2)}) collective-permute-start(bf16[2,2,64,384]{3,2,1,0:T(8,128)(2,1)S(1)} %get-tuple-element.108), channel_id=1, source_target_pairs={{0,2},{1,3},{2,0},{3,1},{4,6},{5,7},{6,4},{7,5},{8,10},{9,11},{10,... | collective-permute-start | bytes 589832 | tf_op jit(solution)/shard_map/ppermute | solution.py:397
  81.9 31.2 %collective-permute-start.10 = (bf16[2,2,64,384]{3,2,1,0:T(8,128)(2,1)S(1)}, bf16[2,2,64,384]{3,2,1,0:T(8,128)(2,1)S(1)}, u32[]{:S(2)}, u32[]{:S(2)}) collective-permute-start(bf16[2,2,64,384]{3,2,1,0:T(8,128)(2,1)S(1)} %get-tuple-element.110), channel_id=1, source_target_pairs={{0,3},{1,0},{2,1},{3,2},{4,7},{5,4},{6,5},{7,6},{8,11},{9,8},{10,9... | collective-permute-start | bytes 589832 | tf_op jit(solution)/shard_map/ppermute | solution.py:397
  83.4 29.7 %collective-permute-start.11 = (bf16[2,2,64,384]{3,2,1,0:T(8,128)(2,1)S(1)}, bf16[2,2,64,384]{3,2,1,0:T(8,128)(2,1)S(1)}, u32[]{:S(2)}, u32[]{:S(2)}) collective-permute-start(bf16[2,2,64,384]{3,2,1,0:T(8,128)(2,1)S(1)} %get-tuple-element.112), channel_id=1, source_target_pairs={{0,1},{1,2},{2,3},{3,0},{4,5},{5,6},{6,7},{7,4},{8,9},{9,10},{10,1... | collective-permute-start | bytes 589832 | tf_op jit(solution)/shard_map/ppermute | solution.py:397
  84.0 29.1 %collective-permute-start.13 = (bf16[2,3,64,384]{3,2,1,0:T(8,128)(2,1)S(1)}, bf16[2,3,64,384]{3,2,1,0:T(8,128)(2,1)S(1)}, u32[]{:S(2)}, u32[]{:S(2)}) collective-permute-start(bf16[2,3,64,384]{3,2,1,0:T(8,128)(2,1)S(1)} %get-tuple-element.117), channel_id=1, source_target_pairs={{0,3},{1,0},{2,1},{3,2},{4,7},{5,4},{6,5},{7,6},{8,11},{9,8},{10,9... | collective-permute-start | bytes 884744 | tf_op jit(solution)/shard_map/ppermute | solution.py:397
  87.2 26.6 %copy-start.27 = (s32[8]{0:T(128)S(1)}, s32[8]{0:T(128)}, u32[]{:S(2)}) copy-start(s32[8]{0:T(128)} %constant.206.clone) | copy-start | bytes 100
  87.2 27.8 %copy-start.26 = (s32[8]{0:T(128)S(1)}, s32[8]{0:T(128)}, u32[]{:S(2)}) copy-start(s32[8]{0:T(128)} %constant.207.clone) | copy-start | bytes 100
  87.2 29.4 %copy-start.8 = (f32[8,384]{1,0:T(8,128)S(1)}, f32[8,384]{1,0:T(8,128)}, u32[]{:S(2)}) copy-start(f32[8,384]{1,0:T(8,128)} %copy-done.7) | copy-start | bytes 36868
  113.8 4.0 %collective-permute-start.15 = (bf16[192,4608]{1,0:T(8,128)(2,1)}, bf16[192,4608]{1,0:T(8,128)(2,1)}, u32[]{:S(2)}, u32[]{:S(2)}) collective-permute-start(bf16[192,4608]{1,0:T(8,128)(2,1)} %get-tuple-element.124), channel_id=1, source_target_pairs={{0,4},{4,0},{8,12},{12,8},{16,20},{20,16},{24,28},{28,24},{1,5},{5... | collective-permute-start | bytes 5308424 | tf_op jit(solution)/shard_map/ppermute | solution.py:393
  120.3 13.1 %collective-permute-start.16 = (bf16[96,4608]{1,0:T(8,128)(2,1)S(1)}, bf16[96,4608]{1,0:T(8,128)(2,1)S(1)}, u32[]{:S(2)}, u32[]{:S(2)}) collective-permute-start(bf16[96,4608]{1,0:T(8,128)(2,1)S(1)} %get-tuple-element.157), channel_id=1, source_target_pairs={{0,8},{4,20},{8,0},{12,28},{16,24},{20,4},{24,16},{28,12},{1,9},{5... | collective-permute-start | bytes 2654216 | tf_op jit(solution)/shard_map/ppermute | solution.py:393
  122.6 23.5 %collective-permute-start.12 = (bf16[2,3,64,384]{3,2,1,0:T(8,128)(2,1)S(1)}, bf16[2,3,64,384]{3,2,1,0:T(8,128)(2,1)S(1)}, u32[]{:S(2)}, u32[]{:S(2)}) collective-permute-start(bf16[2,3,64,384]{3,2,1,0:T(8,128)(2,1)S(1)} %get-tuple-element.115), channel_id=1, source_target_pairs={{0,2},{1,3},{2,0},{3,1},{4,6},{5,7},{6,4},{7,5},{8,10},{9,11},{10,... | collective-permute-start | bytes 884744 | tf_op jit(solution)/shard_map/ppermute | solution.py:397
  122.8 23.3 %collective-permute-start.14 = (bf16[2,3,64,384]{3,2,1,0:T(8,128)(2,1)S(1)}, bf16[2,3,64,384]{3,2,1,0:T(8,128)(2,1)S(1)}, u32[]{:S(2)}, u32[]{:S(2)}) collective-permute-start(bf16[2,3,64,384]{3,2,1,0:T(8,128)(2,1)S(1)} %get-tuple-element.119), channel_id=1, source_target_pairs={{0,1},{1,2},{2,3},{3,0},{4,5},{5,6},{6,7},{7,4},{8,9},{9,10},{10,1... | collective-permute-start | bytes 884744 | tf_op jit(solution)/shard_map/ppermute | solution.py:397
  124.9 12.0 %collective-permute-start.27 = (bf16[8,3840]{1,0:T(8,128)(2,1)S(1)}, bf16[8,3840]{1,0:T(8,128)(2,1)S(1)}, u32[]{:S(2)}, u32[]{:S(2)}) collective-permute-start(bf16[8,3840]{1,0:T(8,128)(2,1)S(1)} %constant_dynamic-update-slice_fusion.4), channel_id=1, source_target_pairs={{0,1},{1,0},{2,3},{3,2},{4,5},{5,4},{6,7},{7,6},{8,9},{9,8},{10,11... | collective-permute-start | bytes 184328 | tf_op jit(solution)/shard_map/ppermute | solution.py:445
  133.5 8.4 %collective-permute-start.17 = (bf16[48,4608]{1,0:T(8,128)(2,1)S(1)}, bf16[48,4608]{1,0:T(8,128)(2,1)S(1)}, u32[]{:S(2)}, u32[]{:S(2)}) collective-permute-start(bf16[48,4608]{1,0:T(8,128)(2,1)S(1)} %add_convert_fusion.3), channel_id=1, source_target_pairs={{0,16},{4,12},{8,24},{12,4},{16,0},{20,28},{24,8},{28,20},{1,17},{... | collective-permute-start | bytes 1327112 | tf_op jit(solution)/shard_map/ppermute | solution.py:393
  137.0 13.2 %collective-permute-start.28 = (bf16[16,3840]{1,0:T(8,128)(2,1)S(1)}, bf16[16,3840]{1,0:T(8,128)(2,1)S(1)}, u32[]{:S(2)}, u32[]{:S(2)}) collective-permute-start(bf16[16,3840]{1,0:T(8,128)(2,1)S(1)} %maximum_select_fusion.5), channel_id=1, source_target_pairs={{0,2},{1,3},{2,0},{3,1},{4,6},{5,7},{6,4},{7,5},{8,10},{9,11},{10,... | collective-permute-start | bytes 368648 | tf_op jit(solution)/shard_map/ppermute | solution.py:445
  146.2 5.0 %collective-permute-start.20 = (bf16[48,1152]{1,0:T(8,128)(2,1)S(1)}, bf16[48,1152]{1,0:T(8,128)(2,1)S(1)}, u32[]{:S(2)}, u32[]{:S(2)}) collective-permute-start(bf16[48,1152]{1,0:T(8,128)(2,1)S(1)} %get-tuple-element.189), channel_id=1, source_target_pairs={{0,3},{1,0},{2,1},{3,2},{4,7},{5,4},{6,5},{7,6},{8,11},{9,8},{10,9... | collective-permute-start | bytes 331784 | tf_op jit(solution)/shard_map/ppermute | solution.py:397
  146.2 9.5 %collective-permute-start.19 = (bf16[48,1152]{1,0:T(8,128)(2,1)S(1)}, bf16[48,1152]{1,0:T(8,128)(2,1)S(1)}, u32[]{:S(2)}, u32[]{:S(2)}) collective-permute-start(bf16[48,1152]{1,0:T(8,128)(2,1)S(1)} %get-tuple-element.190), channel_id=1, source_target_pairs={{0,1},{1,2},{2,3},{3,0},{4,5},{5,6},{6,7},{7,4},{8,9},{9,10},{10,1... | collective-permute-start | bytes 331784 | tf_op jit(solution)/shard_map/ppermute | solution.py:397
  148.2 9.9 %collective-permute-start.18 = (bf16[48,1152]{1,0:T(8,128)(2,1)S(1)}, bf16[48,1152]{1,0:T(8,128)(2,1)S(1)}, u32[]{:S(2)}, u32[]{:S(2)}) collective-permute-start(bf16[48,1152]{1,0:T(8,128)(2,1)S(1)} %get-tuple-element.188), channel_id=1, source_target_pairs={{0,2},{1,3},{2,0},{3,1},{4,6},{5,7},{6,4},{7,5},{8,10},{9,11},{10,... | collective-permute-start | bytes 331784 | tf_op jit(solution)/shard_map/ppermute | solution.py:397
  150.2 12.0 %collective-permute-start.29 = (bf16[32,3840]{1,0:T(8,128)(2,1)S(1)}, bf16[32,3840]{1,0:T(8,128)(2,1)S(1)}, u32[]{:S(2)}, u32[]{:S(2)}) collective-permute-start(bf16[32,3840]{1,0:T(8,128)(2,1)S(1)} %maximum_select_fusion.4), channel_id=1, source_target_pairs={{0,4},{4,0},{8,12},{12,8},{16,20},{20,16},{24,28},{28,24},{1,5},{5... | collective-permute-start | bytes 737288 | tf_op jit(solution)/shard_map/ppermute | solution.py:393
  158.3 10.7 %collective-permute-start.21 = (bf16[48,1152]{1,0:T(8,128)(2,1)S(1)}, bf16[48,1152]{1,0:T(8,128)(2,1)S(1)}, u32[]{:S(2)}, u32[]{:S(2)}) collective-permute-start(bf16[48,1152]{1,0:T(8,128)(2,1)S(1)} %get-tuple-element.155), channel_id=1, source_target_pairs={{0,2},{1,3},{2,0},{3,1},{4,6},{5,7},{6,4},{7,5},{8,10},{9,11},{10,... | collective-permute-start | bytes 331784 | tf_op jit(solution)/shard_map/ppermute | solution.py:397
  158.3 10.7 %collective-permute-start.22 = (bf16[48,1152]{1,0:T(8,128)(2,1)S(1)}, bf16[48,1152]{1,0:T(8,128)(2,1)S(1)}, u32[]{:S(2)}, u32[]{:S(2)}) collective-permute-start(bf16[48,1152]{1,0:T(8,128)(2,1)S(1)} %get-tuple-element.155), channel_id=1, source_target_pairs={{0,1},{1,2},{2,3},{3,0},{4,5},{5,6},{6,7},{7,4},{8,9},{9,10},{10,1... | collective-permute-start | bytes 331784 | tf_op jit(solution)/shard_map/ppermute | solution.py:397
  161.6 8.3 %collective-permute-start.23 = (bf16[48,1152]{1,0:T(8,128)(2,1)S(1)}, bf16[48,1152]{1,0:T(8,128)(2,1)S(1)}, u32[]{:S(2)}, u32[]{:S(2)}) collective-permute-start(bf16[48,1152]{1,0:T(8,128)(2,1)S(1)} %get-tuple-element.155), channel_id=1, source_target_pairs={{0,3},{1,0},{2,1},{3,2},{4,7},{5,4},{6,5},{7,6},{8,11},{9,8},{10,9... | collective-permute-start | bytes 331784 | tf_op jit(solution)/shard_map/ppermute | solution.py:397
  162.3 8.9 %collective-permute-start.30 = (bf16[64,3840]{1,0:T(8,128)(2,1)S(1)}, bf16[64,3840]{1,0:T(8,128)(2,1)S(1)}, u32[]{:S(2)}, u32[]{:S(2)}) collective-permute-start(bf16[64,3840]{1,0:T(8,128)(2,1)S(1)} %maximum_select_fusion.3), channel_id=1, source_target_pairs={{0,16},{4,12},{8,24},{12,4},{16,0},{20,28},{24,8},{28,20},{1,17},{... | collective-permute-start | bytes 1474568 | tf_op jit(solution)/shard_map/ppermute | solution.py:393
  169.9 13.1 %collective-permute-start.32 = (bf16[48,4608]{1,0:T(8,128)(2,1)S(1)}, bf16[48,4608]{1,0:T(8,128)(2,1)S(1)}, u32[]{:S(2)}, u32[]{:S(2)}) collective-permute-start(bf16[48,4608]{1,0:T(8,128)(2,1)S(1)} %constant_dynamic-update-slice_fusion), channel_id=1, source_target_pairs={{0,16},{4,12},{8,24},{12,4},{16,0},{20,28},{24,8},{28,20},{1,17},{... | collective-permute-start | bytes 1327112 | tf_op jit(solution)/shard_map/ppermute | solution.py:393
  171.4 15.7 %collective-permute-start.31 = (bf16[128,3840]{1,0:T(8,128)(2,1)S(1)}, bf16[128,3840]{1,0:T(8,128)(2,1)S(1)}, u32[]{:S(2)}, u32[]{:S(2)}) collective-permute-start(bf16[128,3840]{1,0:T(8,128)(2,1)S(1)} %maximum_select_fusion.1), channel_id=1, source_target_pairs={{0,8},{4,20},{8,0},{12,28},{16,24},{20,4},{24,16},{28,12},{1,9},{5... | collective-permute-start | bytes 2949128 | tf_op jit(solution)/shard_map/ppermute | solution.py:393
  174.3 15.1 %collective-permute-start.24 = (bf16[2,3,64,384]{3,2,1,0:T(8,128)(2,1)S(1)}, bf16[2,3,64,384]{3,2,1,0:T(8,128)(2,1)S(1)}, u32[]{:S(2)}, u32[]{:S(2)}) collective-permute-start(bf16[2,3,64,384]{3,2,1,0:T(8,128)(2,1)S(1)} %get-tuple-element.126), channel_id=1, source_target_pairs={{0,2},{1,3},{2,0},{3,1},{4,6},{5,7},{6,4},{7,5},{8,10},{9,11},{10,... | collective-permute-start | bytes 884744 | tf_op jit(solution)/shard_map/ppermute | solution.py:397
  175.4 14.0 %collective-permute-start.25 = (bf16[2,3,64,384]{3,2,1,0:T(8,128)(2,1)S(1)}, bf16[2,3,64,384]{3,2,1,0:T(8,128)(2,1)S(1)}, u32[]{:S(2)}, u32[]{:S(2)}) collective-permute-start(bf16[2,3,64,384]{3,2,1,0:T(8,128)(2,1)S(1)} %get-tuple-element.128), channel_id=1, source_target_pairs={{0,3},{1,0},{2,1},{3,2},{4,7},{5,4},{6,5},{7,6},{8,11},{9,8},{10,9... | collective-permute-start | bytes 884744 | tf_op jit(solution)/shard_map/ppermute | solution.py:397
  189.4 13.6 %collective-permute-start.33 = (bf16[96,4608]{1,0:T(8,128)(2,1)S(1)}, bf16[96,4608]{1,0:T(8,128)(2,1)S(1)}, u32[]{:S(2)}, u32[]{:S(2)}) collective-permute-start(bf16[96,4608]{1,0:T(8,128)(2,1)S(1)} %maximum_select_fusion.2), channel_id=1, source_target_pairs={{0,8},{4,20},{8,0},{12,28},{16,24},{20,4},{24,16},{28,12},{1,9},{5... | collective-permute-start | bytes 2654216 | tf_op jit(solution)/shard_map/ppermute | solution.py:393
  191.8 12.9 %collective-permute-start.26 = (bf16[2,3,64,384]{3,2,1,0:T(8,128)(2,1)S(1)}, bf16[2,3,64,384]{3,2,1,0:T(8,128)(2,1)S(1)}, u32[]{:S(2)}, u32[]{:S(2)}) collective-permute-start(bf16[2,3,64,384]{3,2,1,0:T(8,128)(2,1)S(1)} %get-tuple-element.130), channel_id=1, source_target_pairs={{0,1},{1,2},{2,3},{3,0},{4,5},{5,6},{6,7},{7,4},{8,9},{9,10},{10,1... | collective-permute-start | bytes 884744 | tf_op jit(solution)/shard_map/ppermute | solution.py:397
  204.7 8.4 %collective-permute-start.34 = (bf16[192,4608]{1,0:T(8,128)(2,1)S(1)}, bf16[192,4608]{1,0:T(8,128)(2,1)}, u32[]{:S(2)}, u32[]{:S(2)}) collective-permute-start(bf16[192,4608]{1,0:T(8,128)(2,1)S(1)} %maximum_select_fusion.mine_ref), channel_id=1, source_target_pairs={{0,4},{4,0},{8,12},{12,8},{16,20},{20,16},{24,28},{28,24},{1,5},{5... | collective-permute-start | bytes 5308424 | tf_op jit(solution)/shard_map/ppermute | solution.py:393
  (16 other events, 53.5 us)

commit v5 on v4

--- a/solution.py
+++ b/solution.py
@@ -622,7 +622,7 @@
         1,
     )
     small = tied(small, given[1])
-    given = iter([given[-2]] + given[-1:] * (len(stages) - 2) + [part])
+    given = iter([given[-2]] * (len(stages) - 1) + given[-1:])
     for k in range(seq.bit_length() - 1):
         small = join_seq(small, place, 1 << k, seq)
     for step in group_steps(index, group):
@@ -632,10 +632,10 @@
     joins = list(reversed(stages[1:]))
     for k, stage in enumerate(joins):
         if k + 1 == len(joins):
-            part = tied(part, (final_rows[1], final_rows[2], small))
+            part = tied(part, (final_rows[1], small))
         part = join(part, index, stage)
     part, grad_ada = lax.optimization_barrier((part, grad_ada))
-    part = tied(part, final_rows[3])
+    part = tied(part, final_rows[2:])
     other = swap(part, stages[0])
     for k, buffer in enumerate(final_rows):
         put(buffer, k, len(chunks) - 1)

time: 220 us -> 217 us (0.986)
  waiting for transfers between devices: 46.9 us -> 57.3 us
  local copies, waits for them, and re-layouts: 17.3 us -> 10.8 us
  starting transfers between devices: 60.1 us -> 55 us
    ppermute x9, waiting for transfers between devices: 19.9 us -> 28.8 us  [swap(): lax.ppermute(array, 'grp', [(i, i ^ bit) for i, bit in enumerate(stage)])]
    dynamic_update_slice x12, local copies, waits for them, and re-layouts: 8.19 us -> 0.55 us  [put(): lax.dynamic_update_slice_in_dim(targets[which], buffer[which], (place + s...]
    ppermute x24, starting transfers between devices: 48.6 us -> 42.8 us  [seq_shift(): lax.ppermute(array, 'seq', [(i, (i + shift) % size) for i in range(size)])]
  transfers between devices with their start and end apart: 35 -> 35, of which waited for: 18 -> 18; matrix products, arithmetic and copies ran while one was open for 11% -> 8% of each run, Pallas kernels for 33% -> 34%
where the time goes in v5:
time: 217 us
  Pallas kernels  77.5 us (36%)
  waiting for transfers between devices  57.3 us (26%)
  starting transfers between devices  55 us (25%)
  other arithmetic  12.8 us (6%)
  local copies, waits for them, and re-layouts  10.8 us (5%)
  between operations  2.89 us (1%)
    pallas_call x3, Pallas kernels, layer_call(): pl.pallas_call(functools.partial(layer_kernel, parts, first, last, buffer...  67 us
    ppermute x24, starting transfers between devices, seq_shift(): lax.ppermute(array, 'seq', [(i, (i + shift) % size) for i in range(size)])  42.8 us
    ppermute x9, waiting for transfers between devices, swap(): lax.ppermute(array, 'grp', [(i, i ^ bit) for i, bit in enumerate(stage)])  28.8 us
    ppermute x24, waiting for transfers between devices, seq_shift(): lax.ppermute(array, 'seq', [(i, (i + shift) % size) for i in range(size)])  27.3 us
    ppermute x9, starting transfers between devices, swap(): lax.ppermute(array, 'grp', [(i, i ^ bit) for i, bit in enumerate(stage)])  7.86 us
    pallas_call x1, Pallas kernels, ada_call(): pl.pallas_call(ada_kernel, in_specs=[full] * 2, out_specs=[full] * 5, out...  5.72 us
    another operation x12, other arithmetic, pieces(): jnp.stack([cut(array, (place + shift) % seq * own + starts[chunk], chunks...  5.28 us
    pallas_call x1, Pallas kernels, finish(): pl.pallas_call(finish_kernel, in_specs=[pl.BlockSpec(memory_space=pltpu.S...  4.78 us
  transfers between devices with their start and end apart: 35, of which 18 were waited for; matrix products, arithmetic and copies ran while one was open for 8% of the time, Pallas kernels for 34%

profile of v5, /device:TPU:0, one launch (start us, length us, event | category | flops | bytes accessed | tf_op | source)
XLA Modules:
  0.0 216.8 jit_solution(495682836915493610)
XLA Ops:
  0.8 1.4 dynamic-slice_bitcast_fusion.16
  2.9 4.1 %collective-permute-start = (bf16[2,2,64,384]{3,2,1,0:T(8,128)(2,1)}, bf16[2,2,64,384]{3,2,1,0:T(8,128)(2,1)S(1)}, u32[]{:S(2)}, u32[]{:S(2)}) collective-permute-start(bf16[2,2,64,384]{3,2,1,0:T(8,128)(2,1)} %pad_maximum_fusion.10), channel_id=1, source_target_pairs={{0,2},{1,3},{2,0},{3,1},{4,6},{5,7},{6,4},{7,5},{8,10},{9,11},{10,... | collective-permute-start | bytes 589832 | tf_op jit(solution)/shard_map/ppermute | solution.py:397
  7.7 1.6 collective-permute-start.1
  10.0 2.2 %collective-permute-start.2 = (bf16[2,2,64,384]{3,2,1,0:T(8,128)(2,1)}, bf16[2,2,64,384]{3,2,1,0:T(8,128)(2,1)S(1)}, u32[]{:S(2)}, u32[]{:S(2)}) collective-permute-start(bf16[2,2,64,384]{3,2,1,0:T(8,128)(2,1)} %pad_maximum_fusion.12), channel_id=1, source_target_pairs={{0,3},{1,0},{2,1},{3,2},{4,7},{5,4},{6,5},{7,6},{8,11},{9,8},{10,9... | collective-permute-start | bytes 589832 | tf_op jit(solution)/shard_map/ppermute | solution.py:397
  14.1 2.0 dynamic-slice_bitcast_fusion
  19.5 1.9 collective-permute-done.refs_3_
  21.4 2.1 collective-permute-done.2.refs_5_
  23.5 3.9 %collective-permute-start.3 = (bf16[2,3,64,384]{3,2,1,0:T(8,128)(2,1)}, bf16[2,3,64,384]{3,2,1,0:T(8,128)(2,1)S(1)}, u32[]{:S(2)}, u32[]{:S(2)}) collective-permute-start(bf16[2,3,64,384]{3,2,1,0:T(8,128)(2,1)} %pad_maximum_fusion.2), channel_id=1, source_target_pairs={{0,2},{1,3},{2,0},{3,1},{4,6},{5,7},{6,4},{7,5},{8,10},{9,11},{10,... | collective-permute-start | bytes 884744 | tf_op jit(solution)/shard_map/ppermute | solution.py:397
  27.4 3.8 %collective-permute-start.5 = (bf16[2,3,64,384]{3,2,1,0:T(8,128)(2,1)S(1)}, bf16[2,3,64,384]{3,2,1,0:T(8,128)(2,1)S(1)}, u32[]{:S(2)}, u32[]{:S(2)}) collective-permute-start(bf16[2,3,64,384]{3,2,1,0:T(8,128)(2,1)S(1)} %copy-done.6), channel_id=1, source_target_pairs={{0,3},{1,0},{2,1},{3,2},{4,7},{5,4},{6,5},{7,6},{8,11},{9,8},{10,9... | collective-permute-start | bytes 884744 | tf_op jit(solution)/shard_map/ppermute | solution.py:397
  31.2 16.7 %shard_map.317 = (bf16[2,2,64,384]{3,2,1,0:T(8,128)(2,1)S(1)}, bf16[2,2,64,384]{3,2,1,0:T(8,128)(2,1)S(1)}, bf16[2,2,64,384]{3,2,1,0:T(8,128)(2,1)S(1)}, bf16[2,...) custom-call(s32[1]{0:T(128)} %bitcast.refs_0_.bit_ref, ...), custom_call_target="tpu_custom_call" | custom-call | flops 60000002048 | bytes 1572864 | tf_op jit(solution)/shard_map/pallas_call | solution.py:291
  48.3 5.2 %collective-permute-start.6 = (bf16[2,3,64,384]{3,2,1,0:T(8,128)(2,1)S(1)}, bf16[2,3,64,384]{3,2,1,0:T(8,128)(2,1)S(1)}, u32[]{:S(2)}, u32[]{:S(2)}) collective-permute-start(bf16[2,3,64,384]{3,2,1,0:T(8,128)(2,1)S(1)} %copy-done.5), channel_id=1, source_target_pairs={{0,2},{1,3},{2,0},{3,1},{4,6},{5,7},{6,4},{7,5},{8,10},{9,11},{10,... | collective-permute-start | bytes 884744 | tf_op jit(solution)/shard_map/ppermute | solution.py:397
  53.5 0.9 collective-permute-start.7
  54.4 2.9 %collective-permute-start.8 = (bf16[2,3,64,384]{3,2,1,0:T(8,128)(2,1)S(1)}, bf16[2,3,64,384]{3,2,1,0:T(8,128)(2,1)S(1)}, u32[]{:S(2)}, u32[]{:S(2)}) collective-permute-start(bf16[2,3,64,384]{3,2,1,0:T(8,128)(2,1)S(1)} %pad_maximum_fusion.8), channel_id=1, source_target_pairs={{0,3},{1,0},{2,1},{3,2},{4,7},{5,4},{6,5},{7,6},{8,11},{9,8},{10,9... | collective-permute-start | bytes 884744 | tf_op jit(solution)/shard_map/ppermute | solution.py:397
  57.3 24.5 %shard_map.318 = (bf16[2,3,64,384]{3,2,1,0:T(8,128)(2,1)S(1)}, bf16[2,3,64,384]{3,2,1,0:T(8,128)(2,1)S(1)}, bf16[2,3,64,384]{3,2,1,0:T(8,128)(2,1)S(1)}, bf16[2,...) custom-call(s32[1]{0:T(128)} %bitcast.refs_0_.bit_ref, ...), custom_call_target="tpu_custom_call", output_to_operand_aliasing={{6}: (15, {})} | custom-call | flops 89999998976 | bytes 2359296 | tf_op jit(solution)/shard_map/pallas_call | solution.py:291
  81.9 1.5 collective-permute-start.10
  84.0 3.2 %collective-permute-start.13 = (bf16[2,3,64,384]{3,2,1,0:T(8,128)(2,1)S(1)}, bf16[2,3,64,384]{3,2,1,0:T(8,128)(2,1)S(1)}, u32[]{:S(2)}, u32[]{:S(2)}) collective-permute-start(bf16[2,3,64,384]{3,2,1,0:T(8,128)(2,1)S(1)} %get-tuple-element.117), channel_id=1, source_target_pairs={{0,3},{1,0},{2,1},{3,2},{4,7},{5,4},{6,5},{7,6},{8,11},{9,8},{10,9... | collective-permute-start | bytes 884744 | tf_op jit(solution)/shard_map/ppermute | solution.py:397
  87.3 25.8 %shard_map.319 = (bf16[2,3,64,384]{3,2,1,0:T(8,128)(2,1)S(1)}, bf16[2,3,64,384]{3,2,1,0:T(8,128)(2,1)S(1)}, bf16[2,3,64,384]{3,2,1,0:T(8,128)(2,1)S(1)}, bf16[2,...) custom-call(s32[1]{0:T(128)} %bitcast.refs_0_.bit_ref, ...), custom_call_target="tpu_custom_call" | custom-call | flops 89999998976 | bytes 2359296 | tf_op jit(solution)/shard_map/pallas_call | solution.py:291
  116.7 1.2 collective-permute-done.15
  117.9 2.5 %add_convert_fusion.1 = (bf16[96,4608]{1,0:T(8,128)(2,1)S(1)}, bf16[96,4608]{1,0:T(8,128)(2,1)S(1)}) fusion(bf16[192,4608]{1,0:T(8,128)(2,1)} %collective-permute-done.15, s32[]{:T(128)S(6)} %select_n.376, bf16[192,4608]{1,0:T(8,128)(2,1)} %get-tuple-element.122, s32[]{:T(128)S(6)} %select_n.379), kind=kLoop, calls=%fused_computation.4 | loop fusion | flops 3538944 | bytes 5308424 | tf_op jit(solution)/shard_map/convert_element_type | solution.py:411
  120.4 1.6 collective-permute-start.16
  122.3 1.5 collective-permute-start.14
  123.8 1.9 collective-permute-start.27
  125.8 7.7 %collective-permute-done.16 = bf16[96,4608]{1,0:T(8,128)(2,1)S(1)} collective-permute-done((bf16[96,4608]{1,0:T(8,128)(2,1)S(1)}, bf16[96,4608]{1,0:T(8,128)(2,1)S(1)}, u32[]{:S(2)}, u32[]{:S(2)}) %collective-permute-start.16) | collective-permute-done | bytes 884768 | tf_op jit(solution)/shard_map/ppermute | solution.py:393
  133.6 1.6 collective-permute-start.17
  135.3 1.2 collective-permute-done.27
  136.5 2.4 %collective-permute-start.28 = (bf16[16,3840]{1,0:T(8,128)(2,1)S(1)}, bf16[16,3840]{1,0:T(8,128)(2,1)S(1)}, u32[]{:S(2)}, u32[]{:S(2)}) collective-permute-start(bf16[16,3840]{1,0:T(8,128)(2,1)S(1)} %maximum_select_fusion.5), channel_id=1, source_target_pairs={{0,2},{1,3},{2,0},{3,1},{4,6},{5,7},{6,4},{7,5},{8,10},{9,11},{10,... | collective-permute-start | bytes 368648 | tf_op jit(solution)/shard_map/ppermute | solution.py:445
  138.9 3.1 %collective-permute-done.17 = bf16[48,4608]{1,0:T(8,128)(2,1)S(1)} collective-permute-done((bf16[48,4608]{1,0:T(8,128)(2,1)S(1)}, bf16[48,4608]{1,0:T(8,128)(2,1)S(1)}, u32[]{:S(2)}, u32[]{:S(2)}) %collective-permute-start.17) | collective-permute-done | bytes 442400 | tf_op jit(solution)/shard_map/ppermute | solution.py:393
  142.2 3.5 %collective-permute-done.12 = bf16[2,3,64,384]{3,2,1,0:T(8,128)(2,1)S(1)} collective-permute-done((bf16[2,3,64,384]{3,2,1,0:T(8,128)(2,1)S(1)}, bf16[2,3,64,384]{3,2,1,0:T(8,128)(2,1)S(1)}, u32[]{:S(2)}, u32[]{:S(2)}) %collective-permute-start.12) | collective-permute-done | bytes 294944 | tf_op jit(solution)/shard_map/ppermute | solution.py:397
  145.7 2.0 collective-permute-start.19
  147.8 2.0 collective-permute-start.18
  149.8 2.9 %collective-permute-done.20 = bf16[48,1152]{1,0:T(8,128)(2,1)S(1)} collective-permute-done((bf16[48,1152]{1,0:T(8,128)(2,1)S(1)}, bf16[48,1152]{1,0:T(8,128)(2,1)S(1)}, u32[]{:S(2)}, u32[]{:S(2)}) %collective-permute-start.20) | collective-permute-done | bytes 110624 | tf_op jit(solution)/shard_map/ppermute | solution.py:397
  152.8 2.4 %collective-permute-done.19 = bf16[48,1152]{1,0:T(8,128)(2,1)S(1)} collective-permute-done((bf16[48,1152]{1,0:T(8,128)(2,1)S(1)}, bf16[48,1152]{1,0:T(8,128)(2,1)S(1)}, u32[]{:S(2)}, u32[]{:S(2)}) %collective-permute-start.19) | collective-permute-done | bytes 110624 | tf_op jit(solution)/shard_map/ppermute | solution.py:397
  155.2 2.4 %collective-permute-done.18 = bf16[48,1152]{1,0:T(8,128)(2,1)S(1)} collective-permute-done((bf16[48,1152]{1,0:T(8,128)(2,1)S(1)}, bf16[48,1152]{1,0:T(8,128)(2,1)S(1)}, u32[]{:S(2)}, u32[]{:S(2)}) %collective-permute-start.18) | collective-permute-done | bytes 110624 | tf_op jit(solution)/shard_map/ppermute | solution.py:397
  157.8 3.2 %collective-permute-start.22 = (bf16[48,1152]{1,0:T(8,128)(2,1)S(1)}, bf16[48,1152]{1,0:T(8,128)(2,1)S(1)}, u32[]{:S(2)}, u32[]{:S(2)}) collective-permute-start(bf16[48,1152]{1,0:T(8,128)(2,1)S(1)} %get-tuple-element.155), channel_id=1, source_target_pairs={{0,1},{1,2},{2,3},{3,0},{4,5},{5,6},{6,7},{7,4},{8,9},{9,10},{10,1... | collective-permute-start | bytes 331784 | tf_op jit(solution)/shard_map/ppermute | solution.py:397
  162.4 6.0 %collective-permute-done.21 = bf16[48,1152]{1,0:T(8,128)(2,1)S(1)} collective-permute-done((bf16[48,1152]{1,0:T(8,128)(2,1)S(1)}, bf16[48,1152]{1,0:T(8,128)(2,1)S(1)}, u32[]{:S(2)}, u32[]{:S(2)}) %collective-permute-start.21) | collective-permute-done | bytes 110624 | tf_op jit(solution)/shard_map/ppermute | solution.py:397
  170.9 1.7 collective-permute-start.31
  172.6 1.1 collective-permute-start.24
  173.7 8.8 %collective-permute-done.32 = bf16[48,4608]{1,0:T(8,128)(2,1)S(1)} collective-permute-done((bf16[48,4608]{1,0:T(8,128)(2,1)S(1)}, bf16[48,4608]{1,0:T(8,128)(2,1)S(1)}, u32[]{:S(2)}, u32[]{:S(2)}) %collective-permute-start.32) | collective-permute-done | bytes 442400 | tf_op jit(solution)/shard_map/ppermute | solution.py:393
  182.7 3.9 %collective-permute-done.31 = bf16[128,3840]{1,0:T(8,128)(2,1)S(1)} collective-permute-done((bf16[128,3840]{1,0:T(8,128)(2,1)S(1)}, bf16[128,3840]{1,0:T(8,128)(2,1)S(1)}, u32[]{:S(2)}, u32[]{:S(2)}) %collective-permute-start.31) | collective-permute-done | bytes 983072 | tf_op jit(solution)/shard_map/ppermute | solution.py:393
  186.9 1.4 pad_maximum_fusion.small_ref
  188.3 1.7 collective-permute-start.33
  190.2 2.0 collective-permute-start.26
  192.2 5.7 %shard_map.320 = (f32[384,2304]{1,0:T(8,128)}, f32[1,2304]{1,0:T(1,128)S(1)}, f32[8,640]{1,0:T(8,128)S(1)}, f32[256,384]{1,0:T(8,128)S(1)}, f32[64,384]{1,0:T(8,128)}) custom-call(bf16[256,3840]{1,0:T(8,128)(2,1)} %pad_maximum_fusion.small_ref, bf16[384,2304]{1,0:T(8,128)(2,1)} %weight_ref.1), custom_call_target="tpu_custom_call" | custom-call | flops 6000000000 | bytes 8000000 | tf_op jit(solution)/shard_map/pallas_call | solution.py:364
  197.9 3.4 %collective-permute-done.33 = bf16[96,4608]{1,0:T(8,128)(2,1)S(1)} collective-permute-done((bf16[96,4608]{1,0:T(8,128)(2,1)S(1)}, bf16[96,4608]{1,0:T(8,128)(2,1)S(1)}, u32[]{:S(2)}, u32[]{:S(2)}) %collective-permute-start.33) | collective-permute-done | bytes 884768 | tf_op jit(solution)/shard_map/ppermute | solution.py:393
  201.7 4.6 %collective-permute-done.26 = bf16[2,3,64,384]{3,2,1,0:T(8,128)(2,1)S(1)} collective-permute-done((bf16[2,3,64,384]{3,2,1,0:T(8,128)(2,1)S(1)}, bf16[2,3,64,384]{3,2,1,0:T(8,128)(2,1)S(1)}, u32[]{:S(2)}, u32[]{:S(2)}) %collective-permute-start.26) | collective-permute-done | bytes 294944 | tf_op jit(solution)/shard_map/ppermute | solution.py:397
  206.7 1.1 copy-done.21
  207.8 1.1 copy-done.23
  212.0 4.8 %shard_map.321 = (f32[384,1536]{1,0:T(8,128)}, f32[1536,384]{1,0:T(8,128)}, f32[384,1152]{1,0:T(8,128)}, f32[384,384]{1,0:T(8,128)}) custom-call(s32[1]{0:T(128)} %bitcast.refs_0_.bit_ref, bf16[192,4608]{1,0:T(8,128)(2,1)S(1)} %maximum_select_fusion.mine_ref, bf16[192,4608]{1,0:T(8,128)(2,1)} %collective-permute-done.34.other_ref), custom_call_target="tpu_custom_call" | custom-call | tf_op jit(solution)/shard_map/pallas_call | solution.py:331
  (180 shorter events, 19.5 us)
Async XLA Ops:
  0.6 12.4 %copy-start = (f32[64,384]{1,0:T(8,128)S(1)}, f32[64,384]{1,0:T(8,128)}, u32[]{:S(2)}) copy-start(f32[64,384]{1,0:T(8,128)} %param.27) | copy-start | bytes 294916
  0.7 11.6 %copy-start.11 = (f32[16,2,384]{2,1,0:T(2,128)S(1)}, f32[16,2,384]{2,1,0:T(2,128)}, u32[]{:S(2)}) copy-start(f32[16,2,384]{2,1,0:T(2,128)} %param.24) | copy-start | bytes 147460
  0.7 11.6 %copy-start.18 = (s32[16,2]{0,1:T(2,128)S(1)}, s32[16,2]{0,1:T(2,128)}, u32[]{:S(2)}) copy-start(s32[16,2]{0,1:T(2,128)} %param.26) | copy-start | bytes 388
  0.7 12.5 %copy-start.3 = (bf16[384,2304]{1,0:T(8,128)(2,1)S(1)}, bf16[384,2304]{1,0:T(8,128)(2,1)}, u32[]{:S(2)}) copy-start(bf16[384,2304]{1,0:T(8,128)(2,1)} %weight_ref.1) | copy-start | bytes 5308420
  0.7 12.5 %copy-start.12 = (f32[2304]{0:T(1024)S(1)}, f32[2304]{0:T(1024)}, u32[]{:S(2)}) copy-start(f32[2304]{0:T(1024)} %param.29) | copy-start | bytes 27652
  2.9 18.5 %collective-permute-start = (bf16[2,2,64,384]{3,2,1,0:T(8,128)(2,1)}, bf16[2,2,64,384]{3,2,1,0:T(8,128)(2,1)S(1)}, u32[]{:S(2)}, u32[]{:S(2)}) collective-permute-start(bf16[2,2,64,384]{3,2,1,0:T(8,128)(2,1)} %pad_maximum_fusion.10), channel_id=1, source_target_pairs={{0,2},{1,3},{2,0},{3,1},{4,6},{5,7},{6,4},{7,5},{8,10},{9,11},{10,... | collective-permute-start | bytes 589832 | tf_op jit(solution)/shard_map/ppermute | solution.py:397
  7.7 13.7 %collective-permute-start.1 = (bf16[2,2,64,384]{3,2,1,0:T(8,128)(2,1)}, bf16[2,2,64,384]{3,2,1,0:T(8,128)(2,1)S(1)}, u32[]{:S(2)}, u32[]{:S(2)}) collective-permute-start(bf16[2,2,64,384]{3,2,1,0:T(8,128)(2,1)} %pad_maximum_fusion.11), channel_id=1, source_target_pairs={{0,1},{1,2},{2,3},{3,0},{4,5},{5,6},{6,7},{7,4},{8,9},{9,10},{10,1... | collective-permute-start | bytes 589832 | tf_op jit(solution)/shard_map/ppermute | solution.py:397
  10.0 13.6 %collective-permute-start.2 = (bf16[2,2,64,384]{3,2,1,0:T(8,128)(2,1)}, bf16[2,2,64,384]{3,2,1,0:T(8,128)(2,1)S(1)}, u32[]{:S(2)}, u32[]{:S(2)}) collective-permute-start(bf16[2,2,64,384]{3,2,1,0:T(8,128)(2,1)} %pad_maximum_fusion.12), channel_id=1, source_target_pairs={{0,3},{1,0},{2,1},{3,2},{4,7},{5,4},{6,5},{7,6},{8,11},{9,8},{10,9... | collective-permute-start | bytes 589832 | tf_op jit(solution)/shard_map/ppermute | solution.py:397
  18.4 12.8 %copy-start.2 = (bf16[384,384]{1,0:T(8,128)(2,1)S(1)}, bf16[384,384]{1,0:T(8,128)(2,1)}, u32[]{:S(2)}) copy-start(bf16[384,384]{1,0:T(8,128)(2,1)} %refs_8_.5) | copy-start | bytes 884740
  19.2 8.2 %copy-start.6 = (bf16[2,3,64,384]{3,2,1,0:T(8,128)(2,1)S(1)}, bf16[2,3,64,384]{3,2,1,0:T(8,128)(2,1)}, u32[]{:S(2)}) copy-start(bf16[2,3,64,384]{3,2,1,0:T(8,128)(2,1)} %pad_maximum_fusion.4) | copy-start | bytes 884740
  23.5 24.4 %collective-permute-start.3 = (bf16[2,3,64,384]{3,2,1,0:T(8,128)(2,1)}, bf16[2,3,64,384]{3,2,1,0:T(8,128)(2,1)S(1)}, u32[]{:S(2)}, u32[]{:S(2)}) collective-permute-start(bf16[2,3,64,384]{3,2,1,0:T(8,128)(2,1)} %pad_maximum_fusion.2), channel_id=1, source_target_pairs={{0,2},{1,3},{2,0},{3,1},{4,6},{5,7},{6,4},{7,5},{8,10},{9,11},{10,... | collective-permute-start | bytes 884744 | tf_op jit(solution)/shard_map/ppermute | solution.py:397
  27.4 20.5 %collective-permute-start.4 = (bf16[2,3,64,384]{3,2,1,0:T(8,128)(2,1)}, bf16[2,3,64,384]{3,2,1,0:T(8,128)(2,1)S(1)}, u32[]{:S(2)}, u32[]{:S(2)}) collective-permute-start(bf16[2,3,64,384]{3,2,1,0:T(8,128)(2,1)} %pad_maximum_fusion.3), channel_id=1, source_target_pairs={{0,1},{1,2},{2,3},{3,0},{4,5},{5,6},{6,7},{7,4},{8,9},{9,10},{10,1... | collective-permute-start | bytes 884744 | tf_op jit(solution)/shard_map/ppermute | solution.py:397
  27.4 20.9 %collective-permute-start.5 = (bf16[2,3,64,384]{3,2,1,0:T(8,128)(2,1)S(1)}, bf16[2,3,64,384]{3,2,1,0:T(8,128)(2,1)S(1)}, u32[]{:S(2)}, u32[]{:S(2)}) collective-permute-start(bf16[2,3,64,384]{3,2,1,0:T(8,128)(2,1)S(1)} %copy-done.6), channel_id=1, source_target_pairs={{0,3},{1,0},{2,1},{3,2},{4,7},{5,4},{6,5},{7,6},{8,11},{9,8},{10,9... | collective-permute-start | bytes 884744 | tf_op jit(solution)/shard_map/ppermute | solution.py:397
  31.2 17.1 %copy-start.5 = (bf16[2,3,64,384]{3,2,1,0:T(8,128)(2,1)S(1)}, bf16[2,3,64,384]{3,2,1,0:T(8,128)(2,1)}, u32[]{:S(2)}) copy-start(bf16[2,3,64,384]{3,2,1,0:T(8,128)(2,1)} %pad_maximum_fusion.6) | copy-start | bytes 884740
  47.9 9.4 %copy-start.26 = (bf16[2,3,64,384]{3,2,1,0:T(8,128)(2,1)}, bf16[2,3,64,384]{3,2,1,0:T(8,128)(2,1)S(1)}, u32[]{:S(2)}) copy-start(bf16[2,3,64,384]{3,2,1,0:T(8,128)(2,1)S(1)} %collective-permute-done.4.refs_4_) | copy-start | bytes 884740
  48.3 9.0 %copy-start.27 = (bf16[2,3,64,384]{3,2,1,0:T(8,128)(2,1)}, bf16[2,3,64,384]{3,2,1,0:T(8,128)(2,1)S(1)}, u32[]{:S(2)}) copy-start(bf16[2,3,64,384]{3,2,1,0:T(8,128)(2,1)S(1)} %collective-permute-done.5.refs_5_) | copy-start | bytes 884740
  48.3 33.5 %collective-permute-start.6 = (bf16[2,3,64,384]{3,2,1,0:T(8,128)(2,1)S(1)}, bf16[2,3,64,384]{3,2,1,0:T(8,128)(2,1)S(1)}, u32[]{:S(2)}, u32[]{:S(2)}) collective-permute-start(bf16[2,3,64,384]{3,2,1,0:T(8,128)(2,1)S(1)} %copy-done.5), channel_id=1, source_target_pairs={{0,2},{1,3},{2,0},{3,1},{4,6},{5,7},{6,4},{7,5},{8,10},{9,11},{10,... | collective-permute-start | bytes 884744 | tf_op jit(solution)/shard_map/ppermute | solution.py:397
  53.5 28.3 %collective-permute-start.7 = (bf16[2,3,64,384]{3,2,1,0:T(8,128)(2,1)S(1)}, bf16[2,3,64,384]{3,2,1,0:T(8,128)(2,1)S(1)}, u32[]{:S(2)}, u32[]{:S(2)}) collective-permute-start(bf16[2,3,64,384]{3,2,1,0:T(8,128)(2,1)S(1)} %pad_maximum_fusion.7), channel_id=1, source_target_pairs={{0,1},{1,2},{2,3},{3,0},{4,5},{5,6},{6,7},{7,4},{8,9},{9,10},{10,1... | collective-permute-start | bytes 884744 | tf_op jit(solution)/shard_map/ppermute | solution.py:397
  54.4 27.4 %collective-permute-start.8 = (bf16[2,3,64,384]{3,2,1,0:T(8,128)(2,1)S(1)}, bf16[2,3,64,384]{3,2,1,0:T(8,128)(2,1)S(1)}, u32[]{:S(2)}, u32[]{:S(2)}) collective-permute-start(bf16[2,3,64,384]{3,2,1,0:T(8,128)(2,1)S(1)} %pad_maximum_fusion.8), channel_id=1, source_target_pairs={{0,3},{1,0},{2,1},{3,2},{4,7},{5,4},{6,5},{7,6},{8,11},{9,8},{10,9... | collective-permute-start | bytes 884744 | tf_op jit(solution)/shard_map/ppermute | solution.py:397
  81.9 31.3 %collective-permute-start.9 = (bf16[2,2,64,384]{3,2,1,0:T(8,128)(2,1)S(1)}, bf16[2,2,64,384]{3,2,1,0:T(8,128)(2,1)S(1)}, u32[]{:S(2)}, u32[]{:S(2)}) collective-permute-start(bf16[2,2,64,384]{3,2,1,0:T(8,128)(2,1)S(1)} %get-tuple-element.108), channel_id=1, source_target_pairs={{0,2},{1,3},{2,0},{3,1},{4,6},{5,7},{6,4},{7,5},{8,10},{9,11},{10,... | collective-permute-start | bytes 589832 | tf_op jit(solution)/shard_map/ppermute | solution.py:397
  81.9 31.2 %collective-permute-start.10 = (bf16[2,2,64,384]{3,2,1,0:T(8,128)(2,1)S(1)}, bf16[2,2,64,384]{3,2,1,0:T(8,128)(2,1)S(1)}, u32[]{:S(2)}, u32[]{:S(2)}) collective-permute-start(bf16[2,2,64,384]{3,2,1,0:T(8,128)(2,1)S(1)} %get-tuple-element.110), channel_id=1, source_target_pairs={{0,3},{1,0},{2,1},{3,2},{4,7},{5,4},{6,5},{7,6},{8,11},{9,8},{10,9... | collective-permute-start | bytes 589832 | tf_op jit(solution)/shard_map/ppermute | solution.py:397
  83.4 29.7 %collective-permute-start.11 = (bf16[2,2,64,384]{3,2,1,0:T(8,128)(2,1)S(1)}, bf16[2,2,64,384]{3,2,1,0:T(8,128)(2,1)S(1)}, u32[]{:S(2)}, u32[]{:S(2)}) collective-permute-start(bf16[2,2,64,384]{3,2,1,0:T(8,128)(2,1)S(1)} %get-tuple-element.112), channel_id=1, source_target_pairs={{0,1},{1,2},{2,3},{3,0},{4,5},{5,6},{6,7},{7,4},{8,9},{9,10},{10,1... | collective-permute-start | bytes 589832 | tf_op jit(solution)/shard_map/ppermute | solution.py:397
  84.0 29.1 %collective-permute-start.13 = (bf16[2,3,64,384]{3,2,1,0:T(8,128)(2,1)S(1)}, bf16[2,3,64,384]{3,2,1,0:T(8,128)(2,1)S(1)}, u32[]{:S(2)}, u32[]{:S(2)}) collective-permute-start(bf16[2,3,64,384]{3,2,1,0:T(8,128)(2,1)S(1)} %get-tuple-element.117), channel_id=1, source_target_pairs={{0,3},{1,0},{2,1},{3,2},{4,7},{5,4},{6,5},{7,6},{8,11},{9,8},{10,9... | collective-permute-start | bytes 884744 | tf_op jit(solution)/shard_map/ppermute | solution.py:397
  87.3 26.6 %copy-start.29 = (s32[8]{0:T(128)S(1)}, s32[8]{0:T(128)}, u32[]{:S(2)}) copy-start(s32[8]{0:T(128)} %constant.206.clone) | copy-start | bytes 100
  87.3 27.8 %copy-start.28 = (s32[8]{0:T(128)S(1)}, s32[8]{0:T(128)}, u32[]{:S(2)}) copy-start(s32[8]{0:T(128)} %constant.207.clone) | copy-start | bytes 100
  87.3 29.4 %copy-start.8 = (f32[8,384]{1,0:T(8,128)S(1)}, f32[8,384]{1,0:T(8,128)}, u32[]{:S(2)}) copy-start(f32[8,384]{1,0:T(8,128)} %copy-done.7) | copy-start | bytes 36868
  113.8 4.0 %collective-permute-start.15 = (bf16[192,4608]{1,0:T(8,128)(2,1)}, bf16[192,4608]{1,0:T(8,128)(2,1)}, u32[]{:S(2)}, u32[]{:S(2)}) collective-permute-start(bf16[192,4608]{1,0:T(8,128)(2,1)} %get-tuple-element.124), channel_id=1, source_target_pairs={{0,4},{4,0},{8,12},{12,8},{16,20},{20,16},{24,28},{28,24},{1,5},{5... | collective-permute-start | bytes 5308424 | tf_op jit(solution)/shard_map/ppermute | solution.py:393
  120.4 13.1 %collective-permute-start.16 = (bf16[96,4608]{1,0:T(8,128)(2,1)S(1)}, bf16[96,4608]{1,0:T(8,128)(2,1)S(1)}, u32[]{:S(2)}, u32[]{:S(2)}) collective-permute-start(bf16[96,4608]{1,0:T(8,128)(2,1)S(1)} %get-tuple-element.157), channel_id=1, source_target_pairs={{0,8},{4,20},{8,0},{12,28},{16,24},{20,4},{24,16},{28,12},{1,9},{5... | collective-permute-start | bytes 2654216 | tf_op jit(solution)/shard_map/ppermute | solution.py:393
  122.1 23.5 %collective-permute-start.12 = (bf16[2,3,64,384]{3,2,1,0:T(8,128)(2,1)S(1)}, bf16[2,3,64,384]{3,2,1,0:T(8,128)(2,1)S(1)}, u32[]{:S(2)}, u32[]{:S(2)}) collective-permute-start(bf16[2,3,64,384]{3,2,1,0:T(8,128)(2,1)S(1)} %get-tuple-element.115), channel_id=1, source_target_pairs={{0,2},{1,3},{2,0},{3,1},{4,6},{5,7},{6,4},{7,5},{8,10},{9,11},{10,... | collective-permute-start | bytes 884744 | tf_op jit(solution)/shard_map/ppermute | solution.py:397
  122.3 23.3 %collective-permute-start.14 = (bf16[2,3,64,384]{3,2,1,0:T(8,128)(2,1)S(1)}, bf16[2,3,64,384]{3,2,1,0:T(8,128)(2,1)S(1)}, u32[]{:S(2)}, u32[]{:S(2)}) collective-permute-start(bf16[2,3,64,384]{3,2,1,0:T(8,128)(2,1)S(1)} %get-tuple-element.119), channel_id=1, source_target_pairs={{0,1},{1,2},{2,3},{3,0},{4,5},{5,6},{6,7},{7,4},{8,9},{9,10},{10,1... | collective-permute-start | bytes 884744 | tf_op jit(solution)/shard_map/ppermute | solution.py:397
  123.8 12.7 %collective-permute-start.27 = (bf16[8,3840]{1,0:T(8,128)(2,1)S(1)}, bf16[8,3840]{1,0:T(8,128)(2,1)S(1)}, u32[]{:S(2)}, u32[]{:S(2)}) collective-permute-start(bf16[8,3840]{1,0:T(8,128)(2,1)S(1)} %constant_dynamic-update-slice_fusion.4), channel_id=1, source_target_pairs={{0,1},{1,0},{2,3},{3,2},{4,5},{5,4},{6,7},{7,6},{8,9},{9,8},{10,11... | collective-permute-start | bytes 184328 | tf_op jit(solution)/shard_map/ppermute | solution.py:445
  133.6 8.4 %collective-permute-start.17 = (bf16[48,4608]{1,0:T(8,128)(2,1)S(1)}, bf16[48,4608]{1,0:T(8,128)(2,1)S(1)}, u32[]{:S(2)}, u32[]{:S(2)}) collective-permute-start(bf16[48,4608]{1,0:T(8,128)(2,1)S(1)} %add_convert_fusion.3), channel_id=1, source_target_pairs={{0,16},{4,12},{8,24},{12,4},{16,0},{20,28},{24,8},{28,20},{1,17},{... | collective-permute-start | bytes 1327112 | tf_op jit(solution)/shard_map/ppermute | solution.py:393
  136.5 13.2 %collective-permute-start.28 = (bf16[16,3840]{1,0:T(8,128)(2,1)S(1)}, bf16[16,3840]{1,0:T(8,128)(2,1)S(1)}, u32[]{:S(2)}, u32[]{:S(2)}) collective-permute-start(bf16[16,3840]{1,0:T(8,128)(2,1)S(1)} %maximum_select_fusion.5), channel_id=1, source_target_pairs={{0,2},{1,3},{2,0},{3,1},{4,6},{5,7},{6,4},{7,5},{8,10},{9,11},{10,... | collective-permute-start | bytes 368648 | tf_op jit(solution)/shard_map/ppermute | solution.py:445
  145.7 7.1 %collective-permute-start.20 = (bf16[48,1152]{1,0:T(8,128)(2,1)S(1)}, bf16[48,1152]{1,0:T(8,128)(2,1)S(1)}, u32[]{:S(2)}, u32[]{:S(2)}) collective-permute-start(bf16[48,1152]{1,0:T(8,128)(2,1)S(1)} %get-tuple-element.189), channel_id=1, source_target_pairs={{0,3},{1,0},{2,1},{3,2},{4,7},{5,4},{6,5},{7,6},{8,11},{9,8},{10,9... | collective-permute-start | bytes 331784 | tf_op jit(solution)/shard_map/ppermute | solution.py:397
  145.7 9.5 %collective-permute-start.19 = (bf16[48,1152]{1,0:T(8,128)(2,1)S(1)}, bf16[48,1152]{1,0:T(8,128)(2,1)S(1)}, u32[]{:S(2)}, u32[]{:S(2)}) collective-permute-start(bf16[48,1152]{1,0:T(8,128)(2,1)S(1)} %get-tuple-element.190), channel_id=1, source_target_pairs={{0,1},{1,2},{2,3},{3,0},{4,5},{5,6},{6,7},{7,4},{8,9},{9,10},{10,1... | collective-permute-start | bytes 331784 | tf_op jit(solution)/shard_map/ppermute | solution.py:397
  147.8 9.9 %collective-permute-start.18 = (bf16[48,1152]{1,0:T(8,128)(2,1)S(1)}, bf16[48,1152]{1,0:T(8,128)(2,1)S(1)}, u32[]{:S(2)}, u32[]{:S(2)}) collective-permute-start(bf16[48,1152]{1,0:T(8,128)(2,1)S(1)} %get-tuple-element.188), channel_id=1, source_target_pairs={{0,2},{1,3},{2,0},{3,1},{4,6},{5,7},{6,4},{7,5},{8,10},{9,11},{10,... | collective-permute-start | bytes 331784 | tf_op jit(solution)/shard_map/ppermute | solution.py:397
  149.8 12.0 %collective-permute-start.29 = (bf16[32,3840]{1,0:T(8,128)(2,1)S(1)}, bf16[32,3840]{1,0:T(8,128)(2,1)S(1)}, u32[]{:S(2)}, u32[]{:S(2)}) collective-permute-start(bf16[32,3840]{1,0:T(8,128)(2,1)S(1)} %maximum_select_fusion.4), channel_id=1, source_target_pairs={{0,4},{4,0},{8,12},{12,8},{16,20},{20,16},{24,28},{28,24},{1,5},{5... | collective-permute-start | bytes 737288 | tf_op jit(solution)/shard_map/ppermute | solution.py:393
  157.8 10.7 %collective-permute-start.21 = (bf16[48,1152]{1,0:T(8,128)(2,1)S(1)}, bf16[48,1152]{1,0:T(8,128)(2,1)S(1)}, u32[]{:S(2)}, u32[]{:S(2)}) collective-permute-start(bf16[48,1152]{1,0:T(8,128)(2,1)S(1)} %get-tuple-element.155), channel_id=1, source_target_pairs={{0,2},{1,3},{2,0},{3,1},{4,6},{5,7},{6,4},{7,5},{8,10},{9,11},{10,... | collective-permute-start | bytes 331784 | tf_op jit(solution)/shard_map/ppermute | solution.py:397
  157.8 10.6 %collective-permute-start.22 = (bf16[48,1152]{1,0:T(8,128)(2,1)S(1)}, bf16[48,1152]{1,0:T(8,128)(2,1)S(1)}, u32[]{:S(2)}, u32[]{:S(2)}) collective-permute-start(bf16[48,1152]{1,0:T(8,128)(2,1)S(1)} %get-tuple-element.155), channel_id=1, source_target_pairs={{0,1},{1,2},{2,3},{3,0},{4,5},{5,6},{6,7},{7,4},{8,9},{9,10},{10,1... | collective-permute-start | bytes 331784 | tf_op jit(solution)/shard_map/ppermute | solution.py:397
  161.1 8.4 %collective-permute-start.23 = (bf16[48,1152]{1,0:T(8,128)(2,1)S(1)}, bf16[48,1152]{1,0:T(8,128)(2,1)S(1)}, u32[]{:S(2)}, u32[]{:S(2)}) collective-permute-start(bf16[48,1152]{1,0:T(8,128)(2,1)S(1)} %get-tuple-element.155), channel_id=1, source_target_pairs={{0,3},{1,0},{2,1},{3,2},{4,7},{5,4},{6,5},{7,6},{8,11},{9,8},{10,9... | collective-permute-start | bytes 331784 | tf_op jit(solution)/shard_map/ppermute | solution.py:397
  161.8 8.9 %collective-permute-start.30 = (bf16[64,3840]{1,0:T(8,128)(2,1)S(1)}, bf16[64,3840]{1,0:T(8,128)(2,1)S(1)}, u32[]{:S(2)}, u32[]{:S(2)}) collective-permute-start(bf16[64,3840]{1,0:T(8,128)(2,1)S(1)} %maximum_select_fusion.3), channel_id=1, source_target_pairs={{0,16},{4,12},{8,24},{12,4},{16,0},{20,28},{24,8},{28,20},{1,17},{... | collective-permute-start | bytes 1474568 | tf_op jit(solution)/shard_map/ppermute | solution.py:393
  169.5 13.1 %collective-permute-start.32 = (bf16[48,4608]{1,0:T(8,128)(2,1)S(1)}, bf16[48,4608]{1,0:T(8,128)(2,1)S(1)}, u32[]{:S(2)}, u32[]{:S(2)}) collective-permute-start(bf16[48,4608]{1,0:T(8,128)(2,1)S(1)} %constant_dynamic-update-slice_fusion), channel_id=1, source_target_pairs={{0,16},{4,12},{8,24},{12,4},{16,0},{20,28},{24,8},{28,20},{1,17},{... | collective-permute-start | bytes 1327112 | tf_op jit(solution)/shard_map/ppermute | solution.py:393
  170.9 15.7 %collective-permute-start.31 = (bf16[128,3840]{1,0:T(8,128)(2,1)S(1)}, bf16[128,3840]{1,0:T(8,128)(2,1)S(1)}, u32[]{:S(2)}, u32[]{:S(2)}) collective-permute-start(bf16[128,3840]{1,0:T(8,128)(2,1)S(1)} %maximum_select_fusion.1), channel_id=1, source_target_pairs={{0,8},{4,20},{8,0},{12,28},{16,24},{20,4},{24,16},{28,12},{1,9},{5... | collective-permute-start | bytes 2949128 | tf_op jit(solution)/shard_map/ppermute | solution.py:393
  172.6 15.7 %collective-permute-start.24 = (bf16[2,3,64,384]{3,2,1,0:T(8,128)(2,1)S(1)}, bf16[2,3,64,384]{3,2,1,0:T(8,128)(2,1)S(1)}, u32[]{:S(2)}, u32[]{:S(2)}) collective-permute-start(bf16[2,3,64,384]{3,2,1,0:T(8,128)(2,1)S(1)} %get-tuple-element.126), channel_id=1, source_target_pairs={{0,2},{1,3},{2,0},{3,1},{4,6},{5,7},{6,4},{7,5},{8,10},{9,11},{10,... | collective-permute-start | bytes 884744 | tf_op jit(solution)/shard_map/ppermute | solution.py:397
  188.3 13.0 %collective-permute-start.33 = (bf16[96,4608]{1,0:T(8,128)(2,1)S(1)}, bf16[96,4608]{1,0:T(8,128)(2,1)S(1)}, u32[]{:S(2)}, u32[]{:S(2)}) collective-permute-start(bf16[96,4608]{1,0:T(8,128)(2,1)S(1)} %maximum_select_fusion.2), channel_id=1, source_target_pairs={{0,8},{4,20},{8,0},{12,28},{16,24},{20,4},{24,16},{28,12},{1,9},{5... | collective-permute-start | bytes 2654216 | tf_op jit(solution)/shard_map/ppermute | solution.py:393
  190.1 11.5 %collective-permute-start.25 = (bf16[2,3,64,384]{3,2,1,0:T(8,128)(2,1)S(1)}, bf16[2,3,64,384]{3,2,1,0:T(8,128)(2,1)S(1)}, u32[]{:S(2)}, u32[]{:S(2)}) collective-permute-start(bf16[2,3,64,384]{3,2,1,0:T(8,128)(2,1)S(1)} %get-tuple-element.128), channel_id=1, source_target_pairs={{0,3},{1,0},{2,1},{3,2},{4,7},{5,4},{6,5},{7,6},{8,11},{9,8},{10,9... | collective-permute-start | bytes 884744 | tf_op jit(solution)/shard_map/ppermute | solution.py:397
  190.2 16.1 %collective-permute-start.26 = (bf16[2,3,64,384]{3,2,1,0:T(8,128)(2,1)S(1)}, bf16[2,3,64,384]{3,2,1,0:T(8,128)(2,1)S(1)}, u32[]{:S(2)}, u32[]{:S(2)}) collective-permute-start(bf16[2,3,64,384]{3,2,1,0:T(8,128)(2,1)S(1)} %get-tuple-element.130), channel_id=1, source_target_pairs={{0,1},{1,2},{2,3},{3,0},{4,5},{5,6},{6,7},{7,4},{8,9},{9,10},{10,1... | collective-permute-start | bytes 884744 | tf_op jit(solution)/shard_map/ppermute | solution.py:397
  206.3 5.7 %collective-permute-start.34 = (bf16[192,4608]{1,0:T(8,128)(2,1)S(1)}, bf16[192,4608]{1,0:T(8,128)(2,1)}, u32[]{:S(2)}, u32[]{:S(2)}) collective-permute-start(bf16[192,4608]{1,0:T(8,128)(2,1)S(1)} %maximum_select_fusion.mine_ref), channel_id=1, source_target_pairs={{0,4},{4,0},{8,12},{12,8},{16,20},{20,16},{24,28},{28,24},{1,5},{5... | collective-permute-start | bytes 5308424 | tf_op jit(solution)/shard_map/ppermute | solution.py:393
  (18 other events, 58.4 us)
